TPU v7x, 128 devices: a whole 4x4x4 slice. The times are simulated.
128 devices in a mesh: dp: 1, ep: 128 (over z, y, x, core).
Axes of the slice: x: 4, y: 4, z: 4, core: 2. Of those that a mesh axis runs over, the one named last changes fastest.
Arguments:
- hidden: bfloat16 [128, 256, 2048], P(('dp', 'ep'))
- expert_ids: int32 [128, 256, 8], P(('dp', 'ep'))
- slot_ids: int32 [128, 256, 8], P(('dp', 'ep'))
- attn_norm: bfloat16 [2048], replicated
- w_query: bfloat16 [2048, 4096], replicated
- w_key: bfloat16 [2048, 512], replicated
- w_value: bfloat16 [2048, 512], replicated
- w_out: bfloat16 [32, 128, 2048], replicated
- ffn_norm: bfloat16 [2048], replicated
- ffn_gate: bfloat16 [2048, 6144], replicated
- ffn_up: bfloat16 [2048, 6144], replicated
- ffn_down: bfloat16 [6144, 2048], replicated
- moe_norm: bfloat16 [2048], replicated
- w_router: bfloat16 [2048, 128], replicated
- exp_gate: bfloat16 [128, 2048, 768], P('ep')
- exp_up: bfloat16 [128, 2048, 768], P('ep')
- exp_down: bfloat16 [128, 768, 2048], P('ep')
Outputs:
- output: bfloat16 [128, 256, 2048], P(('dp', 'ep'))
All inputs are finite; a program needn't handle non-finite values.
Results may differ from a plain program's by a relative error of at most 0.0109522.
Values are sent between devices in bfloat16 or wider.
A program may use at most 1 GiB of HBM per device.

v0:
```python
import jax
import jax.numpy as jnp
from jax import lax
from jax.sharding import PartitionSpec as P, NamedSharding

RMS_EPS = 1e-6
ROPE_BASE = 10000.0
CAP_FACTOR = 3


def rms_norm(row_vals, norm_scale):
    as_float = row_vals.astype(jnp.float32)
    inv_rms = lax.rsqrt(jnp.mean(as_float * as_float, axis=-1, keepdims=True) + RMS_EPS)
    return (as_float * inv_rms * norm_scale.astype(jnp.float32)).astype(jnp.bfloat16)


def rotary(head_vals):
    seq_len, head_dim = head_vals.shape[1], head_vals.shape[3]
    half_dim = head_dim // 2
    inv_freq = ROPE_BASE ** (-2.0 * jnp.arange(half_dim, dtype=jnp.float32) / head_dim)
    angles = jnp.arange(seq_len, dtype=jnp.float32)[:, None] * inv_freq[None, :]
    cos_t = jnp.cos(angles)[:, None, :]
    sin_t = jnp.sin(angles)[:, None, :]
    first_half = head_vals[..., :half_dim]
    second_half = head_vals[..., half_dim:]
    return jnp.concatenate([first_half * cos_t - second_half * sin_t, second_half * cos_t + first_half * sin_t], axis=-1)


def dense_branch(hidden, attn_norm, w_query, w_key, w_value, w_out, ffn_norm, ffn_gate, ffn_up, ffn_down):
    n_seqs, seq_len, model_dim = hidden.shape
    n_heads, head_dim = w_out.shape[0], w_out.shape[1]
    kv_heads = w_key.shape[1] // head_dim
    q_per_kv = n_heads // kv_heads
    normed = rms_norm(hidden, attn_norm)
    queries = rotary(jnp.einsum('bsd,de->bse', normed, w_query, preferred_element_type=jnp.float32).reshape(n_seqs, seq_len, n_heads, head_dim))
    queries = queries.astype(jnp.bfloat16).reshape(n_seqs, seq_len, kv_heads, q_per_kv, head_dim)
    key_vals = rotary(jnp.einsum('bsd,de->bse', normed, w_key, preferred_element_type=jnp.float32).reshape(n_seqs, seq_len, kv_heads, head_dim)).astype(jnp.bfloat16)
    values = jnp.einsum('bsd,de->bse', normed, w_value, preferred_element_type=jnp.float32).astype(jnp.bfloat16).reshape(n_seqs, seq_len, kv_heads, head_dim)
    scores = jnp.einsum('bsgrd,btgd->bgrst', queries, key_vals, preferred_element_type=jnp.float32) * head_dim ** -0.5
    causal = jnp.arange(seq_len)[:, None] >= jnp.arange(seq_len)[None, :]
    attn_prob = jax.nn.softmax(jnp.where(causal, scores, -jnp.inf), axis=-1).astype(jnp.bfloat16)
    context = jnp.einsum('bgrst,btgd->bsgrd', attn_prob, values, preferred_element_type=jnp.float32).astype(jnp.bfloat16)
    context = context.reshape(n_seqs, seq_len, n_heads, head_dim)
    attn_out = (hidden.astype(jnp.float32) + jnp.einsum('bshd,hde->bse', context, w_out, preferred_element_type=jnp.float32)).astype(jnp.bfloat16)
    normed_ffn = rms_norm(attn_out, ffn_norm)
    hidden_act = (jax.nn.silu(jnp.einsum('bsd,df->bsf', normed_ffn, ffn_gate, preferred_element_type=jnp.float32)) * jnp.einsum('bsd,df->bsf', normed_ffn, ffn_up, preferred_element_type=jnp.float32)).astype(jnp.bfloat16)
    return attn_out.astype(jnp.float32) + jnp.einsum('bsf,fd->bsd', hidden_act, ffn_down, preferred_element_type=jnp.float32)


def route_gates(normed, w_router, choice_ids):
    logits = jnp.einsum('...d,de->...e', normed, w_router, preferred_element_type=jnp.float32)
    return jax.nn.softmax(jnp.take_along_axis(logits, choice_ids, axis=-1), axis=-1)


def expert_ffn(expert_in, exp_gate, exp_up, exp_down):
    z_gate = jnp.einsum('egcd,edf->egcf', expert_in, exp_gate, preferred_element_type=jnp.float32)
    z_up = jnp.einsum('egcd,edf->egcf', expert_in, exp_up, preferred_element_type=jnp.float32)
    hidden_act = (jax.nn.silu(z_gate) * z_up).astype(jnp.bfloat16)
    return jnp.einsum('egcf,efd->egcd', hidden_act, exp_down, preferred_element_type=jnp.float32).astype(jnp.bfloat16)


def solution(mesh):
    group_size = mesh.shape['ep']
    row_spec = P(('dp', 'ep'), None, None)
    vec_spec = P(None)
    mat_spec = P(None, None)
    cube_spec = P(None, None, None)
    expert_spec = P('ep', None, None)

    def per_device(hidden, expert_ids, slot_ids, attn_norm, w_query, w_key, w_value, w_out, ffn_norm, ffn_gate, ffn_up, ffn_down, moe_norm, w_router, exp_gate, exp_up, exp_down):
        n_seqs, seq_len, model_dim = hidden.shape
        top_k = expert_ids.shape[-1]
        tokens = n_seqs * seq_len
        local_experts = exp_gate.shape[0]
        n_experts = local_experts * group_size
        capacity = CAP_FACTOR * tokens * top_k // n_experts
        normed = rms_norm(hidden.reshape(tokens, model_dim), moe_norm)
        choice_ids = expert_ids.reshape(tokens, top_k)
        gate_vals = route_gates(normed, w_router, choice_ids)
        buf_pos = choice_ids * capacity + slot_ids.reshape(tokens, top_k)
        owner_tok = jnp.full((n_experts * capacity,), tokens, jnp.int32).at[buf_pos.reshape(-1)].set(jnp.arange(tokens * top_k, dtype=jnp.int32) // top_k)
        padded = jnp.concatenate([normed, jnp.zeros((1, model_dim), jnp.bfloat16)], axis=0)
        send_buf = jnp.take(padded, owner_tok, axis=0).reshape(group_size, local_experts, capacity, model_dim)
        recv_buf = lax.all_to_all(send_buf, 'ep', 0, 1)
        expert_out = expert_ffn(recv_buf, exp_gate, exp_up, exp_down)
        back_buf = lax.all_to_all(expert_out, 'ep', 1, 0).reshape(n_experts * capacity, model_dim)
        picked = jnp.take(back_buf, buf_pos.reshape(-1), axis=0).reshape(tokens, top_k, model_dim)
        moe_out = jnp.sum(gate_vals[:, :, None] * picked.astype(jnp.float32), axis=1)
        dense_out = dense_branch(hidden, attn_norm, w_query, w_key, w_value, w_out, ffn_norm, ffn_gate, ffn_up, ffn_down).reshape(tokens, model_dim)
        return (dense_out + moe_out).astype(jnp.bfloat16).reshape(n_seqs, seq_len, model_dim)

    return jax.shard_map(per_device, mesh=mesh, in_specs=(row_spec, row_spec, row_spec, vec_spec, mat_spec, mat_spec, mat_spec, cube_spec, vec_spec, mat_spec, mat_spec, mat_spec, vec_spec, mat_spec, expert_spec, expert_spec, expert_spec), out_specs=row_spec, check_vma=False)
```

profile of v0, /device:TPU:84, one launch (start us, length us, event | category | flops | bytes accessed | tf_op | source)
XLA Modules:
  0.0 1054.9 jit_solution(4453912537473205493)
XLA Ops:
  1.2 8.1 scatter_custom_fusion
  15.3 47.8 %gather_fusion = bf16[6144,2048]{1,0:T(8,128)(2,1)} fusion(bf16[257,2048]{1,0:T(8,128)(2,1)} %concatenate.32, s32[6144]{0:T(1024)S(1)} %fusion.67), kind=kCustom, calls=%fused_computation | custom fusion | bytes 50356224 | tf_op jit(solution)/shard_map/jit(_take)/gather | solution.py:83
  63.1 12.6 %select_bitcast_fusion = bf16[128,1,1,48,2048]{4,3,2,1,0:T(8,128)(2,1)S(1)} fusion(bf16[128,1,1,48,2048]{4,3,0,2,1:T(8,128)(2,1)} %bitcast.172, pred[128,48]{1,0:T(8,128)(4,1)S(1)} %broadcast_in_dim.66), kind=kLoop, calls=%fused_computation.9 | loop fusion | flops 12582912 | bytes 50337792 | tf_op jit(solution)/shard_map/jit(_take)/select_n | solution.py:83
  75.6 326.5 %all_to_all.8 = bf16[128,1,1,48,2048]{4,3,2,1,0:T(8,128)(2,1)} all-to-all(bf16[128,1,1,48,2048]{4,3,2,1,0:T(8,128)(2,1)S(1)} %select_bitcast_fusion), channel_id=1, replica_groups=mesh['dp'=1,'ep'=128] {'ep'}, dimensions={0} | all-to-all | bytes 50331648 | tf_op jit(solution)/shard_map/all_to_all | solution.py:84
  402.1 43.8 %fusion = f32[128,48,768]{2,0,1:T(8,128)} fusion(bf16[128,1,1,48,2048]{4,3,2,1,0:T(8,128)(2,1)} %all_to_all.8, bf16[1,2048,768]{2,1,0:T(8,128)(2,1)S(1)} %copy-done.15), kind=kOutput, calls=%fused_computation.4 | convolution fusion | flops 19327352832 | bytes 47185920 | tf_op jit(solution)/shard_map/egcd,edf->egcf/dot_general | solution.py:57
  445.9 64.3 %multiply_convert_fusion.clone.4 = bf16[128,48,768]{2,0,1:T(8,128)(2,1)} fusion(f32[128,48,768]{2,0,1:T(8,128)} %fusion, bf16[128,1,1,48,2048]{4,3,2,1,0:T(8,128)(2,1)} %all_to_all.8, bf16[1,2048,768]{2,1,0:T(8,128)(2,1)} %param.31), kind=kOutput, calls=%fused_computation.12.clone.clone.clone.1 | convolution fusion | flops 19355664384 | bytes 56623104 | tf_op jit(solution)/shard_map/egcd,edf->egcf/dot_general | solution.py:56
  510.2 26.7 %convert_bitcast_fusion = bf16[1,1,128,48,2048]{4,2,3,1,0:T(8,128)(2,1)} fusion(bf16[1,768,2048]{2,1,0:T(8,128)(2,1)S(1)} %copy-done, bf16[128,48,768]{2,0,1:T(8,128)(2,1)} %multiply_convert_fusion.clone.4), kind=kOutput, calls=%fused_computation.8 | convolution fusion | flops 19339935744 | bytes 37748736 | tf_op jit(solution)/shard_map/egcf,efd->egcd/dot_general | solution.py:59
  537.0 26.8 %copy.57 = bf16[1,1,128,48,2048]{4,3,1,0,2:T(8,128)(2,1)} copy(bf16[1,1,128,48,2048]{4,2,3,1,0:T(8,128)(2,1)} %convert_bitcast_fusion) | data formatting | bytes 50331648 | tf_op jit(solution)/shard_map/broadcast_in_dim | solution.py:86
  563.8 31.1 %all-to-all-start.1 = ((bf16[1,1,128,48,2048]{4,3,1,0,2:T(8,128)(2,1)}), bf16[1,1,128,48,2048]{4,3,1,0,2:T(8,128)(2,1)}, u32[]{:S(2)}, u32[]{:S(2)}) async-start(bf16[1,1,128,48,2048]{4,3,1,0,2:T(8,128)(2,1)} %copy.57), calls=%async_computation.1 | async-start | bytes 50331648 | tf_op jit(solution)/shard_map/all_to_all | solution.py:86
  595.8 3.0 convolution_convert_fusion
  600.4 13.1 %gather_fusion.2 = f32[2048]{0:T(1024)S(1)} fusion(f32[256,128]{1,0:T(8,128)S(1)} %fusion.85, s32[2048]{0:T(1024)S(1)} %reshape.432), kind=kCustom, calls=%fused_computation.2 | custom fusion | bytes 32768 | tf_op jit(solution)/shard_map/jit(take_along_axis)/gather | solution.py:52
  613.6 3.9 copy.63
  617.5 22.6 %copy.66 = bf16[4096,2048]{1,0:T(8,128)(2,1)} copy(bf16[4096,2048]{0,1:T(8,128)(2,1)} %bitcast.175) | data formatting | bytes 33554432 | tf_op jit(solution)/shard_map/bsd,de->bse/dot_general | solution.py:35
  640.4 8.4 convolution_bitcast_fusion.1
  650.5 2.8 copy.46
  655.6 2.6 convolution_bitcast_fusion.2
  658.3 2.6 fusion.13
  662.8 3.6 fusion.42
  668.2 6.3 fusion.32
  674.7 14.7 %fusion.48 = f32[256,6144]{1,0:T(8,128)} fusion(bf16[2048,6144]{1,0:T(8,128)(2,1)} %param.26, bf16[1,256,2048]{2,1,0:T(8,128)(2,1)S(1)} %get-tuple-element.14, f32[2048]{0:T(1024)S(1)} %convert_element_type.89, f32[256]{0:T(256)S(1)} %add_rsqrt_fusion.1), kind=kOutput, calls=%fused_computation.65 | convolution fusion | flops 6444548096 | bytes 32515072 | tf_op jit(solution)/shard_map/bsd,df->bsf/dot_general | solution.py:46
  689.4 296.9 %all-to-all-done.1 = bf16[1,1,128,48,2048]{4,3,1,0,2:T(8,128)(2,1)} async-done(((bf16[1,1,128,48,2048]{4,3,1,0,2:T(8,128)(2,1)}), bf16[1,1,128,48,2048]{4,3,1,0,2:T(8,128)(2,1)}, u32[]{:S(2)}, u32[]{:S(2)}) %all-to-all-start.1) | async-done | bytes 25165856 | tf_op jit(solution)/shard_map/all_to_all | solution.py:86
  986.3 27.7 %gather_fusion.1 = bf16[2048,2048]{1,0:T(8,128)(2,1)} fusion(bf16[6144,2048]{1,0:T(8,128)(2,1)} %bitcast.41, s32[2048]{0:T(1024)S(1)} %broadcast_clamp_fusion), kind=kCustom, calls=%fused_computation.1 | custom fusion | bytes 16785408 | tf_op jit(solution)/shard_map/jit(_take)/gather | solution.py:87
  1014.0 10.6 %multiply_reduce_fusion = f32[256,2048]{1,0:T(8,128)} fusion(bf16[2048,2048]{1,0:T(8,128)(2,1)} %gather_fusion.1, f32[256,8]{1,0:T(8,128)S(1)} %fusion.63, pred[256,8]{1,0:T(8,128)(4,1)S(1)} %compare_and_fusion), kind=kLoop, calls=%fused_computation.13 | loop fusion | flops 16252928 | bytes 10496000 | tf_op jit(solution)/shard_map/reduce_sum | solution.py:88
  1024.6 30.1 %fusion.28 = bf16[1,256,2048]{2,1,0:T(8,128)(2,1)} fusion(bf16[6144,2048]{1,0:T(8,128)(2,1)} %param.28, bf16[2048,6144]{1,0:T(8,128)(2,1)} %param.27, f32[256,6144]{1,0:T(8,128)} %fusion.48, bf16[1,256,2048]{2,1,0:T(8,128)(2,1)} %copy-done.7, f32[256,2048]{1,0:T(8,128)} %multiply_reduce_fusion, f32[2048]{0:T(1024)S(1)} %convert_element_type.89, ...), kind=kOutput, calls=%fused_computation.44 | convolution fusion | flops 12898533376 | bytes 60826624 | tf_op jit(solution)/shard_map/bsf,fd->bsd/dot_general | solution.py:47
  (79 shorter events, 17.7 us)
Async XLA Ops:
  0.0 510.2 %copy-start = (bf16[1,768,2048]{2,1,0:T(8,128)(2,1)S(1)}, bf16[1,768,2048]{2,1,0:T(8,128)(2,1)}, u32[]{:S(2)}) copy-start(bf16[1,768,2048]{2,1,0:T(8,128)(2,1)} %param.33) | copy-start | bytes 9437188
  1.2 8.1 copy-start.11
  13.1 1.0 copy-start.3
  75.6 326.5 %copy-start.15 = (bf16[1,2048,768]{2,1,0:T(8,128)(2,1)S(1)}, bf16[1,2048,768]{2,1,0:T(8,128)(2,1)}, u32[]{:S(2)}) copy-start(bf16[1,2048,768]{2,1,0:T(8,128)(2,1)} %param.32) | copy-start | bytes 9437188
  563.8 31.1 %copy-start.9 = (s32[1,256,8]{1,2,0:T(8,128)S(1)}, s32[1,256,8]{1,2,0:T(8,128)}, u32[]{:S(2)}) copy-start(s32[1,256,8]{1,2,0:T(8,128)} %param.18) | copy-start | bytes 24580
  563.8 31.3 %copy-start.10 = (s32[1,256,8]{1,2,0:T(8,128)S(1)}, s32[1,256,8]{1,2,0:T(8,128)}, u32[]{:S(2)}) copy-start(s32[1,256,8]{1,2,0:T(8,128)} %param.19) | copy-start | bytes 24580
  563.8 31.4 %copy-start.13 = (bf16[2048]{0:T(1024)(128)(2,1)S(1)}, bf16[2048]{0:T(1024)(128)(2,1)}, u32[]{:S(2)}) copy-start(bf16[2048]{0:T(1024)(128)(2,1)} %param.20) | copy-start | bytes 12292
  563.8 31.5 %copy-start.14 = (bf16[2048]{0:T(1024)(128)(2,1)S(1)}, bf16[2048]{0:T(1024)(128)(2,1)}, u32[]{:S(2)}) copy-start(bf16[2048]{0:T(1024)(128)(2,1)} %param.25) | copy-start | bytes 12292
  563.8 31.7 %copy-start.2 = (bf16[1,256,2048]{2,1,0:T(8,128)(2,1)S(1)}, bf16[1,256,2048]{2,1,0:T(8,128)(2,1)}, u32[]{:S(2)}) copy-start(bf16[1,256,2048]{2,1,0:T(8,128)(2,1)} %param.17) | copy-start | bytes 3145732
  563.8 422.5 %all-to-all-start.1 = ((bf16[1,1,128,48,2048]{4,3,1,0,2:T(8,128)(2,1)}), bf16[1,1,128,48,2048]{4,3,1,0,2:T(8,128)(2,1)}, u32[]{:S(2)}, u32[]{:S(2)}) async-start(bf16[1,1,128,48,2048]{4,3,1,0,2:T(8,128)(2,1)} %copy.57), calls=%async_computation.1 | async-start | bytes 50331648 | tf_op jit(solution)/shard_map/all_to_all | solution.py:86
  594.9 5.0 copy-start.4
  595.0 5.0 copy-start.8
  655.2 3.1 copy-start.5
  655.2 3.1 copy-start.6
  660.9 5.5 slice-start
  662.7 3.7 slice-start.1
  662.7 4.1 slice-start.2
  662.7 5.4 slice-start.3
  668.1 6.3 copy-start.12
  674.4 15.0 %copy-start.7 = (bf16[1,256,2048]{2,1,0:T(8,128)(2,1)}, bf16[1,256,2048]{2,1,0:T(8,128)(2,1)S(1)}, u32[]{:S(2)}) copy-start(bf16[1,256,2048]{2,1,0:T(8,128)(2,1)S(1)} %get-tuple-element.14) | copy-start | bytes 3145732
  1024.6 30.1 %copy-start.1 = (bf16[1,768,2048]{2,1,0:T(8,128)(2,1)S(1)}, bf16[1,768,2048]{2,1,0:T(8,128)(2,1)}, u32[]{:S(2)}) copy-start(bf16[1,768,2048]{2,1,0:T(8,128)(2,1)} %param.33) | copy-start | bytes 9437188
where the time goes:
time: 1070 us; the launch traced here: 1050 us
  blocking collectives  326 us (30%)
  waiting for transfers between devices  297 us (28%)
  matrix products  207 us (19%)
  local copies, waits for them, and re-layouts  161 us (15%)
  other arithmetic  32.5 us (3%)
  starting transfers between devices  31.1 us (3%)
    all_to_all x1, blocking collectives, per_device(): recv_buf = lax.all_to_all(send_buf, 'ep', 0, 1)  326 us
    all_to_all x1, waiting for transfers between devices, per_device(): lax.all_to_all(expert_out, 'ep', 1, 0)  297 us
    dot_general x1, matrix products, expert_ffn(): jnp.einsum('egcd,edf->egcf', expert_in, exp_gate, preferred_element_type=...  64.3 us
    gather x1, local copies, waits for them, and re-layouts, per_device(): jnp.take(padded, owner_tok, axis=0)  47.8 us
    dot_general x1, matrix products, expert_ffn(): jnp.einsum('egcd,edf->egcf', expert_in, exp_up, preferred_element_type=jn...  43.8 us
    all_to_all x1, starting transfers between devices, per_device(): lax.all_to_all(expert_out, 'ep', 1, 0)  31.1 us
    dot_general x1, matrix products, dense_branch(): jnp.einsum('bsf,fd->bsd', hidden_act, ffn_down, preferred_element_type=jn...  30.1 us
    gather x1, local copies, waits for them, and re-layouts, per_device(): jnp.take(back_buf, buf_pos.reshape(-1), axis=0)  27.7 us
  transfers between devices with their start and end apart: 1, of which 1 were waited for; matrix products, arithmetic and copies ran while one was open for 9% of the time, Pallas kernels for 0%

commit v1 on v0

v1 whole, which is shorter than its diff:
```python
import functools
import math

import jax
import jax.numpy as jnp
from jax import lax
from jax.experimental import pallas as pl
from jax.experimental.pallas import tpu as pltpu
from jax.sharding import PartitionSpec as P

RMS_EPS = 1e-6
ROPE_BASE = 10000.0
CAP_FACTOR = 3
N_CHUNKS = 3
MESH = pl.DeviceIdType.MESH

BF16, F32, I32 = jnp.bfloat16, jnp.float32, jnp.int32

AXES = ('z', 'y', 'x', 'c')
LINE = ('z', 'x', 'y')
PLANE = (('y', 'x'), ('z', 'y'), ('z', 'x'))


def rms_norm(row_vals, norm_scale):
    as_float = row_vals.astype(F32)
    inv_rms = lax.rsqrt(jnp.mean(as_float * as_float, axis=-1, keepdims=True) + RMS_EPS)
    return (as_float * inv_rms * norm_scale.astype(F32)).astype(BF16)


def rotary(head_vals):
    seq_len, _, head_dim = head_vals.shape
    half_dim = head_dim // 2
    inv_freq = ROPE_BASE ** (-2.0 * jnp.arange(half_dim, dtype=F32) / head_dim)
    angles = jnp.arange(seq_len, dtype=F32)[:, None] * inv_freq[None, :]
    cos_t = jnp.cos(angles)[:, None, :]
    sin_t = jnp.sin(angles)[:, None, :]
    first_half = head_vals[..., :half_dim]
    second_half = head_vals[..., half_dim:]
    return jnp.concatenate([first_half * cos_t - second_half * sin_t, second_half * cos_t + first_half * sin_t], axis=-1)


def dense_sequence(rows, attn_norm, w_query, w_key, w_value, w_out, ffn_norm, ffn_gate, ffn_up, ffn_down):
    seq_len, model_dim = rows.shape
    n_heads, head_dim = w_out.shape[0], w_out.shape[1]
    kv_heads = w_key.shape[1] // head_dim
    q_per_kv = n_heads // kv_heads
    normed = rms_norm(rows, attn_norm)
    q_flat, k_flat, v_flat = lax.optimization_barrier(
        (
            jnp.dot(normed, w_query, preferred_element_type=F32),
            jnp.dot(normed, w_key, preferred_element_type=F32),
            jnp.dot(normed, w_value, preferred_element_type=F32).astype(BF16),
        )
    )
    queries = rotary(q_flat.reshape(seq_len, n_heads, head_dim)).astype(BF16).reshape(seq_len, kv_heads, q_per_kv, head_dim)
    key_vals = rotary(k_flat.reshape(seq_len, kv_heads, head_dim)).astype(BF16)
    values = v_flat.reshape(seq_len, kv_heads, head_dim)
    scores = jnp.einsum('sgrd,tgd->grst', queries, key_vals, preferred_element_type=F32) * head_dim ** -0.5
    causal = jnp.arange(seq_len)[:, None] >= jnp.arange(seq_len)[None, :]
    attn_prob = jax.nn.softmax(jnp.where(causal, scores, -jnp.inf), axis=-1).astype(BF16)
    context = jnp.einsum('grst,tgd->sgrd', attn_prob, values, preferred_element_type=F32).astype(BF16)
    context = context.reshape(seq_len, n_heads * head_dim)
    attn_out = (rows.astype(F32) + jnp.dot(context, w_out.reshape(n_heads * head_dim, model_dim), preferred_element_type=F32)).astype(BF16)
    normed_ffn = rms_norm(attn_out, ffn_norm)
    hidden_act = (jax.nn.silu(jnp.dot(normed_ffn, ffn_gate, preferred_element_type=F32)) * jnp.dot(normed_ffn, ffn_up, preferred_element_type=F32)).astype(BF16)
    return attn_out.astype(F32) + jnp.dot(hidden_act, ffn_down, preferred_element_type=F32)


def torus_of(n_devices):
    side = round((n_devices // 2) ** (1 / 3))
    assert side ** 3 * 2 == n_devices
    return side


def column_parts(model):
    lanes = model // 128
    first = -(-lanes // 3)
    second = -(-(lanes - first) // 2)
    ends = (0, first * 128, (first + second) * 128, model)
    return tuple((ends[p], ends[p + 1]) for p in range(3))


def expert_index(p, member, line_pos, side):
    pair, core = member // 2, member % 2
    a, b = pair // side, pair % side
    place = {PLANE[p][0]: a, PLANE[p][1]: b, LINE[p]: line_pos}
    return ((place['z'] * side + place['y']) * side + place['x']) * 2 + core


def slot_keys(p, shape, dim, chunk, line_pos, side, capacity):
    slots = capacity // N_CHUNKS
    row = lax.broadcasted_iota(I32, shape, dim)
    return expert_index(p, row // slots, line_pos, side) * capacity + chunk * slots + row % slots


def pick_kernel(place_ref, *refs, side, capacity):
    tokens_refs, key_refs, out_refs = refs[:3], refs[3:6], refs[6:]
    chunk = pl.program_id(1)
    for p in range(3):
        rows, n_tokens = out_refs[p].shape[0], tokens_refs[p].shape[1]
        wanted = slot_keys(p, (rows, n_tokens), 0, chunk, place_ref[p], side, capacity)
        keys = key_refs[p][0]
        hit = wanted == keys[0:1, :]
        for j in range(1, keys.shape[0]):
            hit = jnp.logical_or(hit, wanted == keys[j : j + 1, :])
        pick = jnp.where(hit, 1.0, 0.0).astype(BF16)
        out_refs[p][...] = jnp.dot(pick, tokens_refs[p][0], preferred_element_type=F32).astype(BF16)


def pick_rows(place, tokens, keys_t, side, capacity):
    members, slots = side * side * 2, capacity // N_CHUNKS
    rows = members * slots
    return pl.pallas_call(
        functools.partial(pick_kernel, side=side, capacity=capacity),
        out_shape=[jax.ShapeDtypeStruct((N_CHUNKS * side * rows, t.shape[2]), BF16) for t in tokens],
        grid=(side, N_CHUNKS),
        in_specs=[pl.BlockSpec(memory_space=pltpu.SMEM)]
        + [pl.BlockSpec((1,) + t.shape[1:], lambda d, k: (d, 0, 0)) for t in tokens]
        + [pl.BlockSpec((1,) + t.shape[1:], lambda d, k: (d, 0, 0)) for t in keys_t],
        out_specs=[pl.BlockSpec((rows, t.shape[2]), lambda d, k: (k * side + d, 0)) for t in tokens],
        compiler_params=pltpu.CompilerParams(vmem_limit_bytes=40 * 1024 * 1024),
        cost_estimate=pl.CostEstimate(
            flops=sum(2 * N_CHUNKS * side * rows * t.shape[1] * t.shape[2] for t in tokens),
            bytes_accessed=sum(2 * N_CHUNKS * side * rows * t.shape[2] for t in tokens),
            transcendentals=0,
        ),
    )(place, *tokens, *keys_t)


def weigh_kernel(place_ref, *refs, side, capacity):
    row_refs, key_refs, gate_refs, out_refs = refs[:3], refs[3:6], refs[6:9], refs[9:]
    chunk = pl.program_id(1)
    for p in range(3):
        rows, n_tokens = row_refs[p].shape[0], out_refs[p].shape[1]
        held = slot_keys(p, (n_tokens, rows), 1, chunk, place_ref[p], side, capacity)
        keys, gates = key_refs[p][0], gate_refs[p][0]
        weight = jnp.zeros((n_tokens, rows), F32)
        for j in range(keys.shape[1]):
            weight = jnp.where(held == keys[:, j : j + 1], gates[:, j : j + 1], weight)
        high = weight.astype(BF16)
        rest = weight - high.astype(F32)
        middle = rest.astype(BF16)
        low = (rest - middle.astype(F32)).astype(BF16)
        y = row_refs[p][...]
        total = jnp.dot(high, y, preferred_element_type=F32) + (
            jnp.dot(middle, y, preferred_element_type=F32) + jnp.dot(low, y, preferred_element_type=F32)
        )

        @pl.when(chunk == 0)
        def _():
            out_refs[p][0] = total

        @pl.when(chunk > 0)
        def _():
            out_refs[p][0] += total


def weigh_rows(place, rows, keys, gates, side, capacity):
    block = side * side * 2 * capacity // N_CHUNKS
    n_tokens = keys[0].shape[1]
    by_source = lambda a: pl.BlockSpec((1,) + a.shape[1:], lambda d, k: (d, 0, 0))
    return pl.pallas_call(
        functools.partial(weigh_kernel, side=side, capacity=capacity),
        out_shape=[jax.ShapeDtypeStruct((side, n_tokens, r.shape[1]), F32) for r in rows],
        grid=(side, N_CHUNKS),
        in_specs=[pl.BlockSpec(memory_space=pltpu.SMEM)]
        + [pl.BlockSpec((block, r.shape[1]), lambda d, k: (k * side + d, 0)) for r in rows]
        + [by_source(a) for a in keys]
        + [by_source(a) for a in gates],
        out_specs=[pl.BlockSpec((1, n_tokens, r.shape[1]), lambda d, k: (d, 0, 0)) for r in rows],
        compiler_params=pltpu.CompilerParams(
            dimension_semantics=("arbitrary", "arbitrary"), vmem_limit_bytes=40 * 1024 * 1024
        ),
        cost_estimate=pl.CostEstimate(
            flops=sum(6 * r.shape[0] * n_tokens * r.shape[1] for r in rows),
            bytes_accessed=sum(2 * r.size for r in rows),
            transcendentals=0,
        ),
    )(place, *rows, *keys, *gates)


def expert_kernel(*refs, side, slots, parts, f_chunk, d_chunk):
    sends, weights_hbm = refs[0:3], refs[3:6]
    results, arrivals, outputs = refs[6:9], refs[9:12], refs[12:15]
    weights, bounces = refs[15:18], refs[18:21]
    x_buf, act_buf, y_buf, go_send, go_recv, back_send, back_recv, own_sem, weight_sem, in_sem, out_sem = refs[21:]
    members = side * side * 2
    me = {axis: lax.axis_index(axis) for axis in AXES}

    def member(p, place):
        return (place[PLANE[p][0]] * side + place[PLANE[p][1]]) * 2 + place['c']

    def rows_of(ref, p, chunk, place):
        spot = [pl.ds(0, side) if axis == LINE[p] else place[axis] for axis in ('y', 'x', 'c', 'z')]
        return ref.at[tuple([chunk] + spot)]

    def peer(p, offset):
        first, second = PLANE[p]
        place = dict(me)
        place[first] = lax.rem(me[first] + offset // (2 * side), side)
        place[second] = lax.rem(me[second] + lax.rem(offset // 2, side), side)
        place['c'] = lax.rem(me['c'] + lax.rem(offset, 2), 2)
        return place

    def go(chunk, p, place):
        return pltpu.make_async_remote_copy(
            src_ref=sends[p].at[chunk, pl.ds(0, side), member(p, place)],
            dst_ref=rows_of(arrivals[p], p, chunk, me),
            send_sem=go_send.at[chunk, p],
            recv_sem=go_recv.at[chunk, p],
            device_id=tuple(place[axis] for axis in AXES),
            device_id_type=MESH,
        )

    def back(chunk, p, place):
        return pltpu.make_async_remote_copy(
            src_ref=rows_of(outputs[p], p, chunk, place),
            dst_ref=results[p].at[chunk, pl.ds(0, side), member(p, me)],
            send_sem=back_send.at[chunk, p],
            recv_sem=back_recv.at[chunk, p],
            device_id=tuple(place[axis] for axis in AXES),
            device_id_type=MESH,
        )

    def send_all(copy, chunk):
        def one(offset, carry):
            for p in range(3):
                copy(chunk, p, peer(p, offset)).start()
            return carry

        lax.fori_loop(1, members, one, 0)

    def wait_bytes(ref, sem):
        pltpu.make_async_copy(ref, ref, sem).wait()

    loads = [pltpu.make_async_copy(weights_hbm[i], weights[i], weight_sem.at[i]) for i in range(3)]
    for load in loads:
        load.start()
    for chunk in range(N_CHUNKS):
        send_all(go, chunk)
    for p in range(3):
        for chunk in range(N_CHUNKS):
            pltpu.make_async_copy(sends[p].at[chunk, pl.ds(0, side), member(p, me)], bounces[p].at[chunk], own_sem.at[chunk, p]).start()
    for p in range(3):
        for chunk in range(N_CHUNKS):
            pltpu.make_async_copy(sends[p].at[chunk, pl.ds(0, side), member(p, me)], bounces[p].at[chunk], own_sem.at[chunk, p]).wait()
            pltpu.make_async_copy(bounces[p].at[chunk], rows_of(arrivals[p], p, chunk, me), go_recv.at[chunk, p]).start()
    for load in loads:
        load.wait()

    def fetch(chunk, y, slot):
        return [
            pltpu.make_async_copy(arrivals[p].at[chunk, y], x_buf.at[slot, :, :, :, :, pl.ds(lo, hi - lo)], in_sem.at[slot, p])
            for p, (lo, hi) in enumerate(parts)
        ]

    def flush(chunk, y, slot):
        return [
            pltpu.make_async_copy(y_buf.at[slot, :, :, :, :, pl.ds(lo, hi - lo)], outputs[p].at[chunk, y], out_sem.at[slot, p])
            for p, (lo, hi) in enumerate(parts)
        ]

    width, model = act_buf.shape[1], x_buf.shape[-1]
    group = x_buf.shape[1:-1]
    rows = math.prod(group)
    gate_ref, up_ref, down_ref = weights

    def one_chunk(chunk, carry):
        for p in range(3):
            wait_bytes(arrivals[p].at[chunk], go_recv.at[chunk, p])
        for copy in fetch(chunk, 0, 0):
            copy.start()

        def one_tile(y, carry):
            slot = lax.rem(y, 2)

            @pl.when(y + 1 < side)
            def _():
                for copy in fetch(chunk, y + 1, 1 - slot):
                    copy.start()

            for copy in fetch(chunk, y, slot):
                copy.wait()

            @pl.when(y >= 2)
            def _():
                for copy in flush(chunk, y - 2, slot):
                    copy.wait()

            x = x_buf[slot].reshape(rows, model)
            for lo in range(0, width, f_chunk):
                cols = slice(lo, lo + f_chunk)
                z = jnp.dot(x, gate_ref[:, cols], preferred_element_type=F32)
                u = jnp.dot(x, up_ref[:, cols], preferred_element_type=F32)
                act_buf[:, cols] = (jax.nn.silu(z) * u).astype(BF16)
            act = act_buf[...]
            for lo in range(0, model, d_chunk):
                cols = slice(lo, lo + d_chunk)
                y_rows = jnp.dot(act, down_ref[:, cols], preferred_element_type=F32).astype(BF16)
                y_buf[slot, :, :, :, :, cols] = y_rows.reshape(group + (d_chunk,))
            for copy in flush(chunk, y, slot):
                copy.start()
            return carry

        lax.fori_loop(0, side, one_tile, 0)
        for y in range(max(side - 2, 0), side):
            for copy in flush(chunk, y, y % 2):
                copy.wait()
        send_all(back, chunk)
        for p in range(3):
            pltpu.make_async_copy(rows_of(outputs[p], p, chunk, me), bounces[p].at[chunk], own_sem.at[chunk, p]).start()
        for p in range(3):
            pltpu.make_async_copy(rows_of(outputs[p], p, chunk, me), bounces[p].at[chunk], own_sem.at[chunk, p]).wait()
            pltpu.make_async_copy(bounces[p].at[chunk], results[p].at[chunk, pl.ds(0, side), member(p, me)], back_recv.at[chunk, p]).start()
        return carry

    for chunk in range(N_CHUNKS):
        one_chunk(chunk, 0)
    for chunk in range(N_CHUNKS):
        for p in range(3):
            wait_bytes(results[p].at[chunk], back_recv.at[chunk, p])
            wait_bytes(sends[p].at[chunk, pl.ds(0, side), pl.ds(0, members - 1)], go_send.at[chunk, p])
            wait_bytes(sends[p].at[chunk, pl.ds(0, side), pl.ds(0, members - 1)], back_send.at[chunk, p])


def exchange_experts(sends, gate, up, down, side, capacity):
    slots = capacity // N_CHUNKS
    model, width = gate.shape
    parts = column_parts(model)
    members = side * side * 2
    widths = [hi - lo for lo, hi in parts]
    there = [jax.ShapeDtypeStruct((N_CHUNKS, side, side, 2, side, slots, w), BF16) for w in widths]
    home = [jax.ShapeDtypeStruct((N_CHUNKS, side, members, slots, w), BF16) for w in widths]
    group = (side, 2, side, slots)
    anywhere = pl.BlockSpec(memory_space=pl.ANY)
    total = members * side * capacity
    out = pl.pallas_call(
        functools.partial(
            expert_kernel, side=side, slots=slots, parts=parts, f_chunk=min(256, width), d_chunk=min(512, model)
        ),
        out_shape=home + there + there,
        in_specs=[anywhere] * 6,
        out_specs=[anywhere] * 9,
        scratch_shapes=[
            pltpu.VMEM((model, width), BF16),
            pltpu.VMEM((model, width), BF16),
            pltpu.VMEM((width, model), BF16),
            *[pltpu.VMEM((N_CHUNKS, side, slots, w), BF16) for w in widths],
            pltpu.VMEM((2,) + group + (model,), BF16),
            pltpu.VMEM((math.prod(group), width), BF16),
            pltpu.VMEM((2,) + group + (model,), BF16),
            *[pltpu.SemaphoreType.DMA((N_CHUNKS, 3)) for _ in range(5)],
            pltpu.SemaphoreType.DMA((3,)),
            pltpu.SemaphoreType.DMA((2, 3)),
            pltpu.SemaphoreType.DMA((2, 3)),
        ],
        compiler_params=pltpu.CompilerParams(has_side_effects=True, vmem_limit_bytes=56 * 1024 * 1024),
        cost_estimate=pl.CostEstimate(flops=6 * total * model * width, bytes_accessed=8 * total * model, transcendentals=0),
    )(*[s.reshape(N_CHUNKS, side, members, slots, s.shape[1]) for s in sends], gate, up, down)
    return [r.reshape(-1, r.shape[-1]) for r in out[:3]]


def moe_branch(rows, choice_ids, slots, moe_norm, w_router, exp_gate, exp_up, exp_down, side):
    tokens, model = rows.shape
    top_k = choice_ids.shape[1]
    n_experts = side ** 3 * 2
    capacity = CAP_FACTOR * tokens * top_k // n_experts
    parts = column_parts(model)
    keys = choice_ids * capacity + slots
    normed = rms_norm(rows, moe_norm)
    logits = jnp.dot(normed, w_router, preferred_element_type=F32)
    chosen = choice_ids[:, :, None] == jnp.arange(n_experts, dtype=I32)
    gates = jax.nn.softmax(jnp.sum(jnp.where(chosen, logits[:, None, :], 0.0), axis=-1), axis=-1)
    place = jnp.stack([lax.axis_index(axis) for axis in LINE]).astype(I32)
    keys_t = keys.T
    line_tokens = [lax.all_gather(normed[:, lo:hi], axis) for axis, (lo, hi) in zip(LINE, parts)]
    line_keys_t = [lax.all_gather(keys_t, axis) for axis in LINE]
    line_keys = [k.transpose(0, 2, 1) for k in line_keys_t]
    line_gates = [lax.all_gather(gates, axis) for axis in LINE]
    sends = pick_rows(place, line_tokens, line_keys_t, side, capacity)
    returned = exchange_experts(sends, exp_gate, exp_up, exp_down, side, capacity)
    partial = weigh_rows(place, returned, line_keys, line_gates, side, capacity)
    return jnp.concatenate([lax.psum_scatter(m, axis, scatter_dimension=0) for m, axis in zip(partial, LINE)], axis=-1)


def solution(mesh):
    group_size = mesh.shape['ep']
    side = torus_of(group_size)
    torus = jax.sharding.Mesh(mesh.devices.reshape(side, side, side, 2), AXES)
    row_spec = P(AXES, None, None)
    vec_spec = P(None)
    mat_spec = P(None, None)
    cube_spec = P(None, None, None)
    expert_spec = P(AXES, None, None)

    def per_device(hidden, expert_ids, slot_ids, attn_norm, w_query, w_key, w_value, w_out, ffn_norm, ffn_gate, ffn_up, ffn_down, moe_norm, w_router, exp_gate, exp_up, exp_down):
        n_seqs, seq_len, model = hidden.shape
        assert n_seqs == 1 and exp_gate.shape[0] == 1
        rows = hidden[0]
        moe = moe_branch(rows, expert_ids[0], slot_ids[0], moe_norm, w_router, exp_gate[0], exp_up[0], exp_down[0], side)
        dense = dense_sequence(rows, attn_norm, w_query, w_key, w_value, w_out, ffn_norm, ffn_gate, ffn_up, ffn_down)
        return (dense + moe).astype(BF16).reshape(hidden.shape)

    return jax.shard_map(per_device, mesh=torus, in_specs=(row_spec, row_spec, row_spec, vec_spec, mat_spec, mat_spec, mat_spec, cube_spec, vec_spec, mat_spec, mat_spec, mat_spec, vec_spec, mat_spec, expert_spec, expert_spec, expert_spec), out_specs=row_spec, check_vma=False)
```

time: 1070 us -> 843 us (0.79)
  the two profiles are of different devices: /device:TPU:84 before, /device:TPU:0 now
where the time goes in v1:
time: 843 us; the launch traced here: 841 us
  Pallas kernels  553 us (66%)
  waiting for transfers between devices  85.8 us (10%)
  blocking collectives  73.2 us (9%)
  matrix products  70.2 us (8%)
  local copies, waits for them, and re-layouts  30.8 us (4%)
  other arithmetic  14.1 us (2%)
  between operations  14 us (2%)
    pallas_call x1, Pallas kernels, exchange_experts(): pl.pallas_call(functools.partial(expert_kernel, side=side, slots=slots, p...  461 us
    reduce_scatter x3, waiting for transfers between devices, moe_branch(): lax.psum_scatter(m, axis, scatter_dimension=0)  83.2 us
    pallas_call x1, Pallas kernels, weigh_rows(): pl.pallas_call(functools.partial(weigh_kernel, side=side, capacity=capaci...  69 us
    all_gather x3, blocking collectives, moe_branch(): line_gates = [lax.all_gather(gates, axis) for axis in LINE]  37.8 us
    all_gather x3, blocking collectives, moe_branch(): line_keys_t = [lax.all_gather(keys_t, axis) for axis in LINE]  35.4 us
    dot_general x1, matrix products, dense_sequence(): jnp.dot(hidden_act, ffn_down, preferred_element_type=F32)  29.9 us
    pallas_call x1, Pallas kernels, pick_rows(): pl.pallas_call(functools.partial(pick_kernel, side=side, capacity=capacit...  23.5 us
  transfers between devices with their start and end apart: 6, of which 4 were waited for; matrix products, arithmetic and copies ran while one was open for 8% of the time, Pallas kernels for 0%

profile of v1, /device:TPU:0, one launch (start us, length us, event | category | flops | bytes accessed | tf_op | source)
XLA Modules:
  0.0 841.4 jit_solution(11472056737137767192)
XLA Ops:
  16.0 13.2 %all_gather.54 = f32[4,256,8]{1,2,0:T(8,128)S(1)} all-gather(f32[1,256,8]{1,2,0:T(8,128)S(1)} %fusion.41), channel_id=1, replica_groups=mesh['z'=4,'y'=4,'x'=4,'c'=2] {'z'}, dimensions={0}, use_global_device_ids=true | all-gather | bytes 40960 | tf_op jit(solution)/shard_map/all_gather | solution.py:379
  29.3 12.3 %all_gather.55 = f32[4,256,8]{1,2,0:T(8,128)S(1)} all-gather(f32[1,256,8]{1,2,0:T(8,128)S(1)} %fusion.41), channel_id=1, replica_groups=mesh['z'=4,'y'=4,'x'=4,'c'=2] {'x'}, dimensions={0}, use_global_device_ids=true | all-gather | bytes 40960 | tf_op jit(solution)/shard_map/all_gather | solution.py:379
  41.8 12.3 %all_gather.56 = f32[4,256,8]{1,2,0:T(8,128)S(1)} all-gather(f32[1,256,8]{1,2,0:T(8,128)S(1)} %fusion.41), channel_id=1, replica_groups=mesh['z'=4,'y'=4,'x'=4,'c'=2] {'y'}, dimensions={0}, use_global_device_ids=true | all-gather | bytes 40960 | tf_op jit(solution)/shard_map/all_gather | solution.py:379
  55.2 11.8 %all-gather.3 = s32[32,256]{1,0:T(8,128)S(1)} all-gather(s32[8,256]{1,0:T(8,128)S(1)} %fusion.42), channel_id=5, replica_groups=mesh['z'=4,'y'=4,'x'=4,'c'=2] {'z'}, dimensions={0}, use_global_device_ids=true | all-gather | bytes 40960 | tf_op jit(solution)/shard_map/all_gather | solution.py:377
  68.0 11.8 %all-gather.4 = s32[32,256]{1,0:T(8,128)S(1)} all-gather(s32[8,256]{1,0:T(8,128)S(1)} %fusion.42), channel_id=6, replica_groups=mesh['z'=4,'y'=4,'x'=4,'c'=2] {'x'}, dimensions={0}, use_global_device_ids=true | all-gather | bytes 40960 | tf_op jit(solution)/shard_map/all_gather | solution.py:377
  80.8 11.8 %all-gather.5 = s32[32,256]{1,0:T(8,128)S(1)} all-gather(s32[8,256]{1,0:T(8,128)S(1)} %fusion.42), channel_id=7, replica_groups=mesh['z'=4,'y'=4,'x'=4,'c'=2] {'y'}, dimensions={0}, use_global_device_ids=true | all-gather | bytes 40960 | tf_op jit(solution)/shard_map/all_gather | solution.py:377
  99.0 23.5 %shard_map.163 = (bf16[6144,768]{1,0:T(8,128)(2,1)}, bf16[6144,640]{1,0:T(8,128)(2,1)S(1)}, bf16[6144,640]{1,0:T(8,128)(2,1)}) custom-call(s32[3]{0:T(128)S(1)} %pad_add_fusion.place_ref, bf16[4,256,768]{2,1,0:T(8,128)(2,1)S(1)} %bitcast.98, bf16[4,256,640]{2,1,0:T(8,128)(2,1)S(1)} %bitcast.99, bf16[4,256,640]{2,1,0:T(8,128)(2,1)S(1)} %bitcast.100, ...), custom_call_target="tpu_custom_call" | custom-call | flops 6442450944 | bytes 25165824 | tf_op jit(solution)/shard_map/pallas_call | solution.py:113
  122.5 3.1 copy-done.11
  125.6 460.5 %shard_map.164 = (bf16[3,4,32,16,768]{4,3,2,1,0:T(8,128)(2,1)}, bf16[3,4,32,16,640]{4,3,2,1,0:T(8,128)(2,1)}, bf16[3,4,32,16,640]{4,3,2,1,0:T(8,128)(2,1)}, bf16...) custom-call(bf16[3,4,32,16,768]{4,3,2,1,0:T(8,128)(2,1)} %bitcast.11, ...), custom_call_target="tpu_custom_call" | custom-call | flops 57982058496 | bytes 100663296 | tf_op jit(solution)/shard_map/pallas_call | solution.py:337
  586.2 69.0 %shard_map.165 = (f32[4,256,768]{2,1,0:T(8,128)}, f32[4,256,640]{2,1,0:T(8,128)S(1)}, f32[4,256,640]{2,1,0:T(8,128)S(1)}) custom-call(s32[3]{0:T(128)S(1)} %pad_add_fusion.place_ref, bf16[6144,768]{1,0:T(8,128)(2,1)} %bitcast.118, bf16[6144,640]{1,0:T(8,128)(2,1)} %bitcast.120, bf16[6144,640]{1,0:T(8,128)(2,1)} %bitcast.121, s32[4,256,8]{2,1,0:T(8,128)S(1)} %bitcast.89, ...), custom_call_target="tpu_custom_call" | custom-call | flops 19327352832 | bytes 25165824 | tf_op jit(solution)/shard_map/pallas_call | solution.py:162
  661.6 10.2 %fusion.50 = f32[256,4096]{1,0:T(8,128)} fusion(bf16[2048,4096]{1,0:T(8,128)(2,1)} %param.21, bf16[1,256,2048]{2,1,0:T(8,128)(2,1)S(1)} %copy-done.12, f32[2048]{0:T(1024)S(1)} %convert_element_type.56, f32[256]{0:T(256)S(1)} %add_rsqrt_fusion.1), kind=kOutput, calls=%fused_computation.70 | convolution fusion | flops 4297064448 | bytes 22029312 | tf_op jit(solution)/shard_map/dot_general | solution.py:50
  672.8 2.9 copy.87
  678.7 2.1 copy.70
  680.9 1.8 copy.84
  682.7 2.6 fusion.53
  686.7 3.1 fusion.21
  689.8 5.4 fusion.54
  695.3 4.3 fusion.25
  701.3 4.7 fusion.17
  706.9 14.3 %fusion.28 = f32[256,6144]{1,0:T(8,128)} fusion(bf16[2048,6144]{1,0:T(8,128)(2,1)} %param.26, bf16[256,2048]{1,0:T(8,128)(2,1)S(1)} %get-tuple-element.42, f32[2048]{0:T(1024)S(1)} %convert_element_type.64, f32[256]{0:T(256)S(1)} %add_rsqrt_fusion), kind=kOutput, calls=%fused_computation.38 | convolution fusion | flops 6444548096 | bytes 32515072 | tf_op jit(solution)/shard_map/dot_general | solution.py:65
  721.3 6.7 reduce-scatter.6.cloned.1.call-done
  727.9 36.0 %reduce-scatter.8.cloned.1.call-done = f32[1,256,640]{2,1,0:T(8,128)} async-done(((f32[4,256,640]{2,1,0:T(8,128)}), f32[1,256,640]{2,1,0:T(8,128)}) %reduce-scatter.8.cloned.1.call-update) | async-done | bytes 655376 | tf_op jit(solution)/shard_map/reduce_scatter | solution.py:383
  764.0 40.5 %reduce-scatter.4.cloned.1.call-done = f32[1,256,768]{2,1,0:T(8,128)} async-done(((f32[4,256,768]{2,1,0:T(8,128)}), f32[1,256,768]{2,1,0:T(8,128)}) %reduce-scatter.4.cloned.1.call-update) | async-done | bytes 786448 | tf_op jit(solution)/shard_map/reduce_scatter | solution.py:383
  804.5 29.9 %fusion.14 = bf16[1,256,2048]{2,1,0:T(8,128)(2,1)} fusion(bf16[6144,2048]{1,0:T(8,128)(2,1)} %param.28, bf16[2048,6144]{1,0:T(8,128)(2,1)} %param.27, f32[256,6144]{1,0:T(8,128)} %fusion.28, bf16[256,2048]{1,0:T(8,128)(2,1)} %copy-done.13, f32[256,640]{1,0:T(8,128)} %bitcast.117, f32[256,640]{1,0:T(8,128)} %bitcast.116, f32[256,768]{1,0:T(8,128)} %bitcast.115, ...), kind=kOutput, calls=%fused_computation.26 | convolution fusion | flops 12899581952 | bytes 60826624 | tf_op jit(solution)/shard_map/dot_general | solution.py:66
  (96 shorter events, 33.5 us)
Async XLA Ops:
  6.5 652.4 %copy-start = (bf16[2048,512]{1,0:T(8,128)(2,1)S(1)}, bf16[2048,512]{1,0:T(8,128)(2,1)}, u32[]{:S(2)}) copy-start(bf16[2048,512]{1,0:T(8,128)(2,1)} %param.23) | copy-start | bytes 6291460
  6.5 6.5 copy-start.15
  6.5 87.1 %all-gather.12.cloned.1.call-start = ((), (), s32[]{:S(2)}) async-start(), calls=%async_computation.7 | async-start | bytes 1638400 | tf_op jit(solution)/shard_map/all_gather | solution.py:376
  10.5 44.7 %copy-start.16 = (s32[1,256,8]{1,2,0:T(8,128)S(1)}, s32[1,256,8]{1,2,0:T(8,128)}, u32[]{:S(2)}) copy-start(s32[1,256,8]{1,2,0:T(8,128)} %param.19) | copy-start | bytes 24580
  11.4 82.3 %all-gather.14.cloned.1.call-start = ((), (), s32[]{:S(2)}) async-start(), calls=%async_computation.8 | async-start | bytes 1638400 | tf_op jit(solution)/shard_map/all_gather | solution.py:376
  12.2 82.8 %all-gather.10.cloned.1.call-start = ((), (), s32[]{:S(2)}) async-start(), calls=%async_computation.6 | async-start | bytes 1966080 | tf_op jit(solution)/shard_map/all_gather | solution.py:376
  13.0 714.9 %reduce-scatter.6.cloned.1.call-start = ((), (), s32[]{:S(2)}) async-start(), calls=%async_computation.4 | async-start | bytes 3276800 | tf_op jit(solution)/shard_map/reduce_scatter | solution.py:383
  122.5 3.1 copy-start.11
  125.6 460.6 %copy-start.4 = (f32[4,256,8]{2,1,0:T(8,128)S(1)}, f32[4,256,8]{2,1,0:T(8,128)}, u32[]{:S(2)}) copy-start(f32[4,256,8]{2,1,0:T(8,128)} %copy.80.refs_8_) | copy-start | bytes 98308
  125.6 460.6 %copy-start.5 = (s32[4,8,256]{1,2,0:T(8,128)S(1)}, s32[4,8,256]{1,2,0:T(8,128)}, u32[]{:S(2)}) copy-start(s32[4,8,256]{1,2,0:T(8,128)} %copy.73) | copy-start | bytes 98308
  125.6 460.6 %copy-start.6 = (s32[4,8,256]{1,2,0:T(8,128)S(1)}, s32[4,8,256]{1,2,0:T(8,128)}, u32[]{:S(2)}) copy-start(s32[4,8,256]{1,2,0:T(8,128)} %copy.74) | copy-start | bytes 98308
  125.6 460.6 %copy-start.7 = (s32[4,8,256]{1,2,0:T(8,128)S(1)}, s32[4,8,256]{1,2,0:T(8,128)}, u32[]{:S(2)}) copy-start(s32[4,8,256]{1,2,0:T(8,128)} %copy.75) | copy-start | bytes 98308
  655.2 1.5 copy-start.2
  656.7 1.5 copy-start.3
  658.2 105.8 %reduce-scatter.8.cloned.1.call-start = ((), (), s32[]{:S(2)}) async-start(), calls=%async_computation.5 | async-start | bytes 3276800 | tf_op jit(solution)/shard_map/reduce_scatter | solution.py:383
  658.8 145.7 %reduce-scatter.4.cloned.1.call-start = ((), (), s32[]{:S(2)}) async-start(), calls=%async_computation.3 | async-start | bytes 3932160 | tf_op jit(solution)/shard_map/reduce_scatter | solution.py:383
  658.9 2.0 copy-start.19
  677.9 4.8 copy-start.18
  689.8 5.5 copy-start.14
  689.8 9.8 %slice-start = ((s8[16777216]{0:T(1024)(128)(4,1)}), s8[4194304]{0:T(1024)(128)(4,1)S(1)}, s32[]{:S(2)}) async-start(s8[16777216]{0:T(1024)(128)(4,1)} %bitcast.103), calls=%async_computation.9 | async-start | bytes 8388608
  689.8 9.8 %slice-start.1 = ((s8[16777216]{0:T(1024)(128)(4,1)}), s8[4194304]{0:T(1024)(128)(4,1)S(1)}, s32[]{:S(2)}) async-start(s8[16777216]{0:T(1024)(128)(4,1)} %bitcast.103), calls=%async_computation.10 | async-start | bytes 8388608
  695.2 4.8 slice-start.2
  695.3 6.0 slice-start.3
  804.5 29.9 %copy-start.1 = (bf16[2048,512]{1,0:T(8,128)(2,1)S(1)}, bf16[2048,512]{1,0:T(8,128)(2,1)}, u32[]{:S(2)}) copy-start(bf16[2048,512]{1,0:T(8,128)(2,1)} %param.23) | copy-start | bytes 6291460
  (6 other events, 6.9 us)
Sparse Core Ops, SparseCore 0:
  11.5 27.4 all-gather.11
  40.7 25.4 all-gather.13
  67.8 27.0 all-gather.9
  658.3 69.5 reduce-scatter.5
  730.2 33.7 reduce-scatter.7
  766.2 38.2 reduce-scatter.3

commit v2 on v0

v2 whole, which is shorter than its diff:
```python
import functools
import math
import types

import jax
import jax.numpy as jnp
from jax import lax
from jax.experimental import pallas as pl
from jax.experimental.pallas import tpu as pltpu
from jax.sharding import PartitionSpec as P

RMS_EPS = 1e-6
ROPE_BASE = 10000.0
CAP_FACTOR = 3
N_CHUNKS = 3
RING = 6
TILE = 256
MESH = pl.DeviceIdType.MESH

BF16, F32, I32 = jnp.bfloat16, jnp.float32, jnp.int32

AXES = ('z', 'y', 'x', 'c')
LINE = ('z', 'x', 'y')
PLANE = (('y', 'x'), ('z', 'y'), ('x', 'z'))
ROW_AXES = ('y', 'x', 'c', 'z')


def torus_side(n_devices):
    side = round((n_devices // 2) ** (1 / 3))
    assert side ** 3 * 2 == n_devices
    return side


def column_parts(model):
    lanes = model // 128
    first = -(-lanes // 3)
    second = -(-(lanes - first) // 2)
    ends = (0, first * 128, (first + second) * 128, model)
    return tuple((ends[p], ends[p + 1]) for p in range(3))


def steps(total, size):
    return [(lo, min(size, total - lo)) for lo in range(0, total, size)]


def rms_rows(rows, scale):
    as_float = rows.astype(F32)
    inv_rms = lax.rsqrt(jnp.mean(as_float * as_float, axis=-1, keepdims=True) + RMS_EPS)
    return (as_float * inv_rms * scale.astype(F32)).astype(BF16)


def dot(a, b):
    return jnp.dot(a, b, preferred_element_type=F32)


def kernel(*refs, names, side, parts, capacity, head_dim, f_chunk, d_chunk):
    r = types.SimpleNamespace(**dict(zip(names, refs)))
    each = lambda name: [getattr(r, name + str(p)) for p in range(3)]
    slots = capacity // N_CHUNKS
    members = side * side * 2
    mates = side * 2
    rows_block = members * slots
    tokens, model = r.hidden.shape
    me = {axis: lax.axis_index(axis) for axis in AXES}


    def member(p, place):
        return (place[PLANE[p][0]] * side + place[PLANE[p][1]]) * 2 + place['c']

    def rows_of(ref, p, chunk, place):
        spot = [pl.ds(0, side) if axis == LINE[p] else place[axis] for axis in ROW_AXES]
        return ref.at[tuple([chunk] + spot)]

    def gathered_rows_of(ref, p, chunk, place):
        free = (LINE[p], PLANE[p][0])
        spot = [pl.ds(0, side) if axis in free else place[axis] for axis in ROW_AXES]
        return ref.at[tuple([chunk] + spot)]

    def source_index(p, i, d):
        where = {PLANE[p][0]: i, LINE[p]: d}
        return tuple(where[axis] for axis in ROW_AXES if axis in where)

    def device(place):
        return tuple(place[axis] for axis in AXES)

    def plane_peer(p, offset):
        first, second = PLANE[p]
        place = dict(me)
        place[first] = lax.rem(me[first] + offset // (2 * side), side)
        place[second] = lax.rem(me[second] + lax.rem(offset // 2, side), side)
        place['c'] = lax.rem(me['c'] + lax.rem(offset, 2), 2)
        return place

    def axis_peer(axis, offset):
        return {**me, axis: lax.rem(me[axis] + offset, side)}

    def line_peer(p, offset):
        return axis_peer(LINE[p], offset)

    def remote(src, dst, send_sem, recv_sem, place):
        return pltpu.make_async_remote_copy(
            src_ref=src, dst_ref=dst, send_sem=send_sem, recv_sem=recv_sem, device_id=device(place), device_id_type=MESH
        )

    def wait_bytes(ref, sem):
        pltpu.make_async_copy(ref, ref, sem).wait()

    def expert_key(place, core, slot):
        return (((place['z'] * side + place['y']) * side + place['x']) * 2 + core) * capacity + slot

    def plane_keys(p, shape, chunk):
        row = lax.broadcasted_iota(I32, shape, 1)
        which, slot = row // slots, lax.rem(row, slots)
        pair = which // 2
        place = {PLANE[p][0]: pair // side, PLANE[p][1]: lax.rem(pair, side), LINE[p]: me[LINE[p]]}
        return expert_key(place, lax.rem(which, 2), slot + chunk * slots)

    def mate_keys(p, shape):
        row = lax.broadcasted_iota(I32, shape, 0)
        block, slot = row // slots, lax.rem(row, slots)
        chunk, mate = block // mates, lax.rem(block, mates)
        place = {**me, PLANE[p][1]: mate // 2}
        return expert_key(place, lax.rem(mate, 2), slot + chunk * slots)

    tok, far, sends, arrivals, outputs = each('tok'), each('far'), each('send'), each('arrive'), each('output')
    results, sums, others, bounce = each('result'), each('sum'), each('other'), each('bounce')
    widths = [hi - lo for lo, hi in parts]


    band = min(32, tokens)

    def bands(body):
        lax.fori_loop(0, tokens // band, lambda i, c: (body(pl.ds(pl.multiple_of(i * band, band), band)), c)[1], 0)

    def norm_both(here):
        normed = rms_rows(r.hidden[here, :], r.moe_norm[...])
        for p, (lo, hi) in enumerate(parts):
            tok[p][me[LINE[p]], here, :] = normed[:, lo:hi]
        r.rows[here, :] = rms_rows(r.hidden[here, :], r.attn_norm[...])

    bands(norm_both)
    for p in range(3):
        r.all_keys[p, me[PLANE[p][0]], me[LINE[p]]] = r.keys_t[...]
    pairs = ((r.gate_hbm, r.gate), (r.up_hbm, r.up), (r.down_hbm, r.down))
    loads = [pltpu.make_async_copy(src, dst, r.weight_sem.at[i]) for i, (src, dst) in enumerate(pairs)]
    for load in loads:
        load.start()
    for offset in range(1, side):
        for p in range(3):
            spot, place = me[LINE[p]], line_peer(p, offset)
            remote(tok[p].at[spot], tok[p].at[spot], r.tok_send.at[p], r.tok_recv.at[p], place).start()
            remote(
                r.keys_t, r.all_keys.at[p, me[PLANE[p][0]], spot], r.key_send.at[p], r.key_recv.at[p], place
            ).start()


    ring = r.ring
    ring_sem = r.ring_sem

    def stream(n_steps, group, source, body):
        ahead = RING // group * group - group

        def copy(i, s):
            slot = lax.rem(i * group + s, RING // group * group)
            return pltpu.make_async_copy(source(i, s), ring.at[slot], ring_sem.at[slot])

        for i in range(min(ahead // group, n_steps)):
            for s in range(group):
                copy(i, s).start()

        def step(i, carry):
            @pl.when(i + ahead // group < n_steps)
            def _():
                for s in range(group):
                    copy(i + ahead // group, s).start()

            for s in range(group):
                copy(i, s).wait()
            body(i, [ring.at[lax.rem(i * group + s, RING // group * group)] for s in range(group)])
            return carry

        lax.fori_loop(0, n_steps, step, 0)

    def col_tile(i):
        return pl.ds(pl.multiple_of(i * TILE, TILE), TILE)

    def turned(y):
        return y * r.cos[...] + pltpu.roll(y, head_dim // 2, 1) * r.sin[...]

    def project(weight, out, rotary):
        def body(i, tiles):
            y = dot(r.rows[...], tiles[0][...])
            if rotary:
                y = jnp.concatenate([turned(y[:, lo : lo + head_dim]) for lo in range(0, TILE, head_dim)], axis=1)
            out[:, col_tile(i)] = y.astype(BF16)

        stream(weight.shape[1] // TILE, 1, lambda i, s: weight.at[:, col_tile(i)], body)

    project(r.w_query, r.query, True)
    project(r.w_key, r.key, True)
    project(r.w_value, r.value, False)


    logits = sum(dot(tok[p][me[LINE[p]]], r.w_router[lo:hi, :]) for p, (lo, hi) in enumerate(parts))
    lane = lax.broadcasted_iota(I32, logits.shape, 1)
    top_k = r.ids.shape[1]
    ids = r.ids[...]
    picked = [jnp.sum(jnp.where(lane == ids[:, j : j + 1], logits, 0.0), axis=1, keepdims=True) for j in range(top_k)]
    peak = functools.reduce(jnp.maximum, picked)
    powers = [jnp.exp(v - peak) for v in picked]
    norm = functools.reduce(jnp.add, powers)
    mine = r.keys_f[...]
    lane = lax.broadcasted_iota(I32, mine.shape, 1)
    for j in range(top_k):
        mine = jnp.where(lane == top_k + j, powers[j] / norm, mine)
    r.my_gates[...] = mine
    for p in range(3):
        r.line_gates[p, me[LINE[p]]] = mine


    for p in range(3):
        wait_bytes(r.all_keys.at[p, 0, pl.ds(0, side - 1)], r.key_recv.at[p])
        wait_bytes(tok[p].at[pl.ds(0, side - 1)], r.tok_recv.at[p])
    for offset in range(1, side):
        for p in range(3):
            spot, place = me[PLANE[p][0]], axis_peer(PLANE[p][0], offset)
            remote(
                r.all_keys.at[p, spot], r.all_keys.at[p, spot], r.far_key_send.at[p], r.far_key_recv.at[p], place
            ).start()
            remote(tok[p], far[p].at[spot], r.far_send.at[p], r.far_recv.at[p], place).start()
    for offset in range(1, side):
        for p in range(3):
            spot = me[LINE[p]]
            remote(
                r.my_gates, r.line_gates.at[p, spot], r.gate_send.at[p], r.gate_recv.at[p], line_peer(p, offset)
            ).start()


    n_heads = r.query.shape[1] // head_dim
    per_key = r.query.shape[1] // r.key.shape[1]
    causal = lax.broadcasted_iota(I32, (tokens, tokens), 0) >= lax.broadcasted_iota(I32, (tokens, tokens), 1)

    def one_head(h, carry):
        cols = pl.ds(pl.multiple_of(h * head_dim, head_dim), head_dim)
        key_cols = pl.ds(pl.multiple_of(h // per_key * head_dim, head_dim), head_dim)
        scores = lax.dot_general(
            r.query[:, cols], r.key[:, key_cols], (((1,), (1,)), ((), ())), preferred_element_type=F32
        )
        scores = jnp.where(causal, scores * head_dim ** -0.5, -jnp.inf)
        power = jnp.exp(scores - jnp.max(scores, axis=1, keepdims=True))
        prob = (power / jnp.sum(power, axis=1, keepdims=True)).astype(BF16)
        r.query[:, cols] = dot(prob, r.value[:, key_cols]).astype(BF16)
        return carry

    lax.fori_loop(0, n_heads, one_head, 0)


    stage = r.stage
    blocks = N_CHUNKS * mates
    my_mate = {p: me[PLANE[p][1]] * 2 + me['c'] for p in range(3)}

    def pick_rows(p, i, d, slot, source):
        wanted = mate_keys(p, (blocks * slots, tokens))
        keys = r.all_keys[p, i, d]
        hit = wanted == keys[0:1, :]
        for j in range(1, top_k):
            hit = jnp.logical_or(hit, wanted == keys[j : j + 1, :])
        pick = jnp.where(hit, 1.0, 0.0).astype(BF16)
        for lo, n in steps(widths[p], TILE):
            found = dot(pick, source[:, lo : lo + n]).astype(BF16)
            stage[slot, 0:blocks, :, lo : lo + n] = found.reshape(blocks, slots, n)

    def flush(p, i, d, slot):
        a, b = source_index(p, i, d)
        return pltpu.make_async_copy(
            stage.at[slot, pl.ds(0, blocks), :, pl.ds(0, widths[p])],
            sends[p].at[pl.ds(0, blocks), a, b],
            r.stage_sem.at[slot],
        )

    def keep(p, i, d, slot, chunk):
        spot = {**me, PLANE[p][0]: i, LINE[p]: d}
        return pltpu.make_async_copy(
            stage.at[slot, chunk * mates + my_mate[p], :, pl.ds(0, widths[p])],
            arrivals[p].at[tuple([chunk] + [spot[axis] for axis in ROW_AXES])],
            r.keep_sem.at[slot, chunk],
        )

    for p in range(3):
        sources = side * side
        near = me[PLANE[p][0]]
        wait_bytes(r.all_keys.at[p, pl.ds(0, side - 1)], r.far_key_recv.at[p])
        wait_bytes(far[p].at[pl.ds(0, side - 1)], r.far_recv.at[p])

        def place_of(n):
            return lax.rem(near + n // side, side), lax.rem(n, side)

        def load(n, slot):
            i, d = place_of(n)
            return pltpu.make_async_copy(far[p].at[i, d], r.source.at[slot, :, pl.ds(0, widths[p])], r.source_sem.at[slot])

        def one_source(n, c):
            slot = lax.rem(n, 2)
            i, d = place_of(n)

            @pl.when(jnp.logical_and(n + 1 >= side, n + 1 < sources))
            def _():
                load(n + 1, 1 - slot).start()

            @pl.when(n >= side)
            def _():
                load(n, slot).wait()

            @pl.when(n < side)
            def _():
                r.source[slot, :, 0 : widths[p]] = tok[p][d]

            @pl.when(n >= 2)
            def _():
                i2, d2 = place_of(n - 2)
                flush(p, i2, d2, slot).wait()
                for chunk in range(N_CHUNKS):
                    keep(p, i2, d2, slot, chunk).wait()

            pick_rows(p, i, d, slot, r.source.at[slot])
            flush(p, i, d, slot).start()
            for chunk in range(N_CHUNKS):
                keep(p, i, d, slot, chunk).start()
            return c

        lax.fori_loop(0, sources, one_source, 0)
        for n in range(sources - 2, sources):
            i, d = place_of(n)
            flush(p, i, d, n % 2).wait()
            for chunk in range(N_CHUNKS):
                keep(p, i, d, n % 2, chunk).wait()

        def go_chunk(chunk, c):
            def one_mate(offset, c2):
                axis = PLANE[p][1]
                place = {
                    **me,
                    axis: lax.rem(me[axis] + offset // 2, side),
                    'c': lax.rem(me['c'] + lax.rem(offset, 2), 2),
                }
                remote(
                    sends[p].at[chunk * mates + place[axis] * 2 + place['c']],
                    gathered_rows_of(arrivals[p], p, chunk, me),
                    r.go_send.at[chunk, p],
                    r.go_recv.at[chunk, p],
                    place,
                ).start()
                return c2

            return lax.fori_loop(1, mates, one_mate, c)

        lax.fori_loop(0, N_CHUNKS, go_chunk, 0)


    out_split = n_heads * head_dim // model

    def out_body(i, tiles):
        total = r.hidden[:, col_tile(i)].astype(F32)
        attended = dot(r.query[:, 0:model], tiles[0][...])
        for s in range(1, out_split):
            attended += dot(r.query[:, s * model : (s + 1) * model], tiles[s][...])
        r.attended[:, col_tile(i)] = (total + attended).astype(BF16)

    stream(model // TILE, out_split, lambda i, s: r.w_out.at[pl.ds(s * model, model), col_tile(i)], out_body)

    def norm_attended(here):
        r.rows[here, :] = rms_rows(r.attended[here, :], r.ffn_norm[...])

    bands(norm_attended)

    def act_body(i, tiles):
        z = dot(r.rows[...], tiles[0][...])
        u = dot(r.rows[...], tiles[1][...])
        r.act[:, col_tile(i)] = (jax.nn.silu(z) * u).astype(BF16)

    ff_dim = r.ffn_gate.shape[1]
    stream(
        ff_dim // TILE, 2, lambda i, s: (r.ffn_gate, r.ffn_up)[s].at[:, col_tile(i)], act_body
    )
    down_split = ff_dim // model

    def down_body(i, tiles):
        total = dot(r.act[:, 0:model], tiles[0][...])
        for s in range(1, down_split):
            total += dot(r.act[:, s * model : (s + 1) * model], tiles[s][...])
        r.dense[:, col_tile(i)] = r.attended[:, col_tile(i)].astype(F32) + total

    stream(model // TILE, down_split, lambda i, s: r.ffn_down.at[pl.ds(s * model, model), col_tile(i)], down_body)


    for load in loads:
        load.wait()
    x_buf, y_buf, hidden_buf = r.x_buf, r.y_buf, r.hidden_buf
    group = x_buf.shape[1:-1]
    rows = math.prod(group)
    width = hidden_buf.shape[1]

    def fetch(chunk, y, slot):
        return [
            pltpu.make_async_copy(
                arrivals[p].at[chunk, y], x_buf.at[slot, :, :, :, :, pl.ds(lo, hi - lo)], r.in_sem.at[slot, p]
            )
            for p, (lo, hi) in enumerate(parts)
        ]

    def put(chunk, y, slot):
        return [
            pltpu.make_async_copy(
                y_buf.at[slot, :, :, :, :, pl.ds(lo, hi - lo)], outputs[p].at[chunk, y], r.out_sem.at[slot, p]
            )
            for p, (lo, hi) in enumerate(parts)
        ]

    def expert_chunk(chunk, carry):
        for p in range(3):
            wait_bytes(sends[p].at[pl.ds(0, mates - 1)], r.go_recv.at[chunk, p])
        for copy in fetch(chunk, 0, 0):
            copy.start()

        def one_tile(y, c):
            slot = lax.rem(y, 2)

            @pl.when(y + 1 < side)
            def _():
                for copy in fetch(chunk, y + 1, 1 - slot):
                    copy.start()

            for copy in fetch(chunk, y, slot):
                copy.wait()

            @pl.when(y >= 2)
            def _():
                for copy in put(chunk, y - 2, slot):
                    copy.wait()

            for lo in range(0, width, f_chunk):
                cols = slice(lo, lo + f_chunk)
                z = dot(x_buf[slot].reshape(rows, model), r.gate[:, cols])
                u = dot(x_buf[slot].reshape(rows, model), r.up[:, cols])
                hidden_buf[:, cols] = (jax.nn.silu(z) * u).astype(BF16)
            for lo in range(0, model, d_chunk):
                cols = slice(lo, lo + d_chunk)
                y_rows = dot(hidden_buf[...], r.down[:, cols]).astype(BF16)
                y_buf[slot, :, :, :, :, cols] = y_rows.reshape(group + (d_chunk,))
            for copy in put(chunk, y, slot):
                copy.start()
            return c

        lax.fori_loop(0, side, one_tile, 0)
        for y in range(max(side - 2, 0), side):
            for copy in put(chunk, y, y % 2):
                copy.wait()

        def one_peer(offset, c):
            for p in range(3):
                place = plane_peer(p, offset)
                remote(
                    rows_of(outputs[p], p, chunk, place),
                    results[p].at[chunk, pl.ds(0, side), member(p, me)],
                    r.back_send.at[chunk, p],
                    r.back_recv.at[chunk, p],
                    place,
                ).start()
            return c

        lax.fori_loop(1, members, one_peer, 0)
        own = [
            pltpu.make_async_copy(rows_of(outputs[p], p, chunk, me), bounce[p].at[chunk], r.own_sem.at[p])
            for p in range(3)
        ]
        for copy in own:
            copy.start()
        for p, copy in enumerate(own):
            copy.wait()
            pltpu.make_async_copy(
                bounce[p].at[chunk], results[p].at[chunk, pl.ds(0, side), member(p, me)], r.back_recv.at[chunk, p]
            ).start()
        return carry

    lax.fori_loop(0, N_CHUNKS, expert_chunk, 0)


    for p in range(3):
        wait_bytes(r.line_gates.at[p, pl.ds(0, side - 1)], r.gate_recv.at[p])
    split = r.split
    lanes = min(128, rows_block)

    def weigh_chunk(chunk, carry):
        for p in range(3):
            wait_bytes(results[p].at[chunk], r.back_recv.at[chunk, p])

        for p in range(3):

            def load(d, slot):
                return pltpu.make_async_copy(
                    results[p].at[chunk, d],
                    stage.at[slot, pl.ds(0, members), :, pl.ds(0, widths[p])],
                    r.stage_sem.at[slot],
                )

            load(0, 0).start()

            def one_source(d, c):
                slot = lax.rem(d, 2)

                @pl.when(d + 1 < side)
                def _():
                    load(d + 1, 1 - slot).start()

                info = r.line_gates[p, d]
                keys = [jnp.broadcast_to(info[:, j : j + 1], (tokens, lanes)) for j in range(top_k)]
                gates = [jnp.broadcast_to(info[:, top_k + j : top_k + j + 1], (tokens, lanes)) for j in range(top_k)]
                held = plane_keys(p, (tokens, rows_block), chunk)
                for lo in range(0, rows_block, lanes):
                    here = held[:, lo : lo + lanes].astype(F32)
                    weight = jnp.zeros((tokens, lanes), F32)
                    for j in range(top_k):
                        weight = jnp.where(here == keys[j], gates[j], weight)
                    high = weight.astype(BF16)
                    rest = weight - high.astype(F32)
                    middle = rest.astype(BF16)
                    low = (rest - middle.astype(F32)).astype(BF16)
                    split[0:tokens, lo : lo + lanes] = high
                    split[tokens : 2 * tokens, lo : lo + lanes] = middle
                    split[2 * tokens : 3 * tokens, lo : lo + lanes] = low
                load(d, slot).wait()
                for lo, n in steps(widths[p], TILE):
                    y = stage[slot, 0:members, :, lo : lo + n].reshape(rows_block, n)
                    both = dot(split[...], y)
                    total = both[0:tokens] + (both[tokens : 2 * tokens] + both[2 * tokens : 3 * tokens])

                    @pl.when(chunk == 0)
                    def _():
                        sums[p][d, :, lo : lo + n] = total

                    @pl.when(chunk > 0)
                    def _():
                        sums[p][d, :, lo : lo + n] += total

                return c

            lax.fori_loop(0, side, one_source, 0)

            @pl.when(chunk == N_CHUNKS - 1)
            def _():
                for offset in range(1, side):
                    place = line_peer(p, offset)
                    remote(
                        sums[p].at[place[LINE[p]]],
                        others[p].at[offset - 1],
                        r.sum_send.at[p],
                        r.sum_recv.at[p],
                        place,
                    ).start()

        return carry

    lax.fori_loop(0, N_CHUNKS, weigh_chunk, 0)
    for p, (lo, hi) in enumerate(parts):
        wait_bytes(others[p], r.sum_recv.at[p])

        def finish(here):
            moe = sums[p][me[LINE[p]], here, :]
            for offset in range(1, side):
                moe += others[p][offset - 1, here, :]
            r.out[here, lo:hi] = (r.dense[here, lo:hi] + moe).astype(BF16)

        bands(finish)


    for p in range(3):
        wait_bytes(tok[p].at[pl.ds(0, side - 1)], r.tok_send.at[p])
        wait_bytes(r.all_keys.at[p, 0, pl.ds(0, side - 1)], r.key_send.at[p])
        wait_bytes(far[p].at[pl.ds(0, side - 1)], r.far_send.at[p])
        wait_bytes(r.all_keys.at[p, pl.ds(0, side - 1)], r.far_key_send.at[p])
        wait_bytes(r.line_gates.at[p, pl.ds(0, side - 1)], r.gate_send.at[p])
        wait_bytes(others[p], r.sum_send.at[p])
        for chunk in range(N_CHUNKS):
            wait_bytes(sends[p].at[pl.ds(0, mates - 1)], r.go_send.at[chunk, p])
            wait_bytes(results[p].at[chunk, pl.ds(0, side), pl.ds(0, members - 1)], r.back_send.at[chunk, p])


def layer_pair(small, large, side, capacity, head_dim):
    tokens, model = small['hidden'].shape
    top_k, width = small['ids'].shape[1], large['gate_hbm'].shape[1]
    key_dim, ff_dim = large['w_key'].shape[1], large['ffn_gate'].shape[1]
    parts = column_parts(model)
    widths = [hi - lo for lo, hi in parts]
    slots, members, mates = capacity // N_CHUNKS, side * side * 2, side * 2
    group = (side, 2, side, slots)
    rows = math.prod(group)
    sds, vmem = jax.ShapeDtypeStruct, pltpu.VMEM
    dma = lambda *shape: pltpu.SemaphoreType.DMA(shape)
    outs = dict(out=sds((tokens, model), BF16))
    scratch = dict(
        rows=vmem((tokens, model), BF16),
        query=vmem((tokens, large['w_query'].shape[1]), BF16),
        key=vmem((tokens, key_dim), BF16),
        value=vmem((tokens, key_dim), BF16),
        attended=vmem((tokens, model), BF16),
        act=vmem((tokens, ff_dim), BF16),
        dense=vmem((tokens, model), F32),
        ring=vmem((RING, model, TILE), BF16),
        all_keys=vmem((3, side, side, top_k, tokens), I32),
        my_gates=vmem((tokens, 128), F32),
        line_gates=vmem((3, side, tokens, 128), F32),
        source=vmem((2, tokens, max(widths)), BF16),
        stage=vmem((2, max(members, N_CHUNKS * mates), slots, max(widths)), BF16),
        split=vmem((3 * tokens, members * slots), BF16),
        gate=vmem((model, width), BF16),
        up=vmem((model, width), BF16),
        down=vmem((width, model), BF16),
        x_buf=vmem((2,) + group + (model,), BF16),
        y_buf=vmem((2,) + group + (model,), BF16),
        hidden_buf=vmem((rows, width), BF16),
        weight_sem=dma(3),
        ring_sem=dma(RING),
        source_sem=dma(2),
        stage_sem=dma(2),
        keep_sem=dma(2, N_CHUNKS),
        in_sem=dma(2, 3),
        out_sem=dma(2, 3),
        own_sem=dma(3),
        tok_send=dma(3),
        tok_recv=dma(3),
        key_send=dma(3),
        key_recv=dma(3),
        far_send=dma(3),
        far_recv=dma(3),
        far_key_send=dma(3),
        far_key_recv=dma(3),
        gate_send=dma(3),
        gate_recv=dma(3),
        sum_send=dma(3),
        sum_recv=dma(3),
        go_send=dma(N_CHUNKS, 3),
        go_recv=dma(N_CHUNKS, 3),
        back_send=dma(N_CHUNKS, 3),
        back_recv=dma(N_CHUNKS, 3),
    )
    for p, w in enumerate(widths):
        there = sds((N_CHUNKS, side, side, 2, side, slots, w), BF16)
        outs['far' + str(p)] = sds((side, side, tokens, w), BF16)
        outs['send' + str(p)] = sds((N_CHUNKS * mates, side, side, slots, w), BF16)
        outs['arrive' + str(p)] = there
        outs['output' + str(p)] = there
        outs['result' + str(p)] = sds((N_CHUNKS, side, members, slots, w), BF16)
        scratch['tok' + str(p)] = vmem((side, tokens, w), BF16)
        scratch['bounce' + str(p)] = vmem((N_CHUNKS, side, slots, w), BF16)
        scratch['sum' + str(p)] = vmem((side, tokens, w), F32)
        scratch['other' + str(p)] = vmem((side - 1, tokens, w), F32)
    anywhere = pl.BlockSpec(memory_space=pl.ANY)
    local = pl.BlockSpec(memory_space=pltpu.VMEM)
    n_rows = members * side * capacity
    return pl.pallas_call(
        functools.partial(
            kernel,
            names=tuple(small) + tuple(large) + tuple(outs) + tuple(scratch),
            side=side,
            parts=parts,
            capacity=capacity,
            head_dim=head_dim,
            f_chunk=min(256, width),
            d_chunk=min(512, model),
        ),
        out_shape=list(outs.values()),
        in_specs=[local] * len(small) + [anywhere] * len(large),
        out_specs=[local] + [anywhere] * (len(outs) - 1),
        scratch_shapes=list(scratch.values()),
        compiler_params=pltpu.CompilerParams(has_side_effects=True, vmem_limit_bytes=67043328),
        cost_estimate=pl.CostEstimate(flops=6 * n_rows * model * width, bytes_accessed=8 * n_rows * model, transcendentals=0),
    )(*small.values(), *large.values())[0]


def solution(mesh):
    group_size = mesh.shape['ep']
    side = torus_side(group_size)
    torus = jax.sharding.Mesh(mesh.devices.reshape(side, side, side, 2), AXES)
    row_spec = P(AXES, None, None)
    vec_spec = P(None)
    mat_spec = P(None, None)
    cube_spec = P(None, None, None)
    expert_spec = P(AXES, None, None)

    def per_device(hidden, expert_ids, slot_ids, attn_norm, w_query, w_key, w_value, w_out, ffn_norm, ffn_gate, ffn_up, ffn_down, moe_norm, w_router, exp_gate, exp_up, exp_down):
        n_seqs, tokens, model = hidden.shape
        assert n_seqs == 1 and exp_gate.shape[0] == 1
        n_heads, head_dim = w_out.shape[0], w_out.shape[1]
        ids = expert_ids[0]
        capacity = CAP_FACTOR * tokens * ids.shape[1] // group_size
        keys = ids * capacity + slot_ids[0]
        inv_freq = ROPE_BASE ** (-2.0 * jnp.arange(head_dim // 2, dtype=F32) / head_dim)
        angles = jnp.arange(tokens, dtype=F32)[:, None] * inv_freq[None, :]
        cos, sin = jnp.cos(angles), jnp.sin(angles)
        small = dict(
            hidden=hidden[0],
            attn_norm=attn_norm.reshape(1, model),
            moe_norm=moe_norm.reshape(1, model),
            ffn_norm=ffn_norm.reshape(1, model),
            keys_t=keys.T,
            keys_f=jnp.pad(keys.astype(F32), ((0, 0), (0, 128 - keys.shape[1]))),
            ids=ids,
            w_router=w_router,
            cos=jnp.concatenate([cos, cos], axis=1),
            sin=jnp.concatenate([-sin, sin], axis=1),
        )
        large = dict(
            w_query=w_query,
            w_key=w_key,
            w_value=w_value,
            w_out=w_out.reshape(n_heads * head_dim, model),
            ffn_gate=ffn_gate,
            ffn_up=ffn_up,
            ffn_down=ffn_down,
            gate_hbm=exp_gate[0],
            up_hbm=exp_up[0],
            down_hbm=exp_down[0],
        )
        return layer_pair(small, large, side, capacity, head_dim).reshape(hidden.shape)

    return jax.shard_map(per_device, mesh=torus, in_specs=(row_spec, row_spec, row_spec, vec_spec, mat_spec, mat_spec, mat_spec, cube_spec, vec_spec, mat_spec, mat_spec, mat_spec, vec_spec, mat_spec, expert_spec, expert_spec, expert_spec), out_specs=row_spec, check_vma=False)
```

time: 1070 us -> 527 us (0.49)
  the two profiles are of different devices: /device:TPU:84 before, /device:TPU:100 now
where the time goes in v2:
time: 527 us; the launch traced here: 526 us
  Pallas kernels  515 us (98%)
  local copies, waits for them, and re-layouts  9.16 us (2%)
    pallas_call x1, Pallas kernels, layer_pair(): pl.pallas_call(functools.partial(kernel, names=tuple(small) + tuple(large...  515 us

profile of v2, /device:TPU:100, one launch (start us, length us, event | category | flops | bytes accessed | tf_op | source)
XLA Modules:
  0.0 525.8 jit_solution(14638865474123929164)
XLA Ops:
  0.0 1.3 reshape.20.refs_1_
  1.3 1.3 reshape.22.refs_3_
  2.6 1.3 reshape.21.refs_2_
  3.9 0.8 copy.18
  4.7 0.0 copy-start
  4.7 0.8 copy.19
  5.6 0.7 pad.4.refs_5_
  6.3 0.7 copy.20.refs_4_
  6.9 0.5 fusion.4
  7.4 0.8 pad_maximum_fusion
  8.3 0.0 copy-done
  8.3 515.2 %shard_map.163 = (bf16[256,2048]{1,0:T(8,128)(2,1)}, bf16[4,4,256,768]{3,2,1,0:T(8,128)(2,1)}, bf16[24,4,4,16,768]{4,3,2,1,0:T(8,128)(2,1)}, bf16[3,4,4,2,4,16,7...) custom-call(bf16[256,2048]{1,0:T(8,128)(2,1)} %bitcast.23, ...), custom_call_target="tpu_custom_call" | custom-call | flops 57982058496 | bytes 100663296 | tf_op jit(solution)/shard_map/pallas_call | solution.py:660
  523.5 2.3 copy.22
  (2 shorter events, 0.0 us)
Async XLA Ops:
  4.7 3.6 copy-start

commit v3 on v2

--- a/solution.py
+++ b/solution.py
@@ -4,6 +4,7 @@
 
 import jax
 import jax.numpy as jnp
+import numpy as np
 from jax import lax
 from jax.experimental import pallas as pl
 from jax.experimental.pallas import tpu as pltpu
@@ -64,13 +65,6 @@
     me = {axis: lax.axis_index(axis) for axis in AXES}
 
 
-    def member(p, place):
-        return (place[PLANE[p][0]] * side + place[PLANE[p][1]]) * 2 + place['c']
-
-    def rows_of(ref, p, chunk, place):
-        spot = [pl.ds(0, side) if axis == LINE[p] else place[axis] for axis in ROW_AXES]
-        return ref.at[tuple([chunk] + spot)]
-
     def gathered_rows_of(ref, p, chunk, place):
         free = (LINE[p], PLANE[p][0])
         spot = [pl.ds(0, side) if axis in free else place[axis] for axis in ROW_AXES]
@@ -83,19 +77,19 @@
     def device(place):
         return tuple(place[axis] for axis in AXES)
 
-    def plane_peer(p, offset):
-        first, second = PLANE[p]
-        place = dict(me)
-        place[first] = lax.rem(me[first] + offset // (2 * side), side)
-        place[second] = lax.rem(me[second] + lax.rem(offset // 2, side), side)
-        place['c'] = lax.rem(me['c'] + lax.rem(offset, 2), 2)
-        return place
-
     def axis_peer(axis, offset):
         return {**me, axis: lax.rem(me[axis] + offset, side)}
 
     def line_peer(p, offset):
         return axis_peer(LINE[p], offset)
+
+    def mate_peer(p, offset):
+        axis = PLANE[p][1]
+        return {
+            **me,
+            axis: lax.rem(me[axis] + offset // 2, side),
+            'c': lax.rem(me['c'] + lax.rem(offset, 2), 2),
+        }
 
     def remote(src, dst, send_sem, recv_sem, place):
         return pltpu.make_async_remote_copy(
@@ -123,7 +117,7 @@
         return expert_key(place, lax.rem(mate, 2), slot + chunk * slots)
 
     tok, far, sends, arrivals, outputs = each('tok'), each('far'), each('send'), each('arrive'), each('output')
-    results, sums, others, bounce = each('result'), each('sum'), each('other'), each('bounce')
+    middles, results, sums, others = each('middle'), each('result'), each('sum'), each('other')
     widths = [hi - lo for lo, hi in parts]
 
 
@@ -132,26 +126,42 @@
     def bands(body):
         lax.fori_loop(0, tokens // band, lambda i, c: (body(pl.ds(pl.multiple_of(i * band, band), band)), c)[1], 0)
 
+    def one_row(scale):
+        lines = scale[...].astype(F32)
+        return jnp.concatenate([lines[i : i + 1, :] for i in range(lines.shape[0])], axis=1)
+
     def norm_both(here):
-        normed = rms_rows(r.hidden[here, :], r.moe_norm[...])
+        normed = rms_rows(r.hidden[here, :], one_row(r.moe_scale))
         for p, (lo, hi) in enumerate(parts):
             tok[p][me[LINE[p]], here, :] = normed[:, lo:hi]
-        r.rows[here, :] = rms_rows(r.hidden[here, :], r.attn_norm[...])
+        r.rows[here, :] = rms_rows(r.hidden[here, :], one_row(r.attn_scale))
 
     bands(norm_both)
+    keys_t = r.ids_t[...] * capacity + r.slots_t[...]
     for p in range(3):
-        r.all_keys[p, me[PLANE[p][0]], me[LINE[p]]] = r.keys_t[...]
+        r.all_keys[p, me[PLANE[p][0]], me[LINE[p]]] = keys_t
     pairs = ((r.gate_hbm, r.gate), (r.up_hbm, r.up), (r.down_hbm, r.down))
     loads = [pltpu.make_async_copy(src, dst, r.weight_sem.at[i]) for i, (src, dst) in enumerate(pairs)]
     for load in loads:
         load.start()
+
+    def send_far(p, d):
+        for offset in range(1, side):
+            here = me[PLANE[p][0]]
+            remote(
+                tok[p].at[d], far[p].at[here, d], r.far_send.at[p], r.far_recv.at[p], axis_peer(PLANE[p][0], offset)
+            ).start()
+
     for offset in range(1, side):
         for p in range(3):
             spot, place = me[LINE[p]], line_peer(p, offset)
-            remote(tok[p].at[spot], tok[p].at[spot], r.tok_send.at[p], r.tok_recv.at[p], place).start()
             remote(
-                r.keys_t, r.all_keys.at[p, me[PLANE[p][0]], spot], r.key_send.at[p], r.key_recv.at[p], place
+                tok[p].at[spot], tok[p].at[spot], r.tok_send.at[p, offset - 1], r.tok_recv.at[p, offset - 1], place
             ).start()
+            keys = r.all_keys.at[p, me[PLANE[p][0]], spot]
+            remote(keys, keys, r.key_send.at[p], r.key_recv.at[p], place).start()
+    for p in range(3):
+        send_far(p, me[LINE[p]])
 
 
     ring = r.ring
@@ -202,32 +212,36 @@
 
 
     logits = sum(dot(tok[p][me[LINE[p]]], r.w_router[lo:hi, :]) for p, (lo, hi) in enumerate(parts))
-    lane = lax.broadcasted_iota(I32, logits.shape, 1)
-    top_k = r.ids.shape[1]
-    ids = r.ids[...]
-    picked = [jnp.sum(jnp.where(lane == ids[:, j : j + 1], logits, 0.0), axis=1, keepdims=True) for j in range(top_k)]
+    top_k = r.ids_t.shape[0]
+    gap = jnp.zeros((128 - 3 * top_k, tokens), F32)
+    blank = jnp.zeros((top_k, tokens), F32)
+    info = jnp.concatenate([keys_t.astype(F32), blank, r.ids_t[...].astype(F32), gap], axis=0).T
+    lane = lax.broadcasted_iota(I32, logits.shape, 1).astype(F32)
+    picked = [
+        jnp.sum(jnp.where(lane == info[:, 2 * top_k + j : 2 * top_k + j + 1], logits, 0.0), axis=1, keepdims=True)
+        for j in range(top_k)
+    ]
     peak = functools.reduce(jnp.maximum, picked)
     powers = [jnp.exp(v - peak) for v in picked]
     norm = functools.reduce(jnp.add, powers)
-    mine = r.keys_f[...]
-    lane = lax.broadcasted_iota(I32, mine.shape, 1)
+    lane = lax.broadcasted_iota(I32, info.shape, 1)
     for j in range(top_k):
-        mine = jnp.where(lane == top_k + j, powers[j] / norm, mine)
-    r.my_gates[...] = mine
+        info = jnp.where(lane == top_k + j, powers[j] / norm, info)
+    r.my_gates[...] = info
     for p in range(3):
-        r.line_gates[p, me[LINE[p]]] = mine
-
-
+        r.line_gates[p, me[LINE[p]]] = info
+
+
+    for offset in range(1, side):
+        for p in range(3):
+            d = lax.rem(me[LINE[p]] + side - offset, side)
+            wait_bytes(tok[p].at[d], r.tok_recv.at[p, offset - 1])
+            send_far(p, d)
     for p in range(3):
         wait_bytes(r.all_keys.at[p, 0, pl.ds(0, side - 1)], r.key_recv.at[p])
-        wait_bytes(tok[p].at[pl.ds(0, side - 1)], r.tok_recv.at[p])
-    for offset in range(1, side):
-        for p in range(3):
-            spot, place = me[PLANE[p][0]], axis_peer(PLANE[p][0], offset)
-            remote(
-                r.all_keys.at[p, spot], r.all_keys.at[p, spot], r.far_key_send.at[p], r.far_key_recv.at[p], place
-            ).start()
-            remote(tok[p], far[p].at[spot], r.far_send.at[p], r.far_recv.at[p], place).start()
+        for offset in range(1, side):
+            keys = r.all_keys.at[p, me[PLANE[p][0]]]
+            remote(keys, keys, r.far_key_send.at[p], r.far_key_recv.at[p], axis_peer(PLANE[p][0], offset)).start()
     for offset in range(1, side):
         for p in range(3):
             spot = me[LINE[p]]
@@ -259,15 +273,15 @@
     blocks = N_CHUNKS * mates
     my_mate = {p: me[PLANE[p][1]] * 2 + me['c'] for p in range(3)}
 
-    def pick_rows(p, i, d, slot, source):
-        wanted = mate_keys(p, (blocks * slots, tokens))
+    def pick_rows(p, i, d, slot, source, wanted):
         keys = r.all_keys[p, i, d]
-        hit = wanted == keys[0:1, :]
-        for j in range(1, top_k):
-            hit = jnp.logical_or(hit, wanted == keys[j : j + 1, :])
-        pick = jnp.where(hit, 1.0, 0.0).astype(BF16)
+        for lo, n in steps(tokens, 128):
+            hit = wanted[:, 0:n] == keys[0:1, lo : lo + n]
+            for j in range(1, top_k):
+                hit = jnp.logical_or(hit, wanted[:, 0:n] == keys[j : j + 1, lo : lo + n])
+            r.split[0 : blocks * slots, lo : lo + n] = jnp.where(hit, 1.0, 0.0).astype(BF16)
         for lo, n in steps(widths[p], TILE):
-            found = dot(pick, source[:, lo : lo + n]).astype(BF16)
+            found = dot(r.split[0 : blocks * slots, 0:tokens], source[:, lo : lo + n]).astype(BF16)
             stage[slot, 0:blocks, :, lo : lo + n] = found.reshape(blocks, slots, n)
 
     def flush(p, i, d, slot):
@@ -289,6 +303,7 @@
     for p in range(3):
         sources = side * side
         near = me[PLANE[p][0]]
+        wanted = mate_keys(p, (blocks * slots, min(128, tokens)))
         wait_bytes(r.all_keys.at[p, pl.ds(0, side - 1)], r.far_key_recv.at[p])
         wait_bytes(far[p].at[pl.ds(0, side - 1)], r.far_recv.at[p])
 
@@ -322,7 +337,7 @@
                 for chunk in range(N_CHUNKS):
                     keep(p, i2, d2, slot, chunk).wait()
 
-            pick_rows(p, i, d, slot, r.source.at[slot])
+            pick_rows(p, i, d, slot, r.source.at[slot], wanted)
             flush(p, i, d, slot).start()
             for chunk in range(N_CHUNKS):
                 keep(p, i, d, slot, chunk).start()
@@ -337,14 +352,9 @@
 
         def go_chunk(chunk, c):
             def one_mate(offset, c2):
-                axis = PLANE[p][1]
-                place = {
-                    **me,
-                    axis: lax.rem(me[axis] + offset // 2, side),
-                    'c': lax.rem(me['c'] + lax.rem(offset, 2), 2),
-                }
+                place = mate_peer(p, offset)
                 remote(
-                    sends[p].at[chunk * mates + place[axis] * 2 + place['c']],
+                    sends[p].at[chunk * mates + place[PLANE[p][1]] * 2 + place['c']],
                     gathered_rows_of(arrivals[p], p, chunk, me),
                     r.go_send.at[chunk, p],
                     r.go_recv.at[chunk, p],
@@ -369,7 +379,7 @@
     stream(model // TILE, out_split, lambda i, s: r.w_out.at[pl.ds(s * model, model), col_tile(i)], out_body)
 
     def norm_attended(here):
-        r.rows[here, :] = rms_rows(r.attended[here, :], r.ffn_norm[...])
+        r.rows[here, :] = rms_rows(r.attended[here, :], one_row(r.ffn_scale))
 
     bands(norm_attended)
 
@@ -416,7 +426,39 @@
             for p, (lo, hi) in enumerate(parts)
         ]
 
-    def expert_chunk(chunk, carry):
+    def keep_own(chunk, y, slot, p):
+        lo, hi = parts[p]
+        free = (LINE[p], PLANE[p][0])
+        spot = [pl.ds(0, side) if axis in free else me[axis] for axis in ROW_AXES[1:]]
+        along = {axis: y if axis == 'y' else pl.ds(0, side) for axis in free}
+        mine = pltpu.make_async_copy(
+            y_buf.at[tuple([slot] + spot + [pl.ds(0, slots), pl.ds(lo, hi - lo)])],
+            middles[p].at[tuple([chunk] + [along[axis] for axis in ROW_AXES if axis in free] + [my_mate[p]])],
+            r.own_sem.at[slot, p],
+        )
+        return mine, (None if 'y' in free else y == me['y'])
+
+    def start_put(chunk, y, slot):
+        for copy in put(chunk, y, slot):
+            copy.start()
+        for p in range(3):
+            copy, when = keep_own(chunk, y, slot, p)
+            if when is None:
+                copy.start()
+            else:
+                pl.when(when)(copy.start)
+
+    def wait_put(chunk, y, slot):
+        for copy in put(chunk, y, slot):
+            copy.wait()
+        for p in range(3):
+            copy, when = keep_own(chunk, y, slot, p)
+            if when is None:
+                copy.wait()
+            else:
+                pl.when(when)(copy.wait)
+
+    def expert_chunk(chunk):
         for p in range(3):
             wait_bytes(sends[p].at[pl.ds(0, mates - 1)], r.go_recv.at[chunk, p])
         for copy in fetch(chunk, 0, 0):
@@ -435,8 +477,7 @@
 
             @pl.when(y >= 2)
             def _():
-                for copy in put(chunk, y - 2, slot):
-                    copy.wait()
+                wait_put(chunk, y - 2, slot)
 
             for lo in range(0, width, f_chunk):
                 cols = slice(lo, lo + f_chunk)
@@ -447,77 +488,82 @@
                 cols = slice(lo, lo + d_chunk)
                 y_rows = dot(hidden_buf[...], r.down[:, cols]).astype(BF16)
                 y_buf[slot, :, :, :, :, cols] = y_rows.reshape(group + (d_chunk,))
-            for copy in put(chunk, y, slot):
-                copy.start()
+            start_put(chunk, y, slot)
             return c
 
         lax.fori_loop(0, side, one_tile, 0)
-        for y in range(max(side - 2, 0), side):
-            for copy in put(chunk, y, y % 2):
-                copy.wait()
-
-        def one_peer(offset, c):
+        for y in range(side - 2, side):
+            wait_put(chunk, y, y % 2)
+
+        def one_mate(offset, c):
             for p in range(3):
-                place = plane_peer(p, offset)
+                place = mate_peer(p, offset)
                 remote(
-                    rows_of(outputs[p], p, chunk, place),
-                    results[p].at[chunk, pl.ds(0, side), member(p, me)],
+                    gathered_rows_of(outputs[p], p, chunk, place),
+                    middles[p].at[chunk, pl.ds(0, side), pl.ds(0, side), my_mate[p]],
                     r.back_send.at[chunk, p],
                     r.back_recv.at[chunk, p],
                     place,
                 ).start()
             return c
 
-        lax.fori_loop(1, members, one_peer, 0)
-        own = [
-            pltpu.make_async_copy(rows_of(outputs[p], p, chunk, me), bounce[p].at[chunk], r.own_sem.at[p])
-            for p in range(3)
-        ]
-        for copy in own:
-            copy.start()
-        for p, copy in enumerate(own):
-            copy.wait()
-            pltpu.make_async_copy(
-                bounce[p].at[chunk], results[p].at[chunk, pl.ds(0, side), member(p, me)], r.back_recv.at[chunk, p]
-            ).start()
-        return carry
-
-    lax.fori_loop(0, N_CHUNKS, expert_chunk, 0)
-
-
-    for p in range(3):
-        wait_bytes(r.line_gates.at[p, pl.ds(0, side - 1)], r.gate_recv.at[p])
+        lax.fori_loop(1, mates, one_mate, 0)
+
+    def middle_rows(p, chunk, i, d):
+        a, b = source_index(p, i, d)
+        return middles[p].at[chunk, a, b]
+
+    def pass_on(chunk):
+        for p in range(3):
+            wait_bytes(middles[p].at[chunk, pl.ds(0, side), pl.ds(0, side), pl.ds(0, mates - 1)], r.back_recv.at[chunk, p])
+            for offset in range(1, side):
+                place = axis_peer(PLANE[p][0], offset)
+                remote(
+                    middle_rows(p, chunk, place[PLANE[p][0]], pl.ds(0, side)),
+                    results[p].at[chunk, pl.ds(0, side), me[PLANE[p][0]]],
+                    r.home_send.at[chunk, p],
+                    r.home_recv.at[chunk, p],
+                    place,
+                ).start()
+
+
     split = r.split
     lanes = min(128, rows_block)
 
-    def weigh_chunk(chunk, carry):
+    def weigh_chunk(chunk):
         for p in range(3):
-            wait_bytes(results[p].at[chunk], r.back_recv.at[chunk, p])
-
-        for p in range(3):
+            wait_bytes(results[p].at[chunk, pl.ds(0, side), pl.ds(0, side - 1)], r.home_recv.at[chunk, p])
+            held = plane_keys(p, (1, rows_block), chunk).astype(F32)
 
             def load(d, slot):
-                return pltpu.make_async_copy(
-                    results[p].at[chunk, d],
-                    stage.at[slot, pl.ds(0, members), :, pl.ds(0, widths[p])],
-                    r.stage_sem.at[slot],
-                )
-
-            load(0, 0).start()
+                copies = []
+                for offset in range(side):
+                    i = lax.rem(me[PLANE[p][0]] + offset, side)
+                    copies.append(
+                        pltpu.make_async_copy(
+                            results[p].at[chunk, d, i] if offset else middle_rows(p, chunk, i, d),
+                            stage.at[slot, pl.ds(i * mates, mates), :, pl.ds(0, widths[p])],
+                            r.load_sem.at[slot, offset],
+                        )
+                    )
+                return copies
+
+            for copy in load(0, 0):
+                copy.start()
 
             def one_source(d, c):
                 slot = lax.rem(d, 2)
 
                 @pl.when(d + 1 < side)
                 def _():
-                    load(d + 1, 1 - slot).start()
+                    for copy in load(d + 1, 1 - slot):
+                        copy.start()
 
                 info = r.line_gates[p, d]
                 keys = [jnp.broadcast_to(info[:, j : j + 1], (tokens, lanes)) for j in range(top_k)]
                 gates = [jnp.broadcast_to(info[:, top_k + j : top_k + j + 1], (tokens, lanes)) for j in range(top_k)]
-                held = plane_keys(p, (tokens, rows_block), chunk)
                 for lo in range(0, rows_block, lanes):
-                    here = held[:, lo : lo + lanes].astype(F32)
+                    here = held[:, lo : lo + lanes]
                     weight = jnp.zeros((tokens, lanes), F32)
                     for j in range(top_k):
                         weight = jnp.where(here == keys[j], gates[j], weight)
@@ -528,26 +574,23 @@
                     split[0:tokens, lo : lo + lanes] = high
                     split[tokens : 2 * tokens, lo : lo + lanes] = middle
                     split[2 * tokens : 3 * tokens, lo : lo + lanes] = low
-                load(d, slot).wait()
+                for copy in load(d, slot):
+                    copy.wait()
                 for lo, n in steps(widths[p], TILE):
                     y = stage[slot, 0:members, :, lo : lo + n].reshape(rows_block, n)
                     both = dot(split[...], y)
                     total = both[0:tokens] + (both[tokens : 2 * tokens] + both[2 * tokens : 3 * tokens])
 
-                    @pl.when(chunk == 0)
-                    def _():
+                    if chunk == 0:
                         sums[p][d, :, lo : lo + n] = total
-
-                    @pl.when(chunk > 0)
-                    def _():
+                    else:
                         sums[p][d, :, lo : lo + n] += total
 
                 return c
 
             lax.fori_loop(0, side, one_source, 0)
 
-            @pl.when(chunk == N_CHUNKS - 1)
-            def _():
+            if chunk == N_CHUNKS - 1:
                 for offset in range(1, side):
                     place = line_peer(p, offset)
                     remote(
@@ -558,9 +601,17 @@
                         place,
                     ).start()
 
-        return carry
-
-    lax.fori_loop(0, N_CHUNKS, weigh_chunk, 0)
+
+    expert_chunk(0)
+    for chunk in range(1, N_CHUNKS):
+        expert_chunk(chunk)
+        pass_on(chunk - 1)
+    for p in range(3):
+        wait_bytes(r.line_gates.at[p, pl.ds(0, side - 1)], r.gate_recv.at[p])
+    weigh_chunk(0)
+    pass_on(N_CHUNKS - 1)
+    for chunk in range(1, N_CHUNKS):
+        weigh_chunk(chunk)
     for p, (lo, hi) in enumerate(parts):
         wait_bytes(others[p], r.sum_recv.at[p])
 
@@ -574,7 +625,8 @@
 
 
     for p in range(3):
-        wait_bytes(tok[p].at[pl.ds(0, side - 1)], r.tok_send.at[p])
+        for offset in range(1, side):
+            wait_bytes(tok[p].at[0], r.tok_send.at[p, offset - 1])
         wait_bytes(r.all_keys.at[p, 0, pl.ds(0, side - 1)], r.key_send.at[p])
         wait_bytes(far[p].at[pl.ds(0, side - 1)], r.far_send.at[p])
         wait_bytes(r.all_keys.at[p, pl.ds(0, side - 1)], r.far_key_send.at[p])
@@ -582,12 +634,13 @@
         wait_bytes(others[p], r.sum_send.at[p])
         for chunk in range(N_CHUNKS):
             wait_bytes(sends[p].at[pl.ds(0, mates - 1)], r.go_send.at[chunk, p])
-            wait_bytes(results[p].at[chunk, pl.ds(0, side), pl.ds(0, members - 1)], r.back_send.at[chunk, p])
+            wait_bytes(middles[p].at[chunk, pl.ds(0, side), pl.ds(0, side), pl.ds(0, mates - 1)], r.back_send.at[chunk, p])
+            wait_bytes(results[p].at[chunk, pl.ds(0, side), pl.ds(0, side - 1)], r.home_send.at[chunk, p])
 
 
 def layer_pair(small, large, side, capacity, head_dim):
     tokens, model = small['hidden'].shape
-    top_k, width = small['ids'].shape[1], large['gate_hbm'].shape[1]
+    top_k, width = small['ids_t'].shape[0], large['gate_hbm'].shape[1]
     key_dim, ff_dim = large['w_key'].shape[1], large['ffn_gate'].shape[1]
     parts = column_parts(model)
     widths = [hi - lo for lo, hi in parts]
@@ -625,9 +678,10 @@
         keep_sem=dma(2, N_CHUNKS),
         in_sem=dma(2, 3),
         out_sem=dma(2, 3),
-        own_sem=dma(3),
-        tok_send=dma(3),
-        tok_recv=dma(3),
+        own_sem=dma(2, 3),
+        load_sem=dma(2, side),
+        tok_send=dma(3, side - 1),
+        tok_recv=dma(3, side - 1),
         key_send=dma(3),
         key_recv=dma(3),
         far_send=dma(3),
@@ -642,6 +696,8 @@
         go_recv=dma(N_CHUNKS, 3),
         back_send=dma(N_CHUNKS, 3),
         back_recv=dma(N_CHUNKS, 3),
+        home_send=dma(N_CHUNKS, 3),
+        home_recv=dma(N_CHUNKS, 3),
     )
     for p, w in enumerate(widths):
         there = sds((N_CHUNKS, side, side, 2, side, slots, w), BF16)
@@ -649,9 +705,9 @@
         outs['send' + str(p)] = sds((N_CHUNKS * mates, side, side, slots, w), BF16)
         outs['arrive' + str(p)] = there
         outs['output' + str(p)] = there
-        outs['result' + str(p)] = sds((N_CHUNKS, side, members, slots, w), BF16)
+        outs['middle' + str(p)] = sds((N_CHUNKS, side, side, mates, slots, w), BF16)
+        outs['result' + str(p)] = sds((N_CHUNKS, side, side, mates, slots, w), BF16)
         scratch['tok' + str(p)] = vmem((side, tokens, w), BF16)
-        scratch['bounce' + str(p)] = vmem((N_CHUNKS, side, slots, w), BF16)
         scratch['sum' + str(p)] = vmem((side, tokens, w), F32)
         scratch['other' + str(p)] = vmem((side - 1, tokens, w), F32)
     anywhere = pl.BlockSpec(memory_space=pl.ANY)
@@ -691,23 +747,21 @@
         n_seqs, tokens, model = hidden.shape
         assert n_seqs == 1 and exp_gate.shape[0] == 1
         n_heads, head_dim = w_out.shape[0], w_out.shape[1]
-        ids = expert_ids[0]
-        capacity = CAP_FACTOR * tokens * ids.shape[1] // group_size
-        keys = ids * capacity + slot_ids[0]
-        inv_freq = ROPE_BASE ** (-2.0 * jnp.arange(head_dim // 2, dtype=F32) / head_dim)
-        angles = jnp.arange(tokens, dtype=F32)[:, None] * inv_freq[None, :]
-        cos, sin = jnp.cos(angles), jnp.sin(angles)
+        top_k = expert_ids.shape[2]
+        capacity = CAP_FACTOR * tokens * top_k // group_size
+        inv_freq = np.float32(ROPE_BASE) ** (np.float32(-2.0) * np.arange(head_dim // 2, dtype=np.float32) / head_dim)
+        angles = np.arange(tokens, dtype=np.float32)[:, None] * inv_freq[None, :]
+        cos, sin = np.cos(angles), np.sin(angles)
         small = dict(
             hidden=hidden[0],
-            attn_norm=attn_norm.reshape(1, model),
-            moe_norm=moe_norm.reshape(1, model),
-            ffn_norm=ffn_norm.reshape(1, model),
-            keys_t=keys.T,
-            keys_f=jnp.pad(keys.astype(F32), ((0, 0), (0, 128 - keys.shape[1]))),
-            ids=ids,
+            attn_scale=attn_norm.reshape(-1, 128),
+            moe_scale=moe_norm.reshape(-1, 128),
+            ffn_scale=ffn_norm.reshape(-1, 128),
+            ids_t=expert_ids[0].T,
+            slots_t=slot_ids[0].T,
             w_router=w_router,
-            cos=jnp.concatenate([cos, cos], axis=1),
-            sin=jnp.concatenate([-sin, sin], axis=1),
+            cos=np.concatenate([cos, cos], axis=1).astype(np.float32),
+            sin=np.concatenate([-sin, sin], axis=1).astype(np.float32),
         )
         large = dict(
             w_query=w_query,

time: 527 us -> 459 us (0.87)
  the two profiles are of different devices: /device:TPU:100 before, /device:TPU:0 now
where the time goes in v3:
time: 459 us; the launch traced here: 458 us
  Pallas kernels  456 us (99%)
    pallas_call x1, Pallas kernels, layer_pair(): pl.pallas_call(functools.partial(kernel, names=tuple(small) + tuple(large...  456 us

profile of v3, /device:TPU:0, one launch (start us, length us, event | category | flops | bytes accessed | tf_op | source)
XLA Modules:
  0.0 458.1 jit_solution(3933799801884857862)
XLA Ops:
  0.0 455.8 %shard_map.181 = (bf16[256,2048]{1,0:T(8,128)(2,1)}, bf16[4,4,256,768]{3,2,1,0:T(8,128)(2,1)}, bf16[24,4,4,16,768]{4,3,2,1,0:T(8,128)(2,1)}, bf16[3,4,4,2,4,16,7...) custom-call(bf16[256,2048]{1,0:T(8,128)(2,1)} %bitcast.20, ...), custom_call_target="tpu_custom_call" | custom-call | flops 57982058496 | bytes 100663296 | tf_op jit(solution)/shard_map/pallas_call | solution.py:716
  455.8 2.3 copy.21

commit v4 on v3

--- a/solution.py
+++ b/solution.py
@@ -65,10 +65,12 @@
     me = {axis: lax.axis_index(axis) for axis in AXES}
 
 
-    def gathered_rows_of(ref, p, chunk, place):
-        free = (LINE[p], PLANE[p][0])
+    def rows_of(ref, p, chunk, place, free):
         spot = [pl.ds(0, side) if axis in free else place[axis] for axis in ROW_AXES]
         return ref.at[tuple([chunk] + spot)]
+
+    def gathered_rows_of(ref, p, chunk, place):
+        return rows_of(ref, p, chunk, place, (LINE[p], PLANE[p][0]))
 
     def source_index(p, i, d):
         where = {PLANE[p][0]: i, LINE[p]: d}
@@ -149,7 +151,11 @@
         for offset in range(1, side):
             here = me[PLANE[p][0]]
             remote(
-                tok[p].at[d], far[p].at[here, d], r.far_send.at[p], r.far_recv.at[p], axis_peer(PLANE[p][0], offset)
+                tok[p].at[d],
+                far[p].at[here, d],
+                r.far_send.at[p],
+                r.far_recv.at[p, offset - 1],
+                axis_peer(PLANE[p][0], offset),
             ).start()
 
     for offset in range(1, side):
@@ -232,16 +238,21 @@
         r.line_gates[p, me[LINE[p]]] = info
 
 
-    for offset in range(1, side):
+    def hand_on(offset):
         for p in range(3):
             d = lax.rem(me[LINE[p]] + side - offset, side)
             wait_bytes(tok[p].at[d], r.tok_recv.at[p, offset - 1])
             send_far(p, d)
+
+    for offset in range(1, side):
+        hand_on(offset)
     for p in range(3):
         wait_bytes(r.all_keys.at[p, 0, pl.ds(0, side - 1)], r.key_recv.at[p])
         for offset in range(1, side):
             keys = r.all_keys.at[p, me[PLANE[p][0]]]
-            remote(keys, keys, r.far_key_send.at[p], r.far_key_recv.at[p], axis_peer(PLANE[p][0], offset)).start()
+            remote(
+                keys, keys, r.far_key_send.at[p], r.far_key_recv.at[p, offset - 1], axis_peer(PLANE[p][0], offset)
+            ).start()
     for offset in range(1, side):
         for p in range(3):
             spot = me[LINE[p]]
@@ -266,8 +277,6 @@
         r.query[:, cols] = dot(prob, r.value[:, key_cols]).astype(BF16)
         return carry
 
-    lax.fori_loop(0, n_heads, one_head, 0)
-
 
     stage = r.stage
     blocks = N_CHUNKS * mates
@@ -300,71 +309,81 @@
             r.keep_sem.at[slot, chunk],
         )
 
-    for p in range(3):
-        sources = side * side
-        near = me[PLANE[p][0]]
-        wanted = mate_keys(p, (blocks * slots, min(128, tokens)))
-        wait_bytes(r.all_keys.at[p, pl.ds(0, side - 1)], r.far_key_recv.at[p])
-        wait_bytes(far[p].at[pl.ds(0, side - 1)], r.far_recv.at[p])
-
-        def place_of(n):
-            return lax.rem(near + n // side, side), lax.rem(n, side)
-
-        def load(n, slot):
-            i, d = place_of(n)
-            return pltpu.make_async_copy(far[p].at[i, d], r.source.at[slot, :, pl.ds(0, widths[p])], r.source_sem.at[slot])
-
-        def one_source(n, c):
-            slot = lax.rem(n, 2)
-            i, d = place_of(n)
-
-            @pl.when(jnp.logical_and(n + 1 >= side, n + 1 < sources))
-            def _():
-                load(n + 1, 1 - slot).start()
-
-            @pl.when(n >= side)
-            def _():
-                load(n, slot).wait()
-
-            @pl.when(n < side)
-            def _():
-                r.source[slot, :, 0 : widths[p]] = tok[p][d]
-
-            @pl.when(n >= 2)
-            def _():
-                i2, d2 = place_of(n - 2)
-                flush(p, i2, d2, slot).wait()
+    wanted = [mate_keys(p, (blocks * slots, min(128, tokens))) for p in range(3)]
+
+    def send_rows(p, chunk, i):
+        free = (LINE[p],) if i is not None else (LINE[p], PLANE[p][0])
+        a, b = source_index(p, pl.ds(0, side) if i is None else i, pl.ds(0, side))
+        group_place = me if i is None else {**me, PLANE[p][0]: i}
+
+        def one_mate(offset, c):
+            place = mate_peer(p, offset)
+            remote(
+                sends[p].at[chunk * mates + place[PLANE[p][1]] * 2 + place['c'], a, b],
+                rows_of(arrivals[p], p, chunk, group_place, free),
+                r.go_send.at[chunk, p],
+                r.go_recv.at[chunk, p],
+                place,
+            ).start()
+            return c
+
+        lax.fori_loop(1, mates, one_mate, 0)
+
+    def pick_group(offset):
+        for p in range(3):
+            i = lax.rem(me[PLANE[p][0]] + side - offset, side)
+            if offset:
+                wait_bytes(r.all_keys.at[p, 0], r.far_key_recv.at[p, offset - 1])
+                wait_bytes(far[p].at[0], r.far_recv.at[p, offset - 1])
+
+            def load(d, slot):
+                return pltpu.make_async_copy(
+                    far[p].at[i, d], r.source.at[slot, :, pl.ds(0, widths[p])], r.source_sem.at[slot]
+                )
+
+            if offset:
+                load(0, 0).start()
+
+            def one_source(d, c):
+                slot = lax.rem(d, 2)
+                if offset:
+
+                    @pl.when(d + 1 < side)
+                    def _():
+                        load(d + 1, 1 - slot).start()
+
+                    load(d, slot).wait()
+
+                @pl.when(d >= 2)
+                def _():
+                    flush(p, i, d - 2, slot).wait()
+                    for chunk in range(N_CHUNKS):
+                        keep(p, i, d - 2, slot, chunk).wait()
+
+                pick_rows(p, i, d, slot, r.source.at[slot] if offset else tok[p].at[d], wanted[p])
+                flush(p, i, d, slot).start()
                 for chunk in range(N_CHUNKS):
-                    keep(p, i2, d2, slot, chunk).wait()
-
-            pick_rows(p, i, d, slot, r.source.at[slot], wanted)
-            flush(p, i, d, slot).start()
-            for chunk in range(N_CHUNKS):
-                keep(p, i, d, slot, chunk).start()
-            return c
-
-        lax.fori_loop(0, sources, one_source, 0)
-        for n in range(sources - 2, sources):
-            i, d = place_of(n)
-            flush(p, i, d, n % 2).wait()
-            for chunk in range(N_CHUNKS):
-                keep(p, i, d, n % 2, chunk).wait()
-
-        def go_chunk(chunk, c):
-            def one_mate(offset, c2):
-                place = mate_peer(p, offset)
-                remote(
-                    sends[p].at[chunk * mates + place[PLANE[p][1]] * 2 + place['c']],
-                    gathered_rows_of(arrivals[p], p, chunk, me),
-                    r.go_send.at[chunk, p],
-                    r.go_recv.at[chunk, p],
-                    place,
-                ).start()
-                return c2
-
-            return lax.fori_loop(1, mates, one_mate, c)
-
-        lax.fori_loop(0, N_CHUNKS, go_chunk, 0)
+                    keep(p, i, d, slot, chunk).start()
+                return c
+
+            lax.fori_loop(0, side, one_source, 0)
+            for d in range(side - 2, side):
+                flush(p, i, d, d % 2).wait()
+                for chunk in range(N_CHUNKS):
+                    keep(p, i, d, d % 2, chunk).wait()
+            send_rows(p, 0, i)
+
+    def heads(part, n_parts):
+        lax.fori_loop(n_heads * part // n_parts, n_heads * (part + 1) // n_parts, one_head, 0)
+
+    heads(0, 2)
+    pick_group(0)
+    for offset in range(1, side):
+        heads(side - 2 + offset, 2 * (side - 1))
+        pick_group(offset)
+    for chunk in range(1, N_CHUNKS):
+        for p in range(3):
+            send_rows(p, chunk, None)
 
 
     out_split = n_heads * head_dim // model
@@ -530,35 +549,44 @@
     split = r.split
     lanes = min(128, rows_block)
 
-    def weigh_chunk(chunk):
+    def weigh_chunk(chunk, carry):
+        @pl.when(chunk == 1)
+        def _():
+            pass_on(N_CHUNKS - 1)
+
         for p in range(3):
             wait_bytes(results[p].at[chunk, pl.ds(0, side), pl.ds(0, side - 1)], r.home_recv.at[chunk, p])
-            held = plane_keys(p, (1, rows_block), chunk).astype(F32)
-
-            def load(d, slot):
-                copies = []
-                for offset in range(side):
-                    i = lax.rem(me[PLANE[p][0]] + offset, side)
-                    copies.append(
-                        pltpu.make_async_copy(
-                            results[p].at[chunk, d, i] if offset else middle_rows(p, chunk, i, d),
-                            stage.at[slot, pl.ds(i * mates, mates), :, pl.ds(0, widths[p])],
-                            r.load_sem.at[slot, offset],
-                        )
+
+        def source_of(p, n):
+            return lax.rem(me[LINE[p]] + 1 + n, side)
+
+        def load(p, n, slot):
+            copies = []
+            for offset in range(side):
+                i, d = lax.rem(me[PLANE[p][0]] + offset, side), source_of(p, n)
+                copies.append(
+                    pltpu.make_async_copy(
+                        results[p].at[chunk, d, i] if offset else middle_rows(p, chunk, i, d),
+                        stage.at[slot, pl.ds(i * mates, mates), :, pl.ds(0, widths[p])],
+                        r.load_sem.at[slot, offset],
                     )
-                return copies
-
-            for copy in load(0, 0):
-                copy.start()
-
-            def one_source(d, c):
-                slot = lax.rem(d, 2)
-
-                @pl.when(d + 1 < side)
+                )
+            return copies
+
+        for copy in load(0, 0, 0):
+            copy.start()
+
+        def one_source(n, c):
+            for p in range(3):
+                d = source_of(p, n)
+                slot = lax.rem(n + p, 2)
+
+                @pl.when(n + p // 2 < side)
                 def _():
-                    for copy in load(d + 1, 1 - slot):
+                    for copy in load((p + 1) % 3, n + p // 2, 1 - slot):
                         copy.start()
 
+                held = plane_keys(p, (1, rows_block), chunk).astype(F32)
                 info = r.line_gates[p, d]
                 keys = [jnp.broadcast_to(info[:, j : j + 1], (tokens, lanes)) for j in range(top_k)]
                 gates = [jnp.broadcast_to(info[:, top_k + j : top_k + j + 1], (tokens, lanes)) for j in range(top_k)]
@@ -574,44 +602,41 @@
                     split[0:tokens, lo : lo + lanes] = high
                     split[tokens : 2 * tokens, lo : lo + lanes] = middle
                     split[2 * tokens : 3 * tokens, lo : lo + lanes] = low
-                for copy in load(d, slot):
+                for copy in load(p, n, slot):
                     copy.wait()
-                for lo, n in steps(widths[p], TILE):
-                    y = stage[slot, 0:members, :, lo : lo + n].reshape(rows_block, n)
+                for lo, size in steps(widths[p], TILE):
+                    y = stage[slot, 0:members, :, lo : lo + size].reshape(rows_block, size)
                     both = dot(split[...], y)
                     total = both[0:tokens] + (both[tokens : 2 * tokens] + both[2 * tokens : 3 * tokens])
 
-                    if chunk == 0:
-                        sums[p][d, :, lo : lo + n] = total
-                    else:
-                        sums[p][d, :, lo : lo + n] += total
-
-                return c
-
-            lax.fori_loop(0, side, one_source, 0)
-
-            if chunk == N_CHUNKS - 1:
-                for offset in range(1, side):
-                    place = line_peer(p, offset)
+                    @pl.when(chunk == 0)
+                    def _():
+                        sums[p][d, :, lo : lo + size] = total
+
+                    @pl.when(chunk > 0)
+                    def _():
+                        sums[p][d, :, lo : lo + size] += total
+
+                @pl.when(jnp.logical_and(chunk == N_CHUNKS - 1, n < side - 1))
+                def _():
                     remote(
-                        sums[p].at[place[LINE[p]]],
-                        others[p].at[offset - 1],
-                        r.sum_send.at[p],
-                        r.sum_recv.at[p],
-                        place,
+                        sums[p].at[d], others[p].at[n], r.sum_send.at[p], r.sum_recv.at[p], {**me, LINE[p]: d}
                     ).start()
 
-
-    expert_chunk(0)
-    for chunk in range(1, N_CHUNKS):
+            return c
+
+        return lax.fori_loop(0, side, one_source, carry)
+
+
+    def experts_and_back(chunk, carry):
         expert_chunk(chunk)
-        pass_on(chunk - 1)
+        pl.when(chunk >= 1)(lambda: pass_on(chunk - 1))
+        return carry
+
+    lax.fori_loop(0, N_CHUNKS, experts_and_back, 0)
     for p in range(3):
         wait_bytes(r.line_gates.at[p, pl.ds(0, side - 1)], r.gate_recv.at[p])
-    weigh_chunk(0)
-    pass_on(N_CHUNKS - 1)
-    for chunk in range(1, N_CHUNKS):
-        weigh_chunk(chunk)
+    lax.fori_loop(0, N_CHUNKS, weigh_chunk, 0)
     for p, (lo, hi) in enumerate(parts):
         wait_bytes(others[p], r.sum_recv.at[p])
 
@@ -685,9 +710,9 @@
         key_send=dma(3),
         key_recv=dma(3),
         far_send=dma(3),
-        far_recv=dma(3),
+        far_recv=dma(3, side - 1),
         far_key_send=dma(3),
-        far_key_recv=dma(3),
+        far_key_recv=dma(3, side - 1),
         gate_send=dma(3),
         gate_recv=dma(3),
         sum_send=dma(3),

time: 459 us -> 462 us (level)
  no operation moved by 1% of the time
where the time goes in v4:
time: 462 us; the launch traced here: 459 us
  Pallas kernels  456 us (99%)
    pallas_call x1, Pallas kernels, layer_pair(): pl.pallas_call(functools.partial(kernel, names=tuple(small) + tuple(large...  456 us

profile of v4, /device:TPU:0, one launch (start us, length us, event | category | flops | bytes accessed | tf_op | source)
XLA Modules:
  0.0 458.7 jit_solution(14393886008488488666)
XLA Ops:
  0.0 456.4 %shard_map.181 = (bf16[256,2048]{1,0:T(8,128)(2,1)}, bf16[4,4,256,768]{3,2,1,0:T(8,128)(2,1)}, bf16[24,4,4,16,768]{4,3,2,1,0:T(8,128)(2,1)}, bf16[3,4,4,2,4,16,7...) custom-call(bf16[256,2048]{1,0:T(8,128)(2,1)} %bitcast.20, ...), custom_call_target="tpu_custom_call" | custom-call | flops 57982058496 | bytes 100663296 | tf_op jit(solution)/shard_map/pallas_call | solution.py:741
  456.4 2.3 copy.21

commit v5 on v4

--- a/solution.py
+++ b/solution.py
@@ -21,8 +21,8 @@
 BF16, F32, I32 = jnp.bfloat16, jnp.float32, jnp.int32
 
 AXES = ('z', 'y', 'x', 'c')
-LINE = ('z', 'x', 'y')
-PLANE = (('y', 'x'), ('z', 'y'), ('x', 'z'))
+OUT = (('z', 'y', 'x'), ('x', 'z', 'y'), ('y', 'x', 'z'))
+BACK = (('y', 'z', 'x'), ('z', 'x', 'y'), ('x', 'y', 'z'))
 ROW_AXES = ('y', 'x', 'c', 'z')
 
 
@@ -69,11 +69,7 @@
         spot = [pl.ds(0, side) if axis in free else place[axis] for axis in ROW_AXES]
         return ref.at[tuple([chunk] + spot)]
 
-    def gathered_rows_of(ref, p, chunk, place):
-        return rows_of(ref, p, chunk, place, (LINE[p], PLANE[p][0]))
-
-    def source_index(p, i, d):
-        where = {PLANE[p][0]: i, LINE[p]: d}
+    def ordered(where):
         return tuple(where[axis] for axis in ROW_AXES if axis in where)
 
     def device(place):
@@ -82,11 +78,7 @@
     def axis_peer(axis, offset):
         return {**me, axis: lax.rem(me[axis] + offset, side)}
 
-    def line_peer(p, offset):
-        return axis_peer(LINE[p], offset)
-
-    def mate_peer(p, offset):
-        axis = PLANE[p][1]
+    def mate_peer(axis, offset):
         return {
             **me,
             axis: lax.rem(me[axis] + offset // 2, side),
@@ -105,17 +97,18 @@
         return (((place['z'] * side + place['y']) * side + place['x']) * 2 + core) * capacity + slot
 
     def plane_keys(p, shape, chunk):
+        first, second, _ = BACK[p]
         row = lax.broadcasted_iota(I32, shape, 1)
         which, slot = row // slots, lax.rem(row, slots)
         pair = which // 2
-        place = {PLANE[p][0]: pair // side, PLANE[p][1]: lax.rem(pair, side), LINE[p]: me[LINE[p]]}
+        place = {**me, second: pair // side, first: lax.rem(pair, side)}
         return expert_key(place, lax.rem(which, 2), slot + chunk * slots)
 
     def mate_keys(p, shape):
         row = lax.broadcasted_iota(I32, shape, 0)
         block, slot = row // slots, lax.rem(row, slots)
         chunk, mate = block // mates, lax.rem(block, mates)
-        place = {**me, PLANE[p][1]: mate // 2}
+        place = {**me, OUT[p][2]: mate // 2}
         return expert_key(place, lax.rem(mate, 2), slot + chunk * slots)
 
     tok, far, sends, arrivals, outputs = each('tok'), each('far'), each('send'), each('arrive'), each('output')
@@ -135,13 +128,13 @@
     def norm_both(here):
         normed = rms_rows(r.hidden[here, :], one_row(r.moe_scale))
         for p, (lo, hi) in enumerate(parts):
-            tok[p][me[LINE[p]], here, :] = normed[:, lo:hi]
+            tok[p][me[OUT[p][0]], here, :] = normed[:, lo:hi]
         r.rows[here, :] = rms_rows(r.hidden[here, :], one_row(r.attn_scale))
 
     bands(norm_both)
     keys_t = r.ids_t[...] * capacity + r.slots_t[...]
     for p in range(3):
-        r.all_keys[p, me[PLANE[p][0]], me[LINE[p]]] = keys_t
+        r.all_keys[p, me[OUT[p][1]], me[OUT[p][0]]] = keys_t
     pairs = ((r.gate_hbm, r.gate), (r.up_hbm, r.up), (r.down_hbm, r.down))
     loads = [pltpu.make_async_copy(src, dst, r.weight_sem.at[i]) for i, (src, dst) in enumerate(pairs)]
     for load in loads:
@@ -149,25 +142,25 @@
 
     def send_far(p, d):
         for offset in range(1, side):
-            here = me[PLANE[p][0]]
+            here = me[OUT[p][1]]
             remote(
                 tok[p].at[d],
                 far[p].at[here, d],
                 r.far_send.at[p],
                 r.far_recv.at[p, offset - 1],
-                axis_peer(PLANE[p][0], offset),
+                axis_peer(OUT[p][1], offset),
             ).start()
 
     for offset in range(1, side):
         for p in range(3):
-            spot, place = me[LINE[p]], line_peer(p, offset)
+            spot, place = me[OUT[p][0]], axis_peer(OUT[p][0], offset)
             remote(
                 tok[p].at[spot], tok[p].at[spot], r.tok_send.at[p, offset - 1], r.tok_recv.at[p, offset - 1], place
             ).start()
-            keys = r.all_keys.at[p, me[PLANE[p][0]], spot]
+            keys = r.all_keys.at[p, me[OUT[p][1]], spot]
             remote(keys, keys, r.key_send.at[p], r.key_recv.at[p], place).start()
     for p in range(3):
-        send_far(p, me[LINE[p]])
+        send_far(p, me[OUT[p][0]])
 
 
     ring = r.ring
@@ -217,7 +210,7 @@
     project(r.w_value, r.value, False)
 
 
-    logits = sum(dot(tok[p][me[LINE[p]]], r.w_router[lo:hi, :]) for p, (lo, hi) in enumerate(parts))
+    logits = sum(dot(tok[p][me[OUT[p][0]]], r.w_router[lo:hi, :]) for p, (lo, hi) in enumerate(parts))
     top_k = r.ids_t.shape[0]
     gap = jnp.zeros((128 - 3 * top_k, tokens), F32)
     blank = jnp.zeros((top_k, tokens), F32)
@@ -235,12 +228,12 @@
         info = jnp.where(lane == top_k + j, powers[j] / norm, info)
     r.my_gates[...] = info
     for p in range(3):
-        r.line_gates[p, me[LINE[p]]] = info
+        r.line_gates[p, me[BACK[p][2]]] = info
 
 
     def hand_on(offset):
         for p in range(3):
-            d = lax.rem(me[LINE[p]] + side - offset, side)
+            d = lax.rem(me[OUT[p][0]] + side - offset, side)
             wait_bytes(tok[p].at[d], r.tok_recv.at[p, offset - 1])
             send_far(p, d)
 
@@ -249,15 +242,15 @@
     for p in range(3):
         wait_bytes(r.all_keys.at[p, 0, pl.ds(0, side - 1)], r.key_recv.at[p])
         for offset in range(1, side):
-            keys = r.all_keys.at[p, me[PLANE[p][0]]]
+            keys = r.all_keys.at[p, me[OUT[p][1]]]
             remote(
-                keys, keys, r.far_key_send.at[p], r.far_key_recv.at[p, offset - 1], axis_peer(PLANE[p][0], offset)
+                keys, keys, r.far_key_send.at[p], r.far_key_recv.at[p, offset - 1], axis_peer(OUT[p][1], offset)
             ).start()
     for offset in range(1, side):
         for p in range(3):
-            spot = me[LINE[p]]
+            axis = BACK[p][2]
             remote(
-                r.my_gates, r.line_gates.at[p, spot], r.gate_send.at[p], r.gate_recv.at[p], line_peer(p, offset)
+                r.my_gates, r.line_gates.at[p, me[axis]], r.gate_send.at[p], r.gate_recv.at[p], axis_peer(axis, offset)
             ).start()
 
 
@@ -280,7 +273,8 @@
 
     stage = r.stage
     blocks = N_CHUNKS * mates
-    my_mate = {p: me[PLANE[p][1]] * 2 + me['c'] for p in range(3)}
+    out_mate = [me[OUT[p][2]] * 2 + me['c'] for p in range(3)]
+    back_mate = [me[BACK[p][0]] * 2 + me['c'] for p in range(3)]
 
     def pick_rows(p, i, d, slot, source, wanted):
         keys = r.all_keys[p, i, d]
@@ -294,7 +288,7 @@
             stage[slot, 0:blocks, :, lo : lo + n] = found.reshape(blocks, slots, n)
 
     def flush(p, i, d, slot):
-        a, b = source_index(p, i, d)
+        a, b = ordered({OUT[p][1]: i, OUT[p][0]: d})
         return pltpu.make_async_copy(
             stage.at[slot, pl.ds(0, blocks), :, pl.ds(0, widths[p])],
             sends[p].at[pl.ds(0, blocks), a, b],
@@ -302,24 +296,25 @@
         )
 
     def keep(p, i, d, slot, chunk):
-        spot = {**me, PLANE[p][0]: i, LINE[p]: d}
+        spot = {**me, OUT[p][1]: i, OUT[p][0]: d}
         return pltpu.make_async_copy(
-            stage.at[slot, chunk * mates + my_mate[p], :, pl.ds(0, widths[p])],
-            arrivals[p].at[tuple([chunk] + [spot[axis] for axis in ROW_AXES])],
+            stage.at[slot, chunk * mates + out_mate[p], :, pl.ds(0, widths[p])],
+            arrivals[p].at[(chunk,) + ordered(spot)],
             r.keep_sem.at[slot, chunk],
         )
 
     wanted = [mate_keys(p, (blocks * slots, min(128, tokens))) for p in range(3)]
 
     def send_rows(p, chunk, i):
-        free = (LINE[p],) if i is not None else (LINE[p], PLANE[p][0])
-        a, b = source_index(p, pl.ds(0, side) if i is None else i, pl.ds(0, side))
-        group_place = me if i is None else {**me, PLANE[p][0]: i}
+        near, far_axis, axis = OUT[p]
+        free = (near,) if i is not None else (near, far_axis)
+        a, b = ordered({far_axis: pl.ds(0, side) if i is None else i, near: pl.ds(0, side)})
+        group_place = me if i is None else {**me, far_axis: i}
 
         def one_mate(offset, c):
-            place = mate_peer(p, offset)
+            place = mate_peer(axis, offset)
             remote(
-                sends[p].at[chunk * mates + place[PLANE[p][1]] * 2 + place['c'], a, b],
+                sends[p].at[chunk * mates + place[axis] * 2 + place['c'], a, b],
                 rows_of(arrivals[p], p, chunk, group_place, free),
                 r.go_send.at[chunk, p],
                 r.go_recv.at[chunk, p],
@@ -331,7 +326,7 @@
 
     def pick_group(offset):
         for p in range(3):
-            i = lax.rem(me[PLANE[p][0]] + side - offset, side)
+            i = lax.rem(me[OUT[p][1]] + side - offset, side)
             if offset:
                 wait_bytes(r.all_keys.at[p, 0], r.far_key_recv.at[p, offset - 1])
                 wait_bytes(far[p].at[0], r.far_recv.at[p, offset - 1])
@@ -447,12 +442,13 @@
 
     def keep_own(chunk, y, slot, p):
         lo, hi = parts[p]
-        free = (LINE[p], PLANE[p][0])
+        free = BACK[p][1:]
         spot = [pl.ds(0, side) if axis in free else me[axis] for axis in ROW_AXES[1:]]
-        along = {axis: y if axis == 'y' else pl.ds(0, side) for axis in free}
         mine = pltpu.make_async_copy(
             y_buf.at[tuple([slot] + spot + [pl.ds(0, slots), pl.ds(lo, hi - lo)])],
-            middles[p].at[tuple([chunk] + [along[axis] for axis in ROW_AXES if axis in free] + [my_mate[p]])],
+            middles[p].at[
+                (chunk,) + ordered({axis: y if axis == 'y' else pl.ds(0, side) for axis in free}) + (back_mate[p],)
+            ],
             r.own_sem.at[slot, p],
         )
         return mine, (None if 'y' in free else y == me['y'])
@@ -516,10 +512,10 @@
 
         def one_mate(offset, c):
             for p in range(3):
-                place = mate_peer(p, offset)
+                place = mate_peer(BACK[p][0], offset)
                 remote(
-                    gathered_rows_of(outputs[p], p, chunk, place),
-                    middles[p].at[chunk, pl.ds(0, side), pl.ds(0, side), my_mate[p]],
+                    rows_of(outputs[p], p, chunk, place, BACK[p][1:]),
+                    middles[p].at[chunk, pl.ds(0, side), pl.ds(0, side), back_mate[p]],
                     r.back_send.at[chunk, p],
                     r.back_recv.at[chunk, p],
                     place,
@@ -529,17 +525,17 @@
         lax.fori_loop(1, mates, one_mate, 0)
 
     def middle_rows(p, chunk, i, d):
-        a, b = source_index(p, i, d)
-        return middles[p].at[chunk, a, b]
+        return middles[p].at[(chunk,) + ordered({BACK[p][1]: i, BACK[p][2]: d})]
 
     def pass_on(chunk):
         for p in range(3):
             wait_bytes(middles[p].at[chunk, pl.ds(0, side), pl.ds(0, side), pl.ds(0, mates - 1)], r.back_recv.at[chunk, p])
             for offset in range(1, side):
-                place = axis_peer(PLANE[p][0], offset)
+                axis = BACK[p][1]
+                place = axis_peer(axis, offset)
                 remote(
-                    middle_rows(p, chunk, place[PLANE[p][0]], pl.ds(0, side)),
-                    results[p].at[chunk, pl.ds(0, side), me[PLANE[p][0]]],
+                    middle_rows(p, chunk, place[axis], pl.ds(0, side)),
+                    results[p].at[chunk, pl.ds(0, side), me[axis]],
                     r.home_send.at[chunk, p],
                     r.home_recv.at[chunk, p],
                     place,
@@ -558,12 +554,12 @@
             wait_bytes(results[p].at[chunk, pl.ds(0, side), pl.ds(0, side - 1)], r.home_recv.at[chunk, p])
 
         def source_of(p, n):
-            return lax.rem(me[LINE[p]] + 1 + n, side)
+            return lax.rem(me[BACK[p][2]] + 1 + n, side)
 
         def load(p, n, slot):
             copies = []
             for offset in range(side):
-                i, d = lax.rem(me[PLANE[p][0]] + offset, side), source_of(p, n)
+                i, d = lax.rem(me[BACK[p][1]] + offset, side), source_of(p, n)
                 copies.append(
                     pltpu.make_async_copy(
                         results[p].at[chunk, d, i] if offset else middle_rows(p, chunk, i, d),
@@ -620,7 +616,7 @@
                 @pl.when(jnp.logical_and(chunk == N_CHUNKS - 1, n < side - 1))
                 def _():
                     remote(
-                        sums[p].at[d], others[p].at[n], r.sum_send.at[p], r.sum_recv.at[p], {**me, LINE[p]: d}
+                        sums[p].at[d], others[p].at[n], r.sum_send.at[p], r.sum_recv.at[p], {**me, BACK[p][2]: d}
                     ).start()
 
             return c
@@ -641,7 +637,7 @@
         wait_bytes(others[p], r.sum_recv.at[p])
 
         def finish(here):
-            moe = sums[p][me[LINE[p]], here, :]
+            moe = sums[p][me[BACK[p][2]], here, :]
             for offset in range(1, side):
                 moe += others[p][offset - 1, here, :]
             r.out[here, lo:hi] = (r.dense[here, lo:hi] + moe).astype(BF16)

time: 462 us -> 458 us (level)
  no operation moved by 1% of the time
where the time goes in v5:
time: 458 us; the launch traced here: 456 us
  Pallas kernels  454 us (99%)
    pallas_call x1, Pallas kernels, layer_pair(): pl.pallas_call(functools.partial(kernel, names=tuple(small) + tuple(large...  454 us

profile of v5, /device:TPU:0, one launch (start us, length us, event | category | flops | bytes accessed | tf_op | source)
XLA Modules:
  0.0 456.1 jit_solution(15710981456259586321)
XLA Ops:
  0.0 453.8 %shard_map.181 = (bf16[256,2048]{1,0:T(8,128)(2,1)}, bf16[4,4,256,768]{3,2,1,0:T(8,128)(2,1)}, bf16[24,4,4,16,768]{4,3,2,1,0:T(8,128)(2,1)}, bf16[3,4,4,2,4,16,7...) custom-call(bf16[256,2048]{1,0:T(8,128)(2,1)} %bitcast.20, ...), custom_call_target="tpu_custom_call" | custom-call | flops 57982058496 | bytes 100663296 | tf_op jit(solution)/shard_map/pallas_call | solution.py:737
  453.8 2.3 copy.21

commit v6 on v5

--- a/solution.py
+++ b/solution.py
@@ -60,6 +60,10 @@
     slots = capacity // N_CHUNKS
     members = side * side * 2
     mates = side * 2
+    assert side in (2, 4)
+    relay = side == 4
+    strides = (1, side - 1) if relay else (1,)
+    order = (0, side - 1, 1, 2) if relay else (0, 1)
     rows_block = members * slots
     tokens, model = r.hidden.shape
     me = {axis: lax.axis_index(axis) for axis in AXES}
@@ -140,27 +144,42 @@
     for load in loads:
         load.start()
 
-    def send_far(p, d):
-        for offset in range(1, side):
-            here = me[OUT[p][1]]
+    half = tokens // 2
+    halves = (pl.ds(0, half), pl.ds(half, half))
+
+    def neighbour(axis, k):
+        return lax.rem(me[axis] + side - strides[k], side)
+
+    def send_far(p, n):
+        near, axis, _ = OUT[p]
+        d = lax.rem(me[near] + order[n], side)
+        for k, stride in enumerate(strides):
             remote(
-                tok[p].at[d],
-                far[p].at[here, d],
-                r.far_send.at[p],
-                r.far_recv.at[p, offset - 1],
-                axis_peer(OUT[p][1], offset),
+                tok[p].at[d], far[p].at[me[axis], d], r.far_send.at[p], r.far_recv.at[p, k, n], axis_peer(axis, stride)
             ).start()
 
+    def pass_far(n):
+        for k, stride in enumerate(strides):
+            for p in range(3):
+                near, axis, _ = OUT[p]
+                d = lax.rem(me[near] + order[n], side)
+                wait_bytes(tok[p].at[0], r.far_recv.at[p, k, n])
+                if relay:
+                    block = far[p].at[neighbour(axis, k), d, halves[k]]
+                    remote(block, block, r.far_send.at[p], r.far_half.at[p, k, n], axis_peer(axis, stride)).start()
+
+    for k, stride in enumerate(strides):
+        for p in range(3):
+            axis = OUT[p][0]
+            block = tok[p].at[me[axis]]
+            remote(block, block, r.tok_send.at[p], r.tok_recv.at[p, k], axis_peer(axis, stride)).start()
+    for p in range(3):
+        send_far(p, 0)
     for offset in range(1, side):
         for p in range(3):
-            spot, place = me[OUT[p][0]], axis_peer(OUT[p][0], offset)
-            remote(
-                tok[p].at[spot], tok[p].at[spot], r.tok_send.at[p, offset - 1], r.tok_recv.at[p, offset - 1], place
-            ).start()
-            keys = r.all_keys.at[p, me[OUT[p][1]], spot]
-            remote(keys, keys, r.key_send.at[p], r.key_recv.at[p], place).start()
-    for p in range(3):
-        send_far(p, me[OUT[p][0]])
+            axis = OUT[p][0]
+            keys = r.all_keys.at[p, me[OUT[p][1]], me[axis]]
+            remote(keys, keys, r.key_send.at[p], r.key_recv.at[p], axis_peer(axis, offset)).start()
 
 
     ring = r.ring
@@ -231,14 +250,20 @@
         r.line_gates[p, me[BACK[p][2]]] = info
 
 
-    def hand_on(offset):
-        for p in range(3):
-            d = lax.rem(me[OUT[p][0]] + side - offset, side)
-            wait_bytes(tok[p].at[d], r.tok_recv.at[p, offset - 1])
-            send_far(p, d)
-
-    for offset in range(1, side):
-        hand_on(offset)
+    for k, stride in enumerate(strides):
+        for p in range(3):
+            axis = OUT[p][0]
+            wait_bytes(tok[p].at[0], r.tok_recv.at[p, k])
+            if relay:
+                block = tok[p].at[neighbour(axis, k), halves[k]]
+                remote(block, block, r.tok_send.at[p], r.tok_half.at[p, k], axis_peer(axis, stride)).start()
+            send_far(p, 1 + k)
+    pass_far(0)
+    if relay:
+        for p in range(3):
+            for k in range(2):
+                wait_bytes(tok[p].at[0, halves[k]], r.tok_half.at[p, k])
+            send_far(p, 3)
     for p in range(3):
         wait_bytes(r.all_keys.at[p, 0, pl.ds(0, side - 1)], r.key_recv.at[p])
         for offset in range(1, side):
@@ -329,7 +354,10 @@
             i = lax.rem(me[OUT[p][1]] + side - offset, side)
             if offset:
                 wait_bytes(r.all_keys.at[p, 0], r.far_key_recv.at[p, offset - 1])
-                wait_bytes(far[p].at[0], r.far_recv.at[p, offset - 1])
+            if relay and offset == 2:
+                for n in range(side):
+                    for k in range(2):
+                        wait_bytes(tok[p].at[0, halves[k]], r.far_half.at[p, k, n])
 
             def load(d, slot):
                 return pltpu.make_async_copy(
@@ -371,10 +399,11 @@
     def heads(part, n_parts):
         lax.fori_loop(n_heads * part // n_parts, n_heads * (part + 1) // n_parts, one_head, 0)
 
-    heads(0, 2)
     pick_group(0)
-    for offset in range(1, side):
-        heads(side - 2 + offset, 2 * (side - 1))
+    for n in range(1, side):
+        pass_far(n)
+        heads(n - 1, side - 1)
+    for offset in (1, 3, 2) if relay else (1,):
         pick_group(offset)
     for chunk in range(1, N_CHUNKS):
         for p in range(3):
@@ -554,7 +583,8 @@
             wait_bytes(results[p].at[chunk, pl.ds(0, side), pl.ds(0, side - 1)], r.home_recv.at[chunk, p])
 
         def source_of(p, n):
-            return lax.rem(me[BACK[p][2]] + 1 + n, side)
+            ahead = 2 * side - 2 - 2 * n + 3 * (n // 2) if relay else 1 - n
+            return lax.rem(me[BACK[p][2]] + ahead, side)
 
         def load(p, n, slot):
             copies = []
@@ -613,11 +643,27 @@
                     def _():
                         sums[p][d, :, lo : lo + size] += total
 
-                @pl.when(jnp.logical_and(chunk == N_CHUNKS - 1, n < side - 1))
+                last = chunk == N_CHUNKS - 1
+                axis = BACK[p][2]
+
+                @pl.when(jnp.logical_and(last, n == 0))
                 def _():
-                    remote(
-                        sums[p].at[d], others[p].at[n], r.sum_send.at[p], r.sum_recv.at[p], {**me, BACK[p][2]: d}
-                    ).start()
+                    for k, stride in enumerate(strides):
+                        part, spot, arrived = sums[p].at[d], others[p].at[0], r.sum_recv.at[p, 0]
+                        if relay:
+                            part = sums[p].at[d, halves[k]]
+                            spot, arrived = others[p].at[2, halves[k]], r.sum_half.at[p, k]
+                        remote(part, spot, r.sum_send.at[p], arrived, axis_peer(axis, stride)).start()
+
+                for k in range(2 if relay else 0):
+
+                    @pl.when(jnp.logical_and(last, n == 2 + k))
+                    def _():
+                        wait_bytes(others[p].at[2, halves[k]], r.sum_half.at[p, k])
+                        sums[p][d, halves[k], :] += others[p][2, halves[k], :]
+                        remote(
+                            sums[p].at[d], others[p].at[k], r.sum_send.at[p], r.sum_recv.at[p, k], axis_peer(axis, strides[k])
+                        ).start()
 
             return c
 
@@ -634,20 +680,20 @@
         wait_bytes(r.line_gates.at[p, pl.ds(0, side - 1)], r.gate_recv.at[p])
     lax.fori_loop(0, N_CHUNKS, weigh_chunk, 0)
     for p, (lo, hi) in enumerate(parts):
-        wait_bytes(others[p], r.sum_recv.at[p])
+        for k in range(len(strides)):
+            wait_bytes(others[p].at[k], r.sum_recv.at[p, k])
 
         def finish(here):
             moe = sums[p][me[BACK[p][2]], here, :]
-            for offset in range(1, side):
-                moe += others[p][offset - 1, here, :]
+            for k in range(len(strides)):
+                moe += others[p][k, here, :]
             r.out[here, lo:hi] = (r.dense[here, lo:hi] + moe).astype(BF16)
 
         bands(finish)
 
 
     for p in range(3):
-        for offset in range(1, side):
-            wait_bytes(tok[p].at[0], r.tok_send.at[p, offset - 1])
+        wait_bytes(tok[p].at[pl.ds(0, side - 1)], r.tok_send.at[p])
         wait_bytes(r.all_keys.at[p, 0, pl.ds(0, side - 1)], r.key_send.at[p])
         wait_bytes(far[p].at[pl.ds(0, side - 1)], r.far_send.at[p])
         wait_bytes(r.all_keys.at[p, pl.ds(0, side - 1)], r.far_key_send.at[p])
@@ -701,18 +747,21 @@
         out_sem=dma(2, 3),
         own_sem=dma(2, 3),
         load_sem=dma(2, side),
-        tok_send=dma(3, side - 1),
-        tok_recv=dma(3, side - 1),
+        tok_send=dma(3),
+        tok_recv=dma(3, 2),
+        tok_half=dma(3, 2),
         key_send=dma(3),
         key_recv=dma(3),
         far_send=dma(3),
-        far_recv=dma(3, side - 1),
+        far_recv=dma(3, 2, side),
+        far_half=dma(3, 2, side),
         far_key_send=dma(3),
         far_key_recv=dma(3, side - 1),
         gate_send=dma(3),
         gate_recv=dma(3),
         sum_send=dma(3),
-        sum_recv=dma(3),
+        sum_recv=dma(3, 2),
+        sum_half=dma(3, 2),
         go_send=dma(N_CHUNKS, 3),
         go_recv=dma(N_CHUNKS, 3),
         back_send=dma(N_CHUNKS, 3),

time: 458 us -> 439 us (0.959)
  Pallas kernels: 454 us -> 436 us
    pallas_call x1, Pallas kernels: 454 us -> 436 us  [layer_pair(): pl.pallas_call(functools.partial(kernel, names=tuple(small) + tuple(large...]
where the time goes in v6:
time: 439 us; the launch traced here: 438 us
  Pallas kernels  436 us (99%)
    pallas_call x1, Pallas kernels, layer_pair(): pl.pallas_call(functools.partial(kernel, names=tuple(small) + tuple(large...  436 us

profile of v6, /device:TPU:0, one launch (start us, length us, event | category | flops | bytes accessed | tf_op | source)
XLA Modules:
  0.0 437.8 jit_solution(8270181907850633465)
XLA Ops:
  0.0 435.5 %shard_map.181 = (bf16[256,2048]{1,0:T(8,128)(2,1)}, bf16[4,4,256,768]{3,2,1,0:T(8,128)(2,1)}, bf16[24,4,4,16,768]{4,3,2,1,0:T(8,128)(2,1)}, bf16[3,4,4,2,4,16,7...) custom-call(bf16[256,2048]{1,0:T(8,128)(2,1)} %bitcast.20, ...), custom_call_target="tpu_custom_call" | custom-call | flops 57982058496 | bytes 100663296 | tf_op jit(solution)/shard_map/pallas_call | solution.py:786
  435.5 2.3 copy.21

commit v7 on v6

--- a/solution.py
+++ b/solution.py
@@ -556,36 +556,31 @@
     def middle_rows(p, chunk, i, d):
         return middles[p].at[(chunk,) + ordered({BACK[p][1]: i, BACK[p][2]: d})]
 
+    def source_of(p, n):
+        ahead = 2 * side - 2 - 2 * n + 3 * (n // 2) if relay else 1 - n
+        return lax.rem(me[BACK[p][2]] + ahead, side)
+
     def pass_on(chunk):
         for p in range(3):
             wait_bytes(middles[p].at[chunk, pl.ds(0, side), pl.ds(0, side), pl.ds(0, mates - 1)], r.back_recv.at[chunk, p])
-            for offset in range(1, side):
-                axis = BACK[p][1]
-                place = axis_peer(axis, offset)
-                remote(
-                    middle_rows(p, chunk, place[axis], pl.ds(0, side)),
-                    results[p].at[chunk, pl.ds(0, side), me[axis]],
-                    r.home_send.at[chunk, p],
-                    r.home_recv.at[chunk, p],
-                    place,
-                ).start()
+        for n in range(side):
+            for p in range(3):
+                axis, d = BACK[p][1], source_of(p, n)
+                for offset in range(1, side):
+                    place = axis_peer(axis, offset)
+                    remote(
+                        middle_rows(p, chunk, place[axis], d),
+                        results[p].at[chunk, d, me[axis]],
+                        r.home_send.at[chunk, p],
+                        r.home_recv.at[chunk, p, n],
+                        place,
+                    ).start()
 
 
     split = r.split
     lanes = min(128, rows_block)
 
     def weigh_chunk(chunk, carry):
-        @pl.when(chunk == 1)
-        def _():
-            pass_on(N_CHUNKS - 1)
-
-        for p in range(3):
-            wait_bytes(results[p].at[chunk, pl.ds(0, side), pl.ds(0, side - 1)], r.home_recv.at[chunk, p])
-
-        def source_of(p, n):
-            ahead = 2 * side - 2 - 2 * n + 3 * (n // 2) if relay else 1 - n
-            return lax.rem(me[BACK[p][2]] + ahead, side)
-
         def load(p, n, slot):
             copies = []
             for offset in range(side):
@@ -599,19 +594,15 @@
                 )
             return copies
 
-        for copy in load(0, 0, 0):
-            copy.start()
-
         def one_source(n, c):
             for p in range(3):
-                d = source_of(p, n)
-                slot = lax.rem(n + p, 2)
-
-                @pl.when(n + p // 2 < side)
-                def _():
-                    for copy in load((p + 1) % 3, n + p // 2, 1 - slot):
-                        copy.start()
-
+                wait_bytes(results[p].at[chunk, 0, pl.ds(0, side - 1)], r.home_recv.at[chunk, p, n])
+            for copy in load(0, n, 0):
+                copy.start()
+            for p in range(3):
+                d, slot = source_of(p, n), p % 2
+                for copy in load(p + 1, n, 1 - slot) if p < 2 else ():
+                    copy.start()
                 held = plane_keys(p, (1, rows_block), chunk).astype(F32)
                 info = r.line_gates[p, d]
                 keys = [jnp.broadcast_to(info[:, j : j + 1], (tokens, lanes)) for j in range(top_k)]
@@ -655,16 +646,6 @@
                             spot, arrived = others[p].at[2, halves[k]], r.sum_half.at[p, k]
                         remote(part, spot, r.sum_send.at[p], arrived, axis_peer(axis, stride)).start()
 
-                for k in range(2 if relay else 0):
-
-                    @pl.when(jnp.logical_and(last, n == 2 + k))
-                    def _():
-                        wait_bytes(others[p].at[2, halves[k]], r.sum_half.at[p, k])
-                        sums[p][d, halves[k], :] += others[p][2, halves[k], :]
-                        remote(
-                            sums[p].at[d], others[p].at[k], r.sum_send.at[p], r.sum_recv.at[p, k], axis_peer(axis, strides[k])
-                        ).start()
-
             return c
 
         return lax.fori_loop(0, side, one_source, carry)
@@ -676,9 +657,18 @@
         return carry
 
     lax.fori_loop(0, N_CHUNKS, experts_and_back, 0)
+    pass_on(N_CHUNKS - 1)
     for p in range(3):
         wait_bytes(r.line_gates.at[p, pl.ds(0, side - 1)], r.gate_recv.at[p])
     lax.fori_loop(0, N_CHUNKS, weigh_chunk, 0)
+    for k in range(2 if relay else 0):
+        for p in range(3):
+            axis, d = BACK[p][2], source_of(p, 2 + k)
+            wait_bytes(others[p].at[2, halves[k]], r.sum_half.at[p, k])
+            sums[p][d, halves[k], :] += others[p][2, halves[k], :]
+            remote(
+                sums[p].at[d], others[p].at[k], r.sum_send.at[p], r.sum_recv.at[p, k], axis_peer(axis, strides[k])
+            ).start()
     for p, (lo, hi) in enumerate(parts):
         for k in range(len(strides)):
             wait_bytes(others[p].at[k], r.sum_recv.at[p, k])
@@ -767,7 +757,7 @@
         back_send=dma(N_CHUNKS, 3),
         back_recv=dma(N_CHUNKS, 3),
         home_send=dma(N_CHUNKS, 3),
-        home_recv=dma(N_CHUNKS, 3),
+        home_recv=dma(N_CHUNKS, 3, side),
     )
     for p, w in enumerate(widths):
         there = sds((N_CHUNKS, side, side, 2, side, slots, w), BF16)

time: 439 us -> 456 us (1.039)
  Pallas kernels: 436 us -> 450 us
    pallas_call x1, Pallas kernels: 436 us -> 450 us  [layer_pair(): pl.pallas_call(functools.partial(kernel, names=tuple(small) + tuple(large...]
where the time goes in v7:
time: 456 us; the launch traced here: 452 us
  Pallas kernels  450 us (99%)
    pallas_call x1, Pallas kernels, layer_pair(): pl.pallas_call(functools.partial(kernel, names=tuple(small) + tuple(large...  450 us

profile of v7, /device:TPU:0, one launch (start us, length us, event | category | flops | bytes accessed | tf_op | source)
XLA Modules:
  0.0 452.0 jit_solution(597311561272432033)
XLA Ops:
  0.0 449.7 %shard_map.181 = (bf16[256,2048]{1,0:T(8,128)(2,1)}, bf16[4,4,256,768]{3,2,1,0:T(8,128)(2,1)}, bf16[24,4,4,16,768]{4,3,2,1,0:T(8,128)(2,1)}, bf16[3,4,4,2,4,16,7...) custom-call(bf16[256,2048]{1,0:T(8,128)(2,1)} %bitcast.20, ...), custom_call_target="tpu_custom_call" | custom-call | flops 57982058496 | bytes 100663296 | tf_op jit(solution)/shard_map/pallas_call | solution.py:776
  449.7 2.3 copy.21

commit v8 on v6

--- a/solution.py
+++ b/solution.py
@@ -111,7 +111,7 @@
     def mate_keys(p, shape):
         row = lax.broadcasted_iota(I32, shape, 0)
         block, slot = row // slots, lax.rem(row, slots)
-        chunk, mate = block // mates, lax.rem(block, mates)
+        mate, chunk = block // N_CHUNKS, lax.rem(block, N_CHUNKS)
         place = {**me, OUT[p][2]: mate // 2}
         return expert_key(place, lax.rem(mate, 2), slot + chunk * slots)
 
@@ -245,9 +245,9 @@
     lane = lax.broadcasted_iota(I32, info.shape, 1)
     for j in range(top_k):
         info = jnp.where(lane == top_k + j, powers[j] / norm, info)
-    r.my_gates[...] = info
+    r.my_gates[...] = info.T[0 : 2 * top_k, :]
     for p in range(3):
-        r.line_gates[p, me[BACK[p][2]]] = info
+        r.line_gates[p, me[BACK[p][2]]] = r.my_gates[...]
 
 
     for k, stride in enumerate(strides):
@@ -323,26 +323,24 @@
     def keep(p, i, d, slot, chunk):
         spot = {**me, OUT[p][1]: i, OUT[p][0]: d}
         return pltpu.make_async_copy(
-            stage.at[slot, chunk * mates + out_mate[p], :, pl.ds(0, widths[p])],
+            stage.at[slot, out_mate[p] * N_CHUNKS + chunk, :, pl.ds(0, widths[p])],
             arrivals[p].at[(chunk,) + ordered(spot)],
             r.keep_sem.at[slot, chunk],
         )
 
     wanted = [mate_keys(p, (blocks * slots, min(128, tokens))) for p in range(3)]
 
-    def send_rows(p, chunk, i):
+    def send_rows(p, first, count):
         near, far_axis, axis = OUT[p]
-        free = (near,) if i is not None else (near, far_axis)
-        a, b = ordered({far_axis: pl.ds(0, side) if i is None else i, near: pl.ds(0, side)})
-        group_place = me if i is None else {**me, far_axis: i}
 
         def one_mate(offset, c):
             place = mate_peer(axis, offset)
+            mate = place[axis] * 2 + place['c']
             remote(
-                sends[p].at[chunk * mates + place[axis] * 2 + place['c'], a, b],
-                rows_of(arrivals[p], p, chunk, group_place, free),
-                r.go_send.at[chunk, p],
-                r.go_recv.at[chunk, p],
+                sends[p].at[pl.ds(mate * N_CHUNKS + first, count)],
+                rows_of(arrivals[p], p, pl.ds(first, count), me, (near, far_axis)),
+                r.go_send.at[min(first, 1), p],
+                r.go_recv.at[min(first, 1), p],
                 place,
             ).start()
             return c
@@ -394,7 +392,6 @@
                 flush(p, i, d, d % 2).wait()
                 for chunk in range(N_CHUNKS):
                     keep(p, i, d, d % 2, chunk).wait()
-            send_rows(p, 0, i)
 
     def heads(part, n_parts):
         lax.fori_loop(n_heads * part // n_parts, n_heads * (part + 1) // n_parts, one_head, 0)
@@ -405,9 +402,9 @@
         heads(n - 1, side - 1)
     for offset in (1, 3, 2) if relay else (1,):
         pick_group(offset)
-    for chunk in range(1, N_CHUNKS):
-        for p in range(3):
-            send_rows(p, chunk, None)
+    for first, count in ((0, 1), (1, N_CHUNKS - 1)):
+        for p in range(3):
+            send_rows(p, first, count)
 
 
     out_split = n_heads * head_dim // model
@@ -503,8 +500,13 @@
                 pl.when(when)(copy.wait)
 
     def expert_chunk(chunk):
-        for p in range(3):
-            wait_bytes(sends[p].at[pl.ds(0, mates - 1)], r.go_recv.at[chunk, p])
+        for first, count in ((0, 1), (1, N_CHUNKS - 1)):
+
+            @pl.when(chunk == first)
+            def _():
+                for p in range(3):
+                    wait_bytes(sends[p].at[pl.ds(0, count * (mates - 1))], r.go_recv.at[first, p])
+
         for copy in fetch(chunk, 0, 0):
             copy.start()
 
@@ -613,7 +615,7 @@
                         copy.start()
 
                 held = plane_keys(p, (1, rows_block), chunk).astype(F32)
-                info = r.line_gates[p, d]
+                info = r.line_info[p, d]
                 keys = [jnp.broadcast_to(info[:, j : j + 1], (tokens, lanes)) for j in range(top_k)]
                 gates = [jnp.broadcast_to(info[:, top_k + j : top_k + j + 1], (tokens, lanes)) for j in range(top_k)]
                 for lo in range(0, rows_block, lanes):
@@ -676,8 +678,11 @@
         return carry
 
     lax.fori_loop(0, N_CHUNKS, experts_and_back, 0)
+    gap = jnp.zeros((128 - 2 * top_k, tokens), F32)
     for p in range(3):
         wait_bytes(r.line_gates.at[p, pl.ds(0, side - 1)], r.gate_recv.at[p])
+        for d in range(side):
+            r.line_info[p, d] = jnp.concatenate([r.line_gates[p, d], gap], axis=0).T
     lax.fori_loop(0, N_CHUNKS, weigh_chunk, 0)
     for p, (lo, hi) in enumerate(parts):
         for k in range(len(strides)):
@@ -699,8 +704,9 @@
         wait_bytes(r.all_keys.at[p, pl.ds(0, side - 1)], r.far_key_send.at[p])
         wait_bytes(r.line_gates.at[p, pl.ds(0, side - 1)], r.gate_send.at[p])
         wait_bytes(others[p], r.sum_send.at[p])
+        for first, count in ((0, 1), (1, N_CHUNKS - 1)):
+            wait_bytes(sends[p].at[pl.ds(0, count * (mates - 1))], r.go_send.at[first, p])
         for chunk in range(N_CHUNKS):
-            wait_bytes(sends[p].at[pl.ds(0, mates - 1)], r.go_send.at[chunk, p])
             wait_bytes(middles[p].at[chunk, pl.ds(0, side), pl.ds(0, side), pl.ds(0, mates - 1)], r.back_send.at[chunk, p])
             wait_bytes(results[p].at[chunk, pl.ds(0, side), pl.ds(0, side - 1)], r.home_send.at[chunk, p])
 
@@ -727,8 +733,9 @@
         dense=vmem((tokens, model), F32),
         ring=vmem((RING, model, TILE), BF16),
         all_keys=vmem((3, side, side, top_k, tokens), I32),
-        my_gates=vmem((tokens, 128), F32),
-        line_gates=vmem((3, side, tokens, 128), F32),
+        my_gates=vmem((2 * top_k, tokens), F32),
+        line_gates=vmem((3, side, 2 * top_k, tokens), F32),
+        line_info=vmem((3, side, tokens, 128), F32),
         source=vmem((2, tokens, max(widths)), BF16),
         stage=vmem((2, max(members, N_CHUNKS * mates), slots, max(widths)), BF16),
         split=vmem((3 * tokens, members * slots), BF16),
@@ -762,8 +769,8 @@
         sum_send=dma(3),
         sum_recv=dma(3, 2),
         sum_half=dma(3, 2),
-        go_send=dma(N_CHUNKS, 3),
-        go_recv=dma(N_CHUNKS, 3),
+        go_send=dma(2, 3),
+        go_recv=dma(2, 3),
         back_send=dma(N_CHUNKS, 3),
         back_recv=dma(N_CHUNKS, 3),
         home_send=dma(N_CHUNKS, 3),

time: 439 us -> 469 us (1.068)
  Pallas kernels: 436 us -> 464 us
    pallas_call x1, Pallas kernels: 436 us -> 464 us  [layer_pair(): pl.pallas_call(functools.partial(kernel, names=tuple(small) + tuple(large...]
where the time goes in v8:
time: 469 us; the launch traced here: 466 us
  Pallas kernels  464 us (99%)
    pallas_call x1, Pallas kernels, layer_pair(): pl.pallas_call(functools.partial(kernel, names=tuple(small) + tuple(large...  464 us

profile of v8, /device:TPU:0, one launch (start us, length us, event | category | flops | bytes accessed | tf_op | source)
XLA Modules:
  0.0 466.0 jit_solution(12582134438687947056)
XLA Ops:
  0.0 463.7 %shard_map.181 = (bf16[256,2048]{1,0:T(8,128)(2,1)}, bf16[4,4,256,768]{3,2,1,0:T(8,128)(2,1)}, bf16[24,4,4,16,768]{4,3,2,1,0:T(8,128)(2,1)}, bf16[3,4,4,2,4,16,7...) custom-call(bf16[256,2048]{1,0:T(8,128)(2,1)} %bitcast.20, ...), custom_call_target="tpu_custom_call" | custom-call | flops 57982058496 | bytes 100663296 | tf_op jit(solution)/shard_map/pallas_call | solution.py:793
  463.7 2.3 copy.21

commit v9 on v6

--- a/solution.py
+++ b/solution.py
@@ -109,11 +109,8 @@
         return expert_key(place, lax.rem(which, 2), slot + chunk * slots)
 
     def mate_keys(p, shape):
-        row = lax.broadcasted_iota(I32, shape, 0)
-        block, slot = row // slots, lax.rem(row, slots)
-        chunk, mate = block // mates, lax.rem(block, mates)
-        place = {**me, OUT[p][2]: mate // 2}
-        return expert_key(place, lax.rem(mate, 2), slot + chunk * slots)
+        mate = lax.broadcasted_iota(I32, shape, 0)
+        return expert_key({**me, OUT[p][2]: mate // 2}, lax.rem(mate, 2), 0)
 
     tok, far, sends, arrivals, outputs = each('tok'), each('far'), each('send'), each('arrive'), each('output')
     middles, results, sums, others = each('middle'), each('result'), each('sum'), each('other')
@@ -245,9 +242,9 @@
     lane = lax.broadcasted_iota(I32, info.shape, 1)
     for j in range(top_k):
         info = jnp.where(lane == top_k + j, powers[j] / norm, info)
-    r.my_gates[...] = info
+    r.my_gates[...] = info.T[0 : 2 * top_k, :]
     for p in range(3):
-        r.line_gates[p, me[BACK[p][2]]] = info
+        r.line_gates[p, me[BACK[p][2]]] = r.my_gates[...]
 
 
     for k, stride in enumerate(strides):
@@ -301,13 +298,20 @@
     out_mate = [me[OUT[p][2]] * 2 + me['c'] for p in range(3)]
     back_mate = [me[BACK[p][0]] * 2 + me['c'] for p in range(3)]
 
-    def pick_rows(p, i, d, slot, source, wanted):
+    def pick_rows(p, i, d, slot, source):
         keys = r.all_keys[p, i, d]
-        for lo, n in steps(tokens, 128):
-            hit = wanted[:, 0:n] == keys[0:1, lo : lo + n]
-            for j in range(1, top_k):
-                hit = jnp.logical_or(hit, wanted[:, 0:n] == keys[j : j + 1, lo : lo + n])
-            r.split[0 : blocks * slots, lo : lo + n] = jnp.where(hit, 1.0, 0.0).astype(BF16)
+        first = mate_keys(p, (mates, tokens))
+        held = jnp.full((mates, tokens), -1, I32)
+        for j in range(top_k):
+            slot_there = keys[j : j + 1, :] - first
+            mine = jnp.logical_and(slot_there >= 0, slot_there < capacity)
+            held = jnp.where(mine, slot_there, held)
+        row_slot = lax.broadcasted_iota(I32, (capacity, tokens), 0)
+        for mate in range(mates):
+            pick = jnp.where(row_slot == held[mate : mate + 1, :], 1.0, 0.0).astype(BF16)
+            for chunk in range(N_CHUNKS):
+                at = (chunk * mates + mate) * slots
+                r.split[at : at + slots, 0:tokens] = pick[chunk * slots : (chunk + 1) * slots, :]
         for lo, n in steps(widths[p], TILE):
             found = dot(r.split[0 : blocks * slots, 0:tokens], source[:, lo : lo + n]).astype(BF16)
             stage[slot, 0:blocks, :, lo : lo + n] = found.reshape(blocks, slots, n)
@@ -327,8 +331,6 @@
             arrivals[p].at[(chunk,) + ordered(spot)],
             r.keep_sem.at[slot, chunk],
         )
-
-    wanted = [mate_keys(p, (blocks * slots, min(128, tokens))) for p in range(3)]
 
     def send_rows(p, chunk, i):
         near, far_axis, axis = OUT[p]
@@ -383,7 +385,7 @@
                     for chunk in range(N_CHUNKS):
                         keep(p, i, d - 2, slot, chunk).wait()
 
-                pick_rows(p, i, d, slot, r.source.at[slot] if offset else tok[p].at[d], wanted[p])
+                pick_rows(p, i, d, slot, r.source.at[slot] if offset else tok[p].at[d])
                 flush(p, i, d, slot).start()
                 for chunk in range(N_CHUNKS):
                     keep(p, i, d, slot, chunk).start()
@@ -394,7 +396,8 @@
                 flush(p, i, d, d % 2).wait()
                 for chunk in range(N_CHUNKS):
                     keep(p, i, d, d % 2, chunk).wait()
-            send_rows(p, 0, i)
+            if offset:
+                send_rows(p, 0, i)
 
     def heads(part, n_parts):
         lax.fori_loop(n_heads * part // n_parts, n_heads * (part + 1) // n_parts, one_head, 0)
@@ -403,6 +406,8 @@
     for n in range(1, side):
         pass_far(n)
         heads(n - 1, side - 1)
+    for p in range(3):
+        send_rows(p, 0, me[OUT[p][1]])
     for offset in (1, 3, 2) if relay else (1,):
         pick_group(offset)
     for chunk in range(1, N_CHUNKS):
@@ -613,7 +618,7 @@
                         copy.start()
 
                 held = plane_keys(p, (1, rows_block), chunk).astype(F32)
-                info = r.line_gates[p, d]
+                info = r.line_info[p, d]
                 keys = [jnp.broadcast_to(info[:, j : j + 1], (tokens, lanes)) for j in range(top_k)]
                 gates = [jnp.broadcast_to(info[:, top_k + j : top_k + j + 1], (tokens, lanes)) for j in range(top_k)]
                 for lo in range(0, rows_block, lanes):
@@ -676,8 +681,11 @@
         return carry
 
     lax.fori_loop(0, N_CHUNKS, experts_and_back, 0)
+    gap = jnp.zeros((128 - 2 * top_k, tokens), F32)
     for p in range(3):
         wait_bytes(r.line_gates.at[p, pl.ds(0, side - 1)], r.gate_recv.at[p])
+        for d in range(side):
+            r.line_info[p, d] = jnp.concatenate([r.line_gates[p, d], gap], axis=0).T
     lax.fori_loop(0, N_CHUNKS, weigh_chunk, 0)
     for p, (lo, hi) in enumerate(parts):
         for k in range(len(strides)):
@@ -727,8 +735,9 @@
         dense=vmem((tokens, model), F32),
         ring=vmem((RING, model, TILE), BF16),
         all_keys=vmem((3, side, side, top_k, tokens), I32),
-        my_gates=vmem((tokens, 128), F32),
-        line_gates=vmem((3, side, tokens, 128), F32),
+        my_gates=vmem((2 * top_k, tokens), F32),
+        line_gates=vmem((3, side, 2 * top_k, tokens), F32),
+        line_info=vmem((3, side, tokens, 128), F32),
         source=vmem((2, tokens, max(widths)), BF16),
         stage=vmem((2, max(members, N_CHUNKS * mates), slots, max(widths)), BF16),
         split=vmem((3 * tokens, members * slots), BF16),

time: 439 us -> 427 us (0.973)
  Pallas kernels: 436 us -> 424 us
    pallas_call x1, Pallas kernels: 436 us -> 424 us  [layer_pair(): pl.pallas_call(functools.partial(kernel, names=tuple(small) + tuple(large...]
where the time goes in v9:
time: 427 us; the launch traced here: 426 us
  Pallas kernels  424 us (99%)
    pallas_call x1, Pallas kernels, layer_pair(): pl.pallas_call(functools.partial(kernel, names=tuple(small) + tuple(large...  424 us

profile of v9, /device:TPU:0, one launch (start us, length us, event | category | flops | bytes accessed | tf_op | source)
XLA Modules:
  0.0 426.5 jit_solution(10958641403741679477)
XLA Ops:
  0.0 424.2 %shard_map.181 = (bf16[256,2048]{1,0:T(8,128)(2,1)}, bf16[4,4,256,768]{3,2,1,0:T(8,128)(2,1)}, bf16[24,4,4,16,768]{4,3,2,1,0:T(8,128)(2,1)}, bf16[3,4,4,2,4,16,7...) custom-call(bf16[256,2048]{1,0:T(8,128)(2,1)} %bitcast.20, ...), custom_call_target="tpu_custom_call" | custom-call | flops 57982058496 | bytes 100663296 | tf_op jit(solution)/shard_map/pallas_call | solution.py:795
  424.2 2.3 copy.21

commit v10 on v9

--- a/solution.py
+++ b/solution.py
@@ -100,13 +100,12 @@
     def expert_key(place, core, slot):
         return (((place['z'] * side + place['y']) * side + place['x']) * 2 + core) * capacity + slot
 
-    def plane_keys(p, shape, chunk):
+    def plane_keys(p, shape):
         first, second, _ = BACK[p]
-        row = lax.broadcasted_iota(I32, shape, 1)
-        which, slot = row // slots, lax.rem(row, slots)
+        which = lax.broadcasted_iota(I32, shape, 0)
         pair = which // 2
         place = {**me, second: pair // side, first: lax.rem(pair, side)}
-        return expert_key(place, lax.rem(which, 2), slot + chunk * slots)
+        return expert_key(place, lax.rem(which, 2), 0)
 
     def mate_keys(p, shape):
         mate = lax.broadcasted_iota(I32, shape, 0)
@@ -617,15 +616,12 @@
                     for copy in load((p + 1) % 3, n + p // 2, 1 - slot):
                         copy.start()
 
-                held = plane_keys(p, (1, rows_block), chunk).astype(F32)
-                info = r.line_info[p, d]
-                keys = [jnp.broadcast_to(info[:, j : j + 1], (tokens, lanes)) for j in range(top_k)]
-                gates = [jnp.broadcast_to(info[:, top_k + j : top_k + j + 1], (tokens, lanes)) for j in range(top_k)]
+                lane = lax.broadcasted_iota(I32, (1, lanes), 1)
+                wanted = (lax.rem(lane, slots) + chunk * slots).astype(F32)
                 for lo in range(0, rows_block, lanes):
-                    here = held[:, lo : lo + lanes]
-                    weight = jnp.zeros((tokens, lanes), F32)
-                    for j in range(top_k):
-                        weight = jnp.where(here == keys[j], gates[j], weight)
+                    which = jnp.broadcast_to(lane // slots + lo // slots, (tokens, lanes))
+                    take = functools.partial(jnp.take_along_axis, indices=which, axis=1, mode='promise_in_bounds')
+                    weight = jnp.where(take(r.held[p, d]) == wanted, take(r.gates[p, d]), 0.0)
                     high = weight.astype(BF16)
                     rest = weight - high.astype(F32)
                     middle = rest.astype(BF16)
@@ -681,11 +677,24 @@
         return carry
 
     lax.fori_loop(0, N_CHUNKS, experts_and_back, 0)
-    gap = jnp.zeros((128 - 2 * top_k, tokens), F32)
+    gap = jnp.zeros((128 - members, tokens), F32)
     for p in range(3):
         wait_bytes(r.line_gates.at[p, pl.ds(0, side - 1)], r.gate_recv.at[p])
-        for d in range(side):
-            r.line_info[p, d] = jnp.concatenate([r.line_gates[p, d], gap], axis=0).T
+        first = plane_keys(p, (members, tokens)).astype(F32)
+
+        def spread(d, c):
+            info = r.line_gates[p, d]
+            held, gate = jnp.full((members, tokens), -1.0, F32), jnp.zeros((members, tokens), F32)
+            for j in range(top_k):
+                there = info[j : j + 1, :] - first
+                mine = jnp.logical_and(there >= 0, there < capacity)
+                held = jnp.where(mine, there, held)
+                gate = jnp.where(mine, info[top_k + j : top_k + j + 1, :], gate)
+            r.held[p, d] = jnp.concatenate([held, gap], axis=0).T
+            r.gates[p, d] = jnp.concatenate([gate, gap], axis=0).T
+            return c
+
+        lax.fori_loop(0, side, spread, 0)
     lax.fori_loop(0, N_CHUNKS, weigh_chunk, 0)
     for p, (lo, hi) in enumerate(parts):
         for k in range(len(strides)):
@@ -737,7 +746,8 @@
         all_keys=vmem((3, side, side, top_k, tokens), I32),
         my_gates=vmem((2 * top_k, tokens), F32),
         line_gates=vmem((3, side, 2 * top_k, tokens), F32),
-        line_info=vmem((3, side, tokens, 128), F32),
+        held=vmem((3, side, tokens, 128), F32),
+        gates=vmem((3, side, tokens, 128), F32),
         source=vmem((2, tokens, max(widths)), BF16),
         stage=vmem((2, max(members, N_CHUNKS * mates), slots, max(widths)), BF16),
         split=vmem((3 * tokens, members * slots), BF16),

time: 427 us -> 418 us (0.979)
  Pallas kernels: 424 us -> 415 us
    pallas_call x1, Pallas kernels: 424 us -> 415 us  [layer_pair(): pl.pallas_call(functools.partial(kernel, names=tuple(small) + tuple(large...]
where the time goes in v10:
time: 418 us
  Pallas kernels  415 us (99%)
    pallas_call x1, Pallas kernels, layer_pair(): pl.pallas_call(functools.partial(kernel, names=tuple(small) + tuple(large...  415 us

profile of v10, /device:TPU:0, one launch (start us, length us, event | category | flops | bytes accessed | tf_op | source)
XLA Modules:
  0.0 417.6 jit_solution(14478732440300514842)
XLA Ops:
  0.0 415.3 %shard_map.181 = (bf16[256,2048]{1,0:T(8,128)(2,1)}, bf16[4,4,256,768]{3,2,1,0:T(8,128)(2,1)}, bf16[24,4,4,16,768]{4,3,2,1,0:T(8,128)(2,1)}, bf16[3,4,4,2,4,16,7...) custom-call(bf16[256,2048]{1,0:T(8,128)(2,1)} %bitcast.20, ...), custom_call_target="tpu_custom_call" | custom-call | flops 57982058496 | bytes 100663296 | tf_op jit(solution)/shard_map/pallas_call | solution.py:805
  415.3 2.3 copy.21

commit v11 on v10

--- a/solution.py
+++ b/solution.py
@@ -579,10 +579,6 @@
     lanes = min(128, rows_block)
 
     def weigh_chunk(chunk, carry):
-        @pl.when(chunk == 1)
-        def _():
-            pass_on(N_CHUNKS - 1)
-
         for p in range(3):
             wait_bytes(results[p].at[chunk, pl.ds(0, side), pl.ds(0, side - 1)], r.home_recv.at[chunk, p])
 
@@ -671,12 +667,11 @@
         return lax.fori_loop(0, side, one_source, carry)
 
 
-    def experts_and_back(chunk, carry):
-        expert_chunk(chunk)
-        pl.when(chunk >= 1)(lambda: pass_on(chunk - 1))
-        return carry
-
-    lax.fori_loop(0, N_CHUNKS, experts_and_back, 0)
+    def one_by_one(step):
+        lax.fori_loop(0, N_CHUNKS, lambda chunk, c: (step(chunk), c)[1], 0)
+
+    one_by_one(expert_chunk)
+    one_by_one(pass_on)
     gap = jnp.zeros((128 - members, tokens), F32)
     for p in range(3):
         wait_bytes(r.line_gates.at[p, pl.ds(0, side - 1)], r.gate_recv.at[p])

time: 418 us -> 418 us (level)
  no operation moved by 1% of the time
where the time goes in v11:
time: 418 us
  Pallas kernels  415 us (99%)
    pallas_call x1, Pallas kernels, layer_pair(): pl.pallas_call(functools.partial(kernel, names=tuple(small) + tuple(large...  415 us

profile of v11, /device:TPU:0, one launch (start us, length us, event | category | flops | bytes accessed | tf_op | source)
XLA Modules:
  0.0 417.6 jit_solution(8481697661087029538)
XLA Ops:
  0.0 415.3 %shard_map.181 = (bf16[256,2048]{1,0:T(8,128)(2,1)}, bf16[4,4,256,768]{3,2,1,0:T(8,128)(2,1)}, bf16[24,4,4,16,768]{4,3,2,1,0:T(8,128)(2,1)}, bf16[3,4,4,2,4,16,7...) custom-call(bf16[256,2048]{1,0:T(8,128)(2,1)} %bitcast.20, ...), custom_call_target="tpu_custom_call" | custom-call | flops 57982058496 | bytes 100663296 | tf_op jit(solution)/shard_map/pallas_call | solution.py:800
  415.3 2.3 copy.21

commit v12 on v11

--- a/solution.py
+++ b/solution.py
@@ -331,17 +331,16 @@
             r.keep_sem.at[slot, chunk],
         )
 
-    def send_rows(p, chunk, i):
+    def send_rows(p, chunk, first, count):
         near, far_axis, axis = OUT[p]
-        free = (near,) if i is not None else (near, far_axis)
-        a, b = ordered({far_axis: pl.ds(0, side) if i is None else i, near: pl.ds(0, side)})
-        group_place = me if i is None else {**me, far_axis: i}
+        groups = pl.ds(first, count)
+        a, b = ordered({far_axis: groups, near: pl.ds(0, side)})
 
         def one_mate(offset, c):
             place = mate_peer(axis, offset)
             remote(
                 sends[p].at[chunk * mates + place[axis] * 2 + place['c'], a, b],
-                rows_of(arrivals[p], p, chunk, group_place, free),
+                rows_of(arrivals[p], p, chunk, {**me, far_axis: groups}, (near,)),
                 r.go_send.at[chunk, p],
                 r.go_recv.at[chunk, p],
                 place,
@@ -395,8 +394,6 @@
                 flush(p, i, d, d % 2).wait()
                 for chunk in range(N_CHUNKS):
                     keep(p, i, d, d % 2, chunk).wait()
-            if offset:
-                send_rows(p, 0, i)
 
     def heads(part, n_parts):
         lax.fori_loop(n_heads * part // n_parts, n_heads * (part + 1) // n_parts, one_head, 0)
@@ -405,13 +402,18 @@
     for n in range(1, side):
         pass_far(n)
         heads(n - 1, side - 1)
+    for offset in (1, 3) if relay else (1,):
+        pick_group(offset)
+    pair = [me[OUT[p][1]] // 2 * 2 for p in range(3)]
     for p in range(3):
-        send_rows(p, 0, me[OUT[p][1]])
-    for offset in (1, 3, 2) if relay else (1,):
-        pick_group(offset)
+        send_rows(p, 0, pair[p], 2)
+    if relay:
+        pick_group(2)
+        for p in range(3):
+            send_rows(p, 0, 2 - pair[p], 2)
     for chunk in range(1, N_CHUNKS):
         for p in range(3):
-            send_rows(p, chunk, None)
+            send_rows(p, chunk, 0, side)
 
 
     out_split = n_heads * head_dim // model

time: 418 us -> 423 us (1.012)
  Pallas kernels: 415 us -> 420 us
    pallas_call x1, Pallas kernels: 415 us -> 420 us  [layer_pair(): pl.pallas_call(functools.partial(kernel, names=tuple(small) + tuple(large...]
where the time goes in v12:
time: 423 us
  Pallas kernels  420 us (99%)
    pallas_call x1, Pallas kernels, layer_pair(): pl.pallas_call(functools.partial(kernel, names=tuple(small) + tuple(large...  420 us

profile of v12, /device:TPU:0, one launch (start us, length us, event | category | flops | bytes accessed | tf_op | source)
XLA Modules:
  0.0 422.5 jit_solution(12954510336164941826)
XLA Ops:
  0.0 420.2 %shard_map.181 = (bf16[256,2048]{1,0:T(8,128)(2,1)}, bf16[4,4,256,768]{3,2,1,0:T(8,128)(2,1)}, bf16[24,4,4,16,768]{4,3,2,1,0:T(8,128)(2,1)}, bf16[3,4,4,2,4,16,7...) custom-call(bf16[256,2048]{1,0:T(8,128)(2,1)} %bitcast.20, ...), custom_call_target="tpu_custom_call" | custom-call | flops 57982058496 | bytes 100663296 | tf_op jit(solution)/shard_map/pallas_call | solution.py:802
  420.2 2.3 copy.21

commit v13 on v11

--- a/solution.py
+++ b/solution.py
@@ -63,7 +63,10 @@
     assert side in (2, 4)
     relay = side == 4
     strides = (1, side - 1) if relay else (1,)
-    order = (0, side - 1, 1, 2) if relay else (0, 1)
+
+    def order(n):
+        return 3 * n - 5 * (n // 2) - 2 * (n // 3) if relay else n
+
     rows_block = members * slots
     tokens, model = r.hidden.shape
     me = {axis: lax.axis_index(axis) for axis in AXES}
@@ -148,7 +151,7 @@
 
     def send_far(p, n):
         near, axis, _ = OUT[p]
-        d = lax.rem(me[near] + order[n], side)
+        d = lax.rem(me[near] + order(n), side)
         for k, stride in enumerate(strides):
             remote(
                 tok[p].at[d], far[p].at[me[axis], d], r.far_send.at[p], r.far_recv.at[p, k, n], axis_peer(axis, stride)
@@ -158,7 +161,7 @@
         for k, stride in enumerate(strides):
             for p in range(3):
                 near, axis, _ = OUT[p]
-                d = lax.rem(me[near] + order[n], side)
+                d = lax.rem(me[near] + order(n), side)
                 wait_bytes(tok[p].at[0], r.far_recv.at[p, k, n])
                 if relay:
                     block = far[p].at[neighbour(axis, k), d, halves[k]]
@@ -254,7 +257,6 @@
                 block = tok[p].at[neighbour(axis, k), halves[k]]
                 remote(block, block, r.tok_send.at[p], r.tok_half.at[p, k], axis_peer(axis, stride)).start()
             send_far(p, 1 + k)
-    pass_far(0)
     if relay:
         for p in range(3):
             for k in range(2):
@@ -297,7 +299,7 @@
     out_mate = [me[OUT[p][2]] * 2 + me['c'] for p in range(3)]
     back_mate = [me[BACK[p][0]] * 2 + me['c'] for p in range(3)]
 
-    def pick_rows(p, i, d, slot, source):
+    def pick_rows(p, i, d, source):
         keys = r.all_keys[p, i, d]
         first = mate_keys(p, (mates, tokens))
         held = jnp.full((mates, tokens), -1, I32)
@@ -313,23 +315,34 @@
                 r.split[at : at + slots, 0:tokens] = pick[chunk * slots : (chunk + 1) * slots, :]
         for lo, n in steps(widths[p], TILE):
             found = dot(r.split[0 : blocks * slots, 0:tokens], source[:, lo : lo + n]).astype(BF16)
-            stage[slot, 0:blocks, :, lo : lo + n] = found.reshape(blocks, slots, n)
-
-    def flush(p, i, d, slot):
+            stage[p * blocks : (p + 1) * blocks, :, lo : lo + n] = found.reshape(blocks, slots, n)
+
+    def flush(p, i, d):
         a, b = ordered({OUT[p][1]: i, OUT[p][0]: d})
         return pltpu.make_async_copy(
-            stage.at[slot, pl.ds(0, blocks), :, pl.ds(0, widths[p])],
+            stage.at[pl.ds(p * blocks, blocks), :, pl.ds(0, widths[p])],
             sends[p].at[pl.ds(0, blocks), a, b],
-            r.stage_sem.at[slot],
+            r.stage_sem.at[p],
         )
 
-    def keep(p, i, d, slot, chunk):
+    def keep(p, i, d, chunk):
         spot = {**me, OUT[p][1]: i, OUT[p][0]: d}
         return pltpu.make_async_copy(
-            stage.at[slot, chunk * mates + out_mate[p], :, pl.ds(0, widths[p])],
+            stage.at[p * blocks + chunk * mates + out_mate[p], :, pl.ds(0, widths[p])],
             arrivals[p].at[(chunk,) + ordered(spot)],
-            r.keep_sem.at[slot, chunk],
+            r.keep_sem.at[p, chunk],
         )
+
+    def wait_staged(p):
+        flush(p, 0, 0).wait()
+        for chunk in range(N_CHUNKS):
+            keep(p, 0, 0, chunk).wait()
+
+    def pick_one(p, i, d, source):
+        pick_rows(p, i, d, source)
+        flush(p, i, d).start()
+        for chunk in range(N_CHUNKS):
+            keep(p, i, d, chunk).start()
 
     def send_rows(p, chunk, i):
         near, far_axis, axis = OUT[p]
@@ -350,65 +363,70 @@
 
         lax.fori_loop(1, mates, one_mate, 0)
 
-    def pick_group(offset):
-        for p in range(3):
-            i = lax.rem(me[OUT[p][1]] + side - offset, side)
-            if offset:
-                wait_bytes(r.all_keys.at[p, 0], r.far_key_recv.at[p, offset - 1])
-            if relay and offset == 2:
-                for n in range(side):
-                    for k in range(2):
-                        wait_bytes(tok[p].at[0, halves[k]], r.far_half.at[p, k, n])
-
-            def load(d, slot):
-                return pltpu.make_async_copy(
-                    far[p].at[i, d], r.source.at[slot, :, pl.ds(0, widths[p])], r.source_sem.at[slot]
-                )
-
-            if offset:
-                load(0, 0).start()
-
-            def one_source(d, c):
-                slot = lax.rem(d, 2)
-                if offset:
-
-                    @pl.when(d + 1 < side)
-                    def _():
-                        load(d + 1, 1 - slot).start()
-
-                    load(d, slot).wait()
-
-                @pl.when(d >= 2)
-                def _():
-                    flush(p, i, d - 2, slot).wait()
-                    for chunk in range(N_CHUNKS):
-                        keep(p, i, d - 2, slot, chunk).wait()
-
-                pick_rows(p, i, d, slot, r.source.at[slot] if offset else tok[p].at[d])
-                flush(p, i, d, slot).start()
-                for chunk in range(N_CHUNKS):
-                    keep(p, i, d, slot, chunk).start()
-                return c
-
-            lax.fori_loop(0, side, one_source, 0)
-            for d in range(side - 2, side):
-                flush(p, i, d, d % 2).wait()
-                for chunk in range(N_CHUNKS):
-                    keep(p, i, d, d % 2, chunk).wait()
-            if offset:
-                send_rows(p, 0, i)
-
     def heads(part, n_parts):
         lax.fori_loop(n_heads * part // n_parts, n_heads * (part + 1) // n_parts, one_head, 0)
 
-    pick_group(0)
-    for n in range(1, side):
+    def own_line(d, c):
+        for p in range(3):
+            pl.when(d >= 1)(functools.partial(wait_staged, p))
+            pick_one(p, me[OUT[p][1]], d, tok[p].at[d])
+        return c
+
+    def load_far(p, k, i, n):
+        d = lax.rem(me[OUT[p][0]] + order(n), side)
+        copy = pltpu.make_async_copy(
+            far[p].at[i, d], r.source.at[p, :, pl.ds(0, widths[p])], r.source_sem.at[p]
+        )
+        return copy, d
+
+    def pick_far(k, n, place, first):
+        for p in range(3):
+            i = place(OUT[p][1])
+            copy, d = load_far(p, k, i, n)
+            copy.wait()
+            if first is None:
+                wait_staged(p)
+            else:
+                pl.when(jnp.logical_not(first))(functools.partial(wait_staged, p))
+            pick_one(p, i, d, r.source.at[p])
+
+    def neighbours(n, c):
+        heads(n, side)
         pass_far(n)
-        heads(n - 1, side - 1)
+        for k in range(len(strides)):
+            for p in range(3):
+                load_far(p, k, neighbour(OUT[p][1], k), n)[0].start()
+            pick_far(k, n, functools.partial(neighbour, k=k), None)
+        return c
+
+    def opposite(n, c):
+        for p in range(3):
+            for k in range(2):
+                wait_bytes(tok[p].at[0, halves[k]], r.far_half.at[p, k, n])
+            load_far(p, 0, opposite_of(OUT[p][1]), n)[0].start()
+        pick_far(0, n, opposite_of, n == 0)
+        return c
+
+    def opposite_of(axis):
+        return lax.rem(me[axis] + 2, side)
+
+    lax.fori_loop(0, side, own_line, 0)
+    for p in range(3):
+        for offset in range(1, side):
+            wait_bytes(r.all_keys.at[p, 0], r.far_key_recv.at[p, offset - 1])
+    lax.fori_loop(0, side, neighbours, 0)
+    for p in range(3):
+        wait_staged(p)
     for p in range(3):
         send_rows(p, 0, me[OUT[p][1]])
-    for offset in (1, 3, 2) if relay else (1,):
-        pick_group(offset)
+    for k in range(len(strides)):
+        for p in range(3):
+            send_rows(p, 0, neighbour(OUT[p][1], k))
+    if relay:
+        lax.fori_loop(0, side, opposite, 0)
+        for p in range(3):
+            wait_staged(p)
+            send_rows(p, 0, opposite_of(OUT[p][1]))
     for chunk in range(1, N_CHUNKS):
         for p in range(3):
             send_rows(p, chunk, None)
@@ -593,7 +611,7 @@
                 copies.append(
                     pltpu.make_async_copy(
                         results[p].at[chunk, d, i] if offset else middle_rows(p, chunk, i, d),
-                        stage.at[slot, pl.ds(i * mates, mates), :, pl.ds(0, widths[p])],
+                        stage.at[pl.ds(slot * members + i * mates, mates), :, pl.ds(0, widths[p])],
                         r.load_sem.at[slot, offset],
                     )
                 )
@@ -628,7 +646,7 @@
                 for copy in load(p, n, slot):
                     copy.wait()
                 for lo, size in steps(widths[p], TILE):
-                    y = stage[slot, 0:members, :, lo : lo + size].reshape(rows_block, size)
+                    y = stage[pl.ds(slot * members, members), :, lo : lo + size].reshape(rows_block, size)
                     both = dot(split[...], y)
                     total = both[0:tokens] + (both[tokens : 2 * tokens] + both[2 * tokens : 3 * tokens])
 
@@ -743,8 +761,8 @@
         line_gates=vmem((3, side, 2 * top_k, tokens), F32),
         held=vmem((3, side, tokens, 128), F32),
         gates=vmem((3, side, tokens, 128), F32),
-        source=vmem((2, tokens, max(widths)), BF16),
-        stage=vmem((2, max(members, N_CHUNKS * mates), slots, max(widths)), BF16),
+        source=vmem((3, tokens, max(widths)), BF16),
+        stage=vmem((max(2 * members, 3 * N_CHUNKS * mates), slots, max(widths)), BF16),
         split=vmem((3 * tokens, members * slots), BF16),
         gate=vmem((model, width), BF16),
         up=vmem((model, width), BF16),
@@ -754,9 +772,9 @@
         hidden_buf=vmem((rows, width), BF16),
         weight_sem=dma(3),
         ring_sem=dma(RING),
-        source_sem=dma(2),
-        stage_sem=dma(2),
-        keep_sem=dma(2, N_CHUNKS),
+        source_sem=dma(3),
+        stage_sem=dma(3),
+        keep_sem=dma(3, N_CHUNKS),
         in_sem=dma(2, 3),
         out_sem=dma(2, 3),
         own_sem=dma(2, 3),

time: 418 us -> 423 us (1.012)
  no operation moved by 1% of the time
where the time goes in v13:
time: 423 us; the launch traced here: 420 us
  Pallas kernels  418 us (99%)
    pallas_call x1, Pallas kernels, layer_pair(): pl.pallas_call(functools.partial(kernel, names=tuple(small) + tuple(large...  418 us

profile of v13, /device:TPU:0, one launch (start us, length us, event | category | flops | bytes accessed | tf_op | source)
XLA Modules:
  0.0 420.3 jit_solution(7845686626874319801)
XLA Ops:
  0.0 418.0 %shard_map.181 = (bf16[256,2048]{1,0:T(8,128)(2,1)}, bf16[4,4,256,768]{3,2,1,0:T(8,128)(2,1)}, bf16[24,4,4,16,768]{4,3,2,1,0:T(8,128)(2,1)}, bf16[3,4,4,2,4,16,7...) custom-call(bf16[256,2048]{1,0:T(8,128)(2,1)} %bitcast.20, ...), custom_call_target="tpu_custom_call" | custom-call | flops 57982058496 | bytes 100663296 | tf_op jit(solution)/shard_map/pallas_call | solution.py:818
  418.0 2.3 copy.21

commit v14 on v11

--- a/solution.py
+++ b/solution.py
@@ -403,8 +403,8 @@
 
     pick_group(0)
     for n in range(1, side):
+        heads(n - 1, side - 1)
         pass_far(n)
-        heads(n - 1, side - 1)
     for p in range(3):
         send_rows(p, 0, me[OUT[p][1]])
     for offset in (1, 3, 2) if relay else (1,):

time: 418 us -> 418 us (level)
  no operation moved by 1% of the time
where the time goes in v14:
time: 418 us
  Pallas kernels  415 us (99%)
    pallas_call x1, Pallas kernels, layer_pair(): pl.pallas_call(functools.partial(kernel, names=tuple(small) + tuple(large...  415 us

profile of v14, /device:TPU:0, one launch (start us, length us, event | category | flops | bytes accessed | tf_op | source)
XLA Modules:
  0.0 417.6 jit_solution(16225497425534575969)
XLA Ops:
  0.0 415.3 %shard_map.181 = (bf16[256,2048]{1,0:T(8,128)(2,1)}, bf16[4,4,256,768]{3,2,1,0:T(8,128)(2,1)}, bf16[24,4,4,16,768]{4,3,2,1,0:T(8,128)(2,1)}, bf16[3,4,4,2,4,16,7...) custom-call(bf16[256,2048]{1,0:T(8,128)(2,1)} %bitcast.20, ...), custom_call_target="tpu_custom_call" | custom-call | flops 57982058496 | bytes 100663296 | tf_op jit(solution)/shard_map/pallas_call | solution.py:800
  415.3 2.3 copy.21
